TPU v7x, 8 devices: a whole 2x2x1 slice. The times are simulated.
8 devices in a mesh: sweep: 1 (over z), data: 2 (over y), ent: 4 (over x, core).
Axes of the slice: x: 2, y: 2, z: 1, core: 2. Of those that a mesh axis runs over, the one named last changes fastest.
Arguments:
- ent_table: float32 [65536, 400], P(('sweep', 'ent'))
- ada_state: float32 [65536], P(('sweep', 'ent'))
- rel_table: float32 [14824, 400], P('sweep')
- head_idx: int32 [4, 2, 4, 8192], P(('sweep', 'ent'), 'data')
- tail_idx: int32 [4, 2, 4, 8192], P(('sweep', 'ent'), 'data')
- rel_idx: int32 [4, 2, 4, 8192], P(('sweep', 'ent'), 'data')
- edge_mask: int32 [4, 2, 4, 8192], P(('sweep', 'ent'), 'data')
- neg_idx: int32 [4, 2, 4, 200], P(('sweep', 'ent'), 'data')
Outputs:
- output 1: float32 [65536, 400], P(('sweep', 'ent'))
- output 2: float32 [65536], P(('sweep', 'ent'))
- output 3: float32 [14824, 400], P('sweep')
- output 4: float32 [4, 2, 4], P(('sweep', 'ent'), 'data')
All inputs are finite; a program needn't handle non-finite values.
Results may differ from a plain program's by a relative error of at most 0.001.
Values are sent between devices in bfloat16 or wider.
A program may use at most 1 GiB of HBM per device.

v0:
```python
import jax
import jax.numpy as jnp
from jax import lax
from jax.sharding import PartitionSpec as P

LEARN_ENT = 0.1
LEARN_REL = 0.05
ADA_EPS = 1e-6


def complex_mul(left, right):
    half_dim = left.shape[-1] // 2
    left_re, left_im = left[..., :half_dim], left[..., half_dim:]
    right_re, right_im = right[..., :half_dim], right[..., half_dim:]
    return jnp.concatenate([left_re * right_re - left_im * right_im, left_re * right_im + left_im * right_re], axis=-1)


def complex_mul_conj(left, right):
    half_dim = left.shape[-1] // 2
    left_re, left_im = left[..., :half_dim], left[..., half_dim:]
    right_re, right_im = right[..., :half_dim], right[..., half_dim:]
    return jnp.concatenate([left_re * right_re + left_im * right_im, left_im * right_re - left_re * right_im], axis=-1)


def bucket_grads(head_rows, tail_rows, neg_rows, rel_rows, weight):
    query_vec = complex_mul(head_rows, rel_rows)
    tail_f32 = tail_rows.astype(jnp.float32)
    pos_score = jnp.sum(query_vec * tail_f32, axis=-1)
    query_bf = query_vec.astype(jnp.bfloat16)
    neg_score = jnp.einsum("...bd,...nd->...bn", query_bf, neg_rows, preferred_element_type=jnp.float32)
    top_score = jnp.maximum(pos_score, jnp.max(neg_score, axis=-1))
    pos_exp = jnp.exp(pos_score - top_score)
    neg_exp = jnp.exp(neg_score - top_score[..., None])
    norm_sum = pos_exp + jnp.sum(neg_exp, axis=-1)
    loss_sum = jnp.sum(weight * (top_score + jnp.log(norm_sum) - pos_score), axis=-1)
    pos_coef = weight * (pos_exp / norm_sum - 1.0)
    neg_coef = ((weight / norm_sum)[..., None] * neg_exp).astype(jnp.bfloat16)
    query_grad = pos_coef[..., None] * tail_f32 + jnp.einsum("...bn,...nd->...bd", neg_coef, neg_rows, preferred_element_type=jnp.float32)
    tail_grad = pos_coef[..., None] * query_vec
    neg_grad = jnp.einsum("...bn,...bd->...nd", neg_coef, query_bf, preferred_element_type=jnp.float32)
    head_grad = complex_mul_conj(query_grad, rel_rows)
    rel_grad = complex_mul_conj(query_grad, head_rows)
    return head_grad, tail_grad, neg_grad, rel_grad, loss_sum


def adagrad_rows(param_rows, state_vec, grad_rows, step_rate):
    new_state = state_vec + jnp.mean(grad_rows * grad_rows, axis=-1)
    return param_rows - step_rate * grad_rows * lax.rsqrt(new_state + ADA_EPS)[:, None], new_state


def solution(mesh):
    ent_size = mesh.shape["ent"]

    def device_epoch(ent_table, ada_state, rel_table, head_idx, tail_idx, rel_idx, edge_mask, neg_idx):
        part_rows = ent_table.shape[0]
        rel_count = rel_table.shape[0]
        edge_count = head_idx.shape[-1]
        ent_cur, state_cur, rel_cur = ent_table, ada_state, rel_table
        rel_state = jnp.zeros((rel_count,), jnp.float32)
        round_losses = []
        for round_idx in range(ent_size):
            head_ids = head_idx[0, 0, round_idx]
            tail_ids = tail_idx[0, 0, round_idx]
            neg_ids = neg_idx[0, 0, round_idx]
            rel_ids = rel_idx[0, 0, round_idx]
            fetch_perm = [((dest_idx + round_idx) % ent_size, dest_idx) for dest_idx in range(ent_size)]
            return_perm = [(src_idx, (src_idx + round_idx) % ent_size) for src_idx in range(ent_size)]
            table_bf = ent_cur.astype(jnp.bfloat16)
            tail_table = table_bf
            if round_idx:
                tail_table = lax.ppermute(table_bf, "ent", fetch_perm)
            head_grad, tail_grad, neg_grad, rel_grad, loss_sum = bucket_grads(
                jnp.take(ent_cur, head_ids, axis=0),
                jnp.take(tail_table, tail_ids, axis=0),
                jnp.take(tail_table, neg_ids, axis=0),
                jnp.take(rel_cur, rel_ids, axis=0),
                edge_mask[0, 0, round_idx].astype(jnp.float32))
            back_rows = jnp.concatenate([tail_grad, neg_grad], axis=0)
            back_ids = jnp.concatenate([tail_ids, neg_ids], axis=0)
            if round_idx:
                back_rows = lax.ppermute(back_rows, "ent", return_perm)
                back_ids = lax.ppermute(back_ids, "ent", return_perm)
            row_grad = jax.ops.segment_sum(
                jnp.concatenate([head_grad, back_rows], axis=0),
                jnp.concatenate([head_ids, back_ids], axis=0),
                num_segments=part_rows)
            row_grad = lax.psum(row_grad, "data")
            rel_grad_sum = lax.psum(jax.ops.segment_sum(rel_grad, rel_ids, num_segments=rel_count), ("data", "ent"))
            ent_cur, state_cur = adagrad_rows(ent_cur, state_cur, row_grad, LEARN_ENT)
            rel_cur, rel_state = adagrad_rows(rel_cur, rel_state, rel_grad_sum, LEARN_REL)
            round_losses.append(loss_sum / edge_count)
        return ent_cur, state_cur, rel_cur, jnp.stack(round_losses)[None, None, :]

    ent_spec = P(("sweep", "ent"), None)
    row_spec = P(("sweep", "ent"))
    rel_spec = P("sweep", None)
    edge_spec = P(("sweep", "ent"), "data", None, None)
    loss_spec = P(("sweep", "ent"), "data", None)
    return jax.shard_map(
        device_epoch, mesh=mesh,
        in_specs=(ent_spec, row_spec, rel_spec, edge_spec, edge_spec, edge_spec, edge_spec, edge_spec),
        out_specs=(ent_spec, row_spec, rel_spec, loss_spec),
        check_vma=False)
```

profile of v0, /device:TPU:0, one launch (start us, length us, event | category | flops | bytes accessed | tf_op | source)
XLA Modules:
  0.0 6723.6 jit_solution(16863214514048098253)
XLA Ops:
  76.9 44.4 gather_fusion.1
  154.9 45.3 gather_fusion
  373.8 61.2 scatter_custom_fusion.1
  502.9 113.2 %scatter_custom_fusion = f32[16384,400]{1,0:T(8,128)} fusion(s32[16584]{0:T(1024)S(1)} %pad_add_fusion, f32[16584,400]{1,0:T(8,128)} %copy.73, f32[]{:T(128)} %constant.50.clone.1), kind=kCustom, calls=%fused_computation.50 | custom fusion | flops 6633600 | bytes 26214912 | tf_op jit(solution)/shard_map/scatter-add | solution.py:83
  619.7 170.1 %all-reduce.11.cloned.1.call-done = f32[14824,400]{1,0:T(8,128)} async-done(((f32[14824,400]{1,0:T(8,128)}), f32[14824,400]{1,0:T(8,128)}) %all-reduce.11.cloned.1.call-update) | async-done | bytes 23718416 | tf_op jit(solution)/shard_map/psum | solution.py:88
  805.0 719.1 %all-reduce.9.cloned.1.call-done = f32[16384,400]{1,0:T(8,128)} async-done(((f32[16384,400]{1,0:T(8,128)}), f32[16384,400]{1,0:T(8,128)}) %all-reduce.9.cloned.1.call-update) | async-done | bytes 26214416 | tf_op jit(solution)/shard_map/psum | solution.py:87
  1697.4 45.3 gather_fusion.4
  1964.2 61.2 scatter_custom_fusion.3
  2027.1 127.4 %collective-permute-done = s32[8392]{0:T(1024)S(1)} collective-permute-done((s32[8392]{0:T(1024)S(1)}, s32[8392]{0:T(1024)S(1)}, u32[]{:S(2)}, u32[]{:S(2)}) %collective-permute-start) | collective-permute-done | bytes 33600 | tf_op jit(solution)/shard_map/ppermute | solution.py:82
  2204.1 113.2 %scatter_custom_fusion.2 = f32[16384,400]{1,0:T(8,128)} fusion(s32[16584]{0:T(1024)S(1)} %pad_add_fusion.1, f32[16584,400]{1,0:T(8,128)} %copy.84, f32[]{:T(128)} %constant.50.clone.1), kind=kCustom, calls=%fused_computation.48 | custom fusion | flops 6633600 | bytes 26214912 | tf_op jit(solution)/shard_map/scatter-add | solution.py:83
  2320.9 99.8 %all-reduce.15.cloned.1.call-done = f32[14824,400]{1,0:T(8,128)} async-done(((f32[14824,400]{1,0:T(8,128)}), f32[14824,400]{1,0:T(8,128)}) %all-reduce.15.cloned.1.call-update) | async-done | bytes 23718416 | tf_op jit(solution)/shard_map/psum | solution.py:88
  2435.7 719.2 %all-reduce.13.cloned.1.call-done = f32[16384,400]{1,0:T(8,128)} async-done(((f32[16384,400]{1,0:T(8,128)}), f32[16384,400]{1,0:T(8,128)}) %all-reduce.13.cloned.1.call-update) | async-done | bytes 26214416 | tf_op jit(solution)/shard_map/psum | solution.py:87
  3328.9 45.3 gather_fusion.8
  3416.7 92.1 %collective-permute-done.4 = bf16[16384,400]{0,1:T(8,128)(2,1)} collective-permute-done((bf16[16384,400]{0,1:T(8,128)(2,1)}, bf16[16384,400]{0,1:T(8,128)(2,1)}, u32[]{:S(2)}, u32[]{:S(2)}) %collective-permute-start.4) | collective-permute-done | bytes 13107232 | tf_op jit(solution)/shard_map/ppermute | solution.py:71
  3688.8 61.4 scatter_custom_fusion.5
  3751.5 358.9 %collective-permute-done.3 = s32[8392]{0:T(1024)S(1)} collective-permute-done((s32[8392]{0:T(1024)S(1)}, s32[8392]{0:T(1024)S(1)}, u32[]{:S(2)}, u32[]{:S(2)}) %collective-permute-start.3) | collective-permute-done | bytes 33600 | tf_op jit(solution)/shard_map/ppermute | solution.py:82
  4160.1 113.2 %scatter_custom_fusion.4 = f32[16384,400]{1,0:T(8,128)} fusion(s32[16584]{0:T(1024)S(1)} %pad_add_fusion.2, f32[16584,400]{1,0:T(8,128)} %copy.93, f32[]{:T(128)} %constant.50.clone.1), kind=kCustom, calls=%fused_computation.46 | custom fusion | flops 6633600 | bytes 26214912 | tf_op jit(solution)/shard_map/scatter-add | solution.py:83
  4292.0 715.8 %all-reduce.17.cloned.1.call-done = f32[16384,400]{1,0:T(8,128)} async-done(((f32[16384,400]{1,0:T(8,128)}), f32[16384,400]{1,0:T(8,128)}) %all-reduce.17.cloned.1.call-update) | async-done | bytes 26214416 | tf_op jit(solution)/shard_map/psum | solution.py:87
  5180.5 45.3 gather_fusion.12
  5448.9 61.2 scatter_custom_fusion.7
  5510.9 127.7 %collective-permute-done.6 = s32[8392]{0:T(1024)S(1)} collective-permute-done((s32[8392]{0:T(1024)S(1)}, s32[8392]{0:T(1024)S(1)}, u32[]{:S(2)}, u32[]{:S(2)}) %collective-permute-start.6) | collective-permute-done | bytes 33600 | tf_op jit(solution)/shard_map/ppermute | solution.py:82
  5688.2 113.4 %scatter_custom_fusion.6 = f32[16384,400]{1,0:T(8,128)} fusion(s32[16584]{0:T(1024)S(1)} %pad_add_fusion.3, f32[16584,400]{1,0:T(8,128)} %copy.102, f32[]{:T(128)} %constant.50.clone.1), kind=kCustom, calls=%fused_computation.44 | custom fusion | flops 6633600 | bytes 26214912 | tf_op jit(solution)/shard_map/scatter-add | solution.py:83
  5804.7 100.6 %all-reduce.23.cloned.1.call-done = f32[14824,400]{1,0:T(8,128)} async-done(((f32[14824,400]{1,0:T(8,128)}), f32[14824,400]{1,0:T(8,128)}) %all-reduce.23.cloned.1.call-update) | async-done | bytes 23718416 | tf_op jit(solution)/shard_map/psum | solution.py:88
  5977.5 662.1 %all-reduce.21.cloned.1.call-done = f32[16384,400]{1,0:T(8,128)} async-done(((f32[16384,400]{1,0:T(8,128)}), f32[16384,400]{1,0:T(8,128)}) %all-reduce.21.cloned.1.call-update) | async-done | bytes 26214416 | tf_op jit(solution)/shard_map/psum | solution.py:87
  (375 shorter events, 1889.4 us)
Async XLA Ops:
  7.2 782.6 %all-reduce.11.cloned.1.call-start = ((), (), s32[]{:S(2)}) async-start(), calls=%async_computation.1 | async-start | bytes 60719104 | tf_op jit(solution)/shard_map/psum | solution.py:88
  435.0 1089.0 %all-reduce.9.cloned.1.call-start = ((), (), s32[]{:S(2)}) async-start(), calls=%async_computation | async-start | bytes 67108864 | tf_op jit(solution)/shard_map/psum | solution.py:87
  616.1 1804.6 %all-reduce.15.cloned.1.call-start = ((), (), s32[]{:S(2)}) async-start(), calls=%async_computation.3 | async-start | bytes 60719104 | tf_op jit(solution)/shard_map/psum | solution.py:88
  805.0 732.1 %copy-start.42 = (f32[16384]{0:T(1024)S(1)}, f32[16384]{0:T(1024)}, u32[]{:S(2)}) copy-start(f32[16384]{0:T(1024)} %param.17) | copy-start | bytes 196612
  1595.0 190.4 %collective-permute-start.1 = (bf16[16384,400]{0,1:T(8,128)(2,1)}, bf16[16384,400]{0,1:T(8,128)(2,1)}, u32[]{:S(2)}, u32[]{:S(2)}) collective-permute-start(bf16[16384,400]{0,1:T(8,128)(2,1)} %copy.79), channel_id=1, source_target_pairs={{1,0},{2,1},{3,2},{0,3},{5,4},{6,5},{7,6},{4,7}} | collective-permute-start | bytes 39321608 | tf_op jit(solution)/shard_map/ppermute | solution.py:71
  1924.7 229.8 %collective-permute-start.2 = (f32[8392,400]{0,1:T(8,128)}, f32[8392,400]{0,1:T(8,128)}, u32[]{:S(2)}, u32[]{:S(2)}) collective-permute-start(f32[8392,400]{0,1:T(8,128)} %pad_maximum_fusion.4), channel_id=1, source_target_pairs={{0,1},{1,2},{2,3},{3,0},{4,5},{5,6},{6,7},{7,4}} | collective-permute-start | bytes 40281608 | tf_op jit(solution)/shard_map/ppermute | solution.py:81
  2025.5 1129.4 %all-reduce.13.cloned.1.call-start = ((), (), s32[]{:S(2)}) async-start(), calls=%async_computation.2 | async-start | bytes 67108864 | tf_op jit(solution)/shard_map/psum | solution.py:87
  2026.2 128.3 %collective-permute-start = (s32[8392]{0:T(1024)S(1)}, s32[8392]{0:T(1024)S(1)}, u32[]{:S(2)}, u32[]{:S(2)}) collective-permute-start(s32[8392]{0:T(1024)S(1)} %pad_add_fusion.4), channel_id=1, source_target_pairs={{0,1},{1,2},{2,3},{3,0},{4,5},{5,6},{6,7},{7,4}} | collective-permute-start | bytes 100712 | tf_op jit(solution)/shard_map/ppermute | solution.py:82
  2317.3 1959.6 %all-reduce.19.cloned.1.call-start = ((), (), s32[]{:S(2)}) async-start(), calls=%async_computation.5 | async-start | bytes 60719104 | tf_op jit(solution)/shard_map/psum | solution.py:88
  2435.7 731.5 %copy-start.17 = (f32[16384]{0:T(1024)S(1)}, f32[16384]{0:T(1024)}, u32[]{:S(2)}) copy-start(f32[16384]{0:T(1024)} %copy-done.16) | copy-start | bytes 196612
  2435.7 731.5 %copy-start.43 = (f32[16384]{0:T(1024)S(1)}, f32[16384]{0:T(1024)}, u32[]{:S(2)}) copy-start(f32[16384]{0:T(1024)} %param.17) | copy-start | bytes 196612
  3225.7 283.1 %collective-permute-start.4 = (bf16[16384,400]{0,1:T(8,128)(2,1)}, bf16[16384,400]{0,1:T(8,128)(2,1)}, u32[]{:S(2)}, u32[]{:S(2)}) collective-permute-start(bf16[16384,400]{0,1:T(8,128)(2,1)} %copy.88), channel_id=1, source_target_pairs={{2,0},{3,1},{0,2},{1,3},{6,4},{7,5},{4,6},{5,7}} | collective-permute-start | bytes 39321608 | tf_op jit(solution)/shard_map/ppermute | solution.py:71
  3647.8 462.7 %collective-permute-start.5 = (f32[8392,400]{0,1:T(8,128)}, f32[8392,400]{0,1:T(8,128)}, u32[]{:S(2)}, u32[]{:S(2)}) collective-permute-start(f32[8392,400]{0,1:T(8,128)} %pad_maximum_fusion.5), channel_id=1, source_target_pairs={{0,2},{1,3},{2,0},{3,1},{4,6},{5,7},{6,4},{7,5}} | collective-permute-start | bytes 40281608 | tf_op jit(solution)/shard_map/ppermute | solution.py:81
  3750.2 360.3 %copy-start.27 = (s32[1,1,1,8192]{3,2,1,0:T(1,128)S(1)}, s32[1,1,1,8192]{3,2,1,0:T(1,128)}, u32[]{:S(2)}) copy-start(s32[1,1,1,8192]{3,2,1,0:T(1,128)} %get-tuple-element.85) | copy-start | bytes 98308
  3750.2 1257.6 %all-reduce.17.cloned.1.call-start = ((), (), s32[]{:S(2)}) async-start(), calls=%async_computation.4 | async-start | bytes 67108864 | tf_op jit(solution)/shard_map/psum | solution.py:87
  3751.0 359.5 %collective-permute-start.3 = (s32[8392]{0:T(1024)S(1)}, s32[8392]{0:T(1024)S(1)}, u32[]{:S(2)}, u32[]{:S(2)}) collective-permute-start(s32[8392]{0:T(1024)S(1)} %pad_add_fusion.5), channel_id=1, source_target_pairs={{0,2},{1,3},{2,0},{3,1},{4,6},{5,7},{6,4},{7,5}} | collective-permute-start | bytes 100712 | tf_op jit(solution)/shard_map/ppermute | solution.py:82
  4273.3 1632.0 %all-reduce.23.cloned.1.call-start = ((), (), s32[]{:S(2)}) async-start(), calls=%async_computation.7 | async-start | bytes 60719104 | tf_op jit(solution)/shard_map/psum | solution.py:88
  4292.0 728.8 %copy-start.18 = (f32[16384]{0:T(1024)S(1)}, f32[16384]{0:T(1024)}, u32[]{:S(2)}) copy-start(f32[16384]{0:T(1024)} %get-tuple-element.27) | copy-start | bytes 196612
  5078.7 189.7 %collective-permute-start.7 = (bf16[16384,400]{0,1:T(8,128)(2,1)}, bf16[16384,400]{0,1:T(8,128)(2,1)}, u32[]{:S(2)}, u32[]{:S(2)}) collective-permute-start(bf16[16384,400]{0,1:T(8,128)(2,1)} %copy.97), channel_id=1, source_target_pairs={{3,0},{0,1},{1,2},{2,3},{7,4},{4,5},{5,6},{6,7}} | collective-permute-start | bytes 39321608 | tf_op jit(solution)/shard_map/ppermute | solution.py:71
  5407.6 230.9 %collective-permute-start.8 = (f32[8392,400]{0,1:T(8,128)}, f32[8392,400]{0,1:T(8,128)}, u32[]{:S(2)}, u32[]{:S(2)}) collective-permute-start(f32[8392,400]{0,1:T(8,128)} %pad_maximum_fusion.6), channel_id=1, source_target_pairs={{0,3},{1,0},{2,1},{3,2},{4,7},{5,4},{6,5},{7,6}} | collective-permute-start | bytes 40281608 | tf_op jit(solution)/shard_map/ppermute | solution.py:81
  5510.1 1129.5 %all-reduce.21.cloned.1.call-start = ((), (), s32[]{:S(2)}) async-start(), calls=%async_computation.6 | async-start | bytes 67108864 | tf_op jit(solution)/shard_map/psum | solution.py:87
  5510.8 127.7 %collective-permute-start.6 = (s32[8392]{0:T(1024)S(1)}, s32[8392]{0:T(1024)S(1)}, u32[]{:S(2)}, u32[]{:S(2)}) collective-permute-start(s32[8392]{0:T(1024)S(1)} %pad_add_fusion.6), channel_id=1, source_target_pairs={{0,3},{1,0},{2,1},{3,2},{4,7},{5,4},{6,5},{7,6}} | collective-permute-start | bytes 100712 | tf_op jit(solution)/shard_map/ppermute | solution.py:82
  5977.5 674.4 %copy-start.15 = (f32[16384]{0:T(1024)S(1)}, f32[16384]{0:T(1024)}, u32[]{:S(2)}) copy-start(f32[16384]{0:T(1024)} %copy-done.14) | copy-start | bytes 196612
  5977.5 674.4 %copy-start.19 = (f32[16384]{0:T(1024)S(1)}, f32[16384]{0:T(1024)}, u32[]{:S(2)}) copy-start(f32[16384]{0:T(1024)} %get-tuple-element.27) | copy-start | bytes 196612
  (77 other events, 1531.7 us)
Sparse Core Ops, SparseCore 0:
  435.2 354.5 all-reduce.10
  792.2 731.8 all-reduce.8
  2025.6 395.0 all-reduce.14
  2423.0 731.8 all-reduce.12
  3750.4 523.0 all-reduce.18
  4275.8 731.9 all-reduce.16
  5510.2 395.0 all-reduce.22
  5907.8 731.8 all-reduce.20
where the time goes:
time: 6750 us; the launch traced here: 6720 us
  waiting for transfers between devices  3890 us (58%)
  other arithmetic  1530 us (23%)
  local copies, waits for them, and re-layouts  1170 us (17%)
  matrix products  104 us (2%)
    psum x4, waiting for transfers between devices, device_epoch(): row_grad = lax.psum(row_grad, 'data')  2820 us
    ppermute x3, waiting for transfers between devices, device_epoch(): back_ids = lax.ppermute(back_ids, 'ent', return_perm)  614 us
    scatter-add x4, other arithmetic, device_epoch(): jax.ops.segment_sum(jnp.concatenate([head_grad, back_rows], axis=0), jnp....  453 us
    psum x4, waiting for transfers between devices, device_epoch(): lax.psum(jax.ops.segment_sum(rel_grad, rel_ids, num_segments=rel_count),...  370 us
    gather x8, local copies, waits for them, and re-layouts, device_epoch(): jnp.take(ent_cur, head_ids, axis=0)  246 us
    scatter-add x4, other arithmetic, device_epoch(): jax.ops.segment_sum(rel_grad, rel_ids, num_segments=rel_count)  245 us
    gather x8, local copies, waits for them, and re-layouts, device_epoch(): jnp.take(rel_cur, rel_ids, axis=0)  242 us
    gather x8, local copies, waits for them, and re-layouts, device_epoch(): jnp.take(tail_table, tail_ids, axis=0)  210 us
  transfers between devices with their start and end apart: 17, of which 11 were waited for; matrix products, arithmetic and copies ran while one was open for 25% of the time, Pallas kernels for 0%

commit v1 on v0

v1 whole, which is shorter than its diff:
```python
import functools

import jax
import jax.numpy as jnp
from jax import lax
from jax.experimental import pallas as pl
from jax.experimental.pallas import tpu as pltpu
from jax.sharding import PartitionSpec as P

LEARN_ENT = 0.1
LEARN_REL = 0.05
ADA_EPS = 1e-6
LANES = 128
BLOCK = 256
VMEM_CAP = 66_000_000


def pair_at(row):
    return pl.ds(pl.multiple_of(row, 2), 2)


def halves(ref):
    count = ref.shape[0] // 2
    return ref[pl.ds(0, count, stride=2), :], ref[pl.ds(1, count, stride=2), :]


def put_halves(ref, real, imag):
    count = ref.shape[0] // 2
    ref[pl.ds(0, count, stride=2), :] = real
    ref[pl.ds(1, count, stride=2), :] = imag


def query_kernel(head_ref, rel_ref, ent_hbm, rel_hbm, a_ref, r_ref, q_ref, ent_v, rel_v, sems):
    @pl.when(pl.program_id(0) == 0)
    def _():
        first = pltpu.make_async_copy(ent_hbm, ent_v, sems.at[0])
        second = pltpu.make_async_copy(rel_hbm, rel_v, sems.at[1])
        first.start()
        second.start()
        first.wait()
        second.wait()

    unroll = 32

    def some(step, carry):
        for sub in range(unroll):
            edge = step * unroll + sub
            a_ref[pair_at(2 * edge), :] = ent_v[pair_at(head_ref[0, 0, edge]), :]
            r_ref[pair_at(2 * edge), :] = rel_v[pair_at(rel_ref[0, 0, edge]), :]
        return carry

    lax.fori_loop(0, BLOCK // unroll, some, 0)
    a_re, a_im = halves(a_ref)
    r_re, r_im = halves(r_ref)
    q_ref[:, :LANES] = (a_re * r_re - a_im * r_im).astype(jnp.bfloat16)
    q_ref[:, LANES:] = (a_re * r_im + a_im * r_re).astype(jnp.bfloat16)


def tail_kernel(tail_ref, a_ref, r_ref, tab_hbm, c_ref, p_ref, tab_bf, tab_v, sem):
    @pl.when(pl.program_id(0) == 0)
    def _():
        copy = pltpu.make_async_copy(tab_hbm, tab_bf, sem)
        copy.start()
        copy.wait()
        rows = 512

        def widen(step, carry):
            at = pl.ds(pl.multiple_of(step * rows, rows), rows)
            tab_v[at, :] = tab_bf[at, :].astype(jnp.float32)
            return carry

        lax.fori_loop(0, tab_v.shape[0] // rows, widen, 0)

    unroll = 32

    def some(step, carry):
        for sub in range(unroll):
            edge = step * unroll + sub
            c_ref[pair_at(2 * edge), :] = tab_v[pair_at(tail_ref[0, 0, edge]), :]
        return carry

    lax.fori_loop(0, BLOCK // unroll, some, 0)
    a_re, a_im = halves(a_ref)
    r_re, r_im = halves(r_ref)
    c_re, c_im = halves(c_ref)
    prod = (a_re * r_re - a_im * r_im) * c_re + (a_re * r_im + a_im * r_re) * c_im
    p_ref[0] = jnp.sum(prod.T, axis=0, keepdims=True)


def column(row):
    return jnp.broadcast_to(row, (LANES, row.shape[-1])).T


def grad_kernel(
    per_bucket, negs,
    head_ref, tail_ref, rel_ref, neg_ref, a_ref, r_ref, c_ref, qp_ref, pm_ref, pp_ref, w_ref, mm_ref, mp_ref,
    gh_hbm, gt_hbm, gr_hbm, loss_ref,
    acc_h, acc_t, acc_r, blk_h, blk_t, blk_r, neg_acc, sems,
):
    block = pl.program_id(0)
    in_bucket = lax.rem(block, per_bucket)

    @pl.when(block == 0)
    def _():
        for acc in (acc_h, acc_t, acc_r):
            rows = 16

            def clear(step, carry):
                acc[pl.ds(pl.multiple_of(step * rows, rows), rows), :] = jnp.zeros((rows, LANES), jnp.float32)
                return carry

            lax.fori_loop(0, acc.shape[0] // rows, clear, 0)

    @pl.when(in_bucket == 0)
    def _():
        neg_acc[...] = jnp.zeros_like(neg_acc)
        loss_ref[...] = jnp.zeros_like(loss_ref)

    a_re, a_im = halves(a_ref)
    r_re, r_im = halves(r_ref)
    c_re, c_im = halves(c_ref)
    q_re = a_re * r_re - a_im * r_im
    q_im = a_re * r_im + a_im * r_re
    q_bf = jnp.concatenate([q_re.astype(jnp.bfloat16), q_im.astype(jnp.bfloat16)], axis=1)
    m_mine = mm_ref[0]
    nt = (((1,), (1,)), ((), ()))
    score = lax.dot_general(q_bf, m_mine, nt, preferred_element_type=jnp.float32)
    score = score + lax.dot_general(qp_ref[...], mp_ref[0], nt, preferred_element_type=jnp.float32)
    lane = lax.broadcasted_iota(jnp.int32, score.shape, 1)
    score = jnp.where(lane < negs, score, -jnp.inf)
    pos = column(pm_ref[0] + pp_ref[0])
    weight = column(w_ref[0])
    low, high = score[:, :LANES], score[:, LANES:]
    top = jnp.maximum(pos, jnp.max(jnp.maximum(low, high), axis=1, keepdims=True))
    pos_exp = jnp.exp(pos - top)
    low_exp, high_exp = jnp.exp(low - top), jnp.exp(high - top)
    norm = pos_exp + jnp.sum(low_exp + high_exp, axis=1, keepdims=True)
    loss_ref[0] = loss_ref[0] + jnp.sum(weight * (top + jnp.log(norm) - pos), axis=0, keepdims=True)
    alpha = weight * (pos_exp / norm - 1.0)
    scale = weight / norm
    beta = jnp.concatenate([(scale * low_exp).astype(jnp.bfloat16), (scale * high_exp).astype(jnp.bfloat16)], axis=1)
    nn = (((1,), (0,)), ((), ()))
    mixed = lax.dot_general(beta, m_mine, nn, preferred_element_type=jnp.float32)
    tn = (((0,), (0,)), ((), ()))
    neg_acc[...] += lax.dot_general(beta, q_bf, tn, preferred_element_type=jnp.float32)
    d_re = alpha * c_re + mixed[:, :LANES]
    d_im = alpha * c_im + mixed[:, LANES:]
    put_halves(blk_t, alpha * q_re, alpha * q_im)
    put_halves(blk_h, d_re * r_re + d_im * r_im, d_im * r_re - d_re * r_im)
    put_halves(blk_r, d_re * a_re + d_im * a_im, d_im * a_re - d_re * a_im)

    unroll = 16

    def some(step, carry):
        for sub in range(unroll):
            edge = step * unroll + sub
            here = pair_at(2 * edge)
            at_h, at_t, at_r = (pair_at(ref[0, 0, edge]) for ref in (head_ref, tail_ref, rel_ref))
            acc_h[at_h, :] = acc_h[at_h, :] + blk_h[here, :]
            acc_t[at_t, :] = acc_t[at_t, :] + blk_t[here, :]
            acc_r[at_r, :] = acc_r[at_r, :] + blk_r[here, :]
        return carry

    lax.fori_loop(0, BLOCK // unroll, some, 0)

    @pl.when(in_bucket == per_bucket - 1)
    def _():
        put_halves(blk_t, neg_acc[:, :LANES], neg_acc[:, LANES:])
        small = 8

        def more(step, carry):
            for sub in range(small):
                row = step * small + sub
                at_t = pair_at(neg_ref[0, 0, row])
                acc_t[at_t, :] = acc_t[at_t, :] + blk_t[pair_at(2 * row), :]
            return carry

        lax.fori_loop(0, negs // small, more, 0)

    @pl.when(block == pl.num_programs(0) - 1)
    def _():
        copies = [
            pltpu.make_async_copy(acc, out, sems.at[slot])
            for slot, (acc, out) in enumerate(((acc_h, gh_hbm), (acc_t, gt_hbm), (acc_r, gr_hbm)))
        ]
        for copy in copies:
            copy.start()
        for copy in copies:
            copy.wait()


def smem_block(width):
    return pl.BlockSpec((1, 1, width), lambda b: (b, 0, 0), memory_space=pltpu.SMEM)


PAIRS = pl.BlockSpec((2 * BLOCK, LANES), lambda b: (b, 0))
WIDE = pl.BlockSpec((BLOCK, 2 * LANES), lambda b: (b, 0))
ROW = pl.BlockSpec((1, 1, BLOCK), lambda b: (b, 0, 0))
ANYWHERE = pl.BlockSpec(memory_space=pl.ANY)
PARAMS = dict(dimension_semantics=("arbitrary",), vmem_limit_bytes=VMEM_CAP)


def query_rows(ent, rel, head_ids, rel_ids):
    blocks = head_ids.shape[0]
    edges = blocks * BLOCK
    return pl.pallas_call(
        query_kernel,
        grid=(blocks,),
        in_specs=[smem_block(BLOCK), smem_block(BLOCK), ANYWHERE, ANYWHERE],
        out_specs=[PAIRS, PAIRS, WIDE],
        out_shape=[
            jax.ShapeDtypeStruct((2 * edges, LANES), jnp.float32),
            jax.ShapeDtypeStruct((2 * edges, LANES), jnp.float32),
            jax.ShapeDtypeStruct((edges, 2 * LANES), jnp.bfloat16),
        ],
        scratch_shapes=[
            pltpu.VMEM(ent.shape, jnp.float32),
            pltpu.VMEM(rel.shape, jnp.float32),
            pltpu.SemaphoreType.DMA((2,)),
        ],
        compiler_params=pltpu.CompilerParams(**PARAMS),
        cost_estimate=pl.CostEstimate(flops=200_000_000, bytes_accessed=80_000_000, transcendentals=0),
        name="query_rows",
    )(head_ids, rel_ids, ent, rel)


def tail_rows(table, tail_ids, a_rows, r_rows):
    blocks = tail_ids.shape[0]
    edges = blocks * BLOCK
    return pl.pallas_call(
        tail_kernel,
        grid=(blocks,),
        in_specs=[smem_block(BLOCK), PAIRS, PAIRS, ANYWHERE],
        out_specs=[PAIRS, ROW],
        out_shape=[
            jax.ShapeDtypeStruct((2 * edges, LANES), jnp.float32),
            jax.ShapeDtypeStruct((blocks, 1, BLOCK), jnp.float32),
        ],
        scratch_shapes=[
            pltpu.VMEM(table.shape, jnp.bfloat16),
            pltpu.VMEM(table.shape, jnp.float32),
            pltpu.SemaphoreType.DMA,
        ],
        compiler_params=pltpu.CompilerParams(**PARAMS),
        cost_estimate=pl.CostEstimate(flops=200_000_000, bytes_accessed=60_000_000, transcendentals=0),
        name="tail_rows",
    )(tail_ids, a_rows, r_rows, table)


def bucket_grads(ids, neg_ids, rows, q_peer, p_mine, p_peer, weight, m_mine, m_peer, ent_shape, rel_shape, negs):
    head_ids, tail_ids, rel_ids = ids
    blocks = head_ids.shape[0]
    buckets = neg_ids.shape[0]
    per_bucket = blocks // buckets
    of_bucket = lambda b: (b // per_bucket, 0, 0)
    neg_block = pl.BlockSpec((1, 2 * LANES, 2 * LANES), of_bucket)
    return pl.pallas_call(
        functools.partial(grad_kernel, per_bucket, negs),
        grid=(blocks,),
        in_specs=[
            smem_block(BLOCK), smem_block(BLOCK), smem_block(BLOCK),
            pl.BlockSpec((1, 1, neg_ids.shape[-1]), of_bucket, memory_space=pltpu.SMEM),
            PAIRS, PAIRS, PAIRS, WIDE, ROW, ROW, ROW, neg_block, neg_block,
        ],
        out_specs=[ANYWHERE, ANYWHERE, ANYWHERE, pl.BlockSpec((1, 1, LANES), of_bucket)],
        out_shape=[
            jax.ShapeDtypeStruct(ent_shape, jnp.float32),
            jax.ShapeDtypeStruct(ent_shape, jnp.float32),
            jax.ShapeDtypeStruct(rel_shape, jnp.float32),
            jax.ShapeDtypeStruct((buckets, 1, LANES), jnp.float32),
        ],
        scratch_shapes=[
            pltpu.VMEM(ent_shape, jnp.float32),
            pltpu.VMEM(ent_shape, jnp.float32),
            pltpu.VMEM(rel_shape, jnp.float32),
            pltpu.VMEM((2 * BLOCK, LANES), jnp.float32),
            pltpu.VMEM((2 * BLOCK, LANES), jnp.float32),
            pltpu.VMEM((2 * BLOCK, LANES), jnp.float32),
            pltpu.VMEM((2 * LANES, 2 * LANES), jnp.float32),
            pltpu.SemaphoreType.DMA((3,)),
        ],
        compiler_params=pltpu.CompilerParams(**PARAMS),
        cost_estimate=pl.CostEstimate(flops=500_000_000, bytes_accessed=110_000_000, transcendentals=4_000_000),
        name="bucket_grads",
    )(head_ids, tail_ids, rel_ids, neg_ids, *rows, q_peer, p_mine, p_peer, weight, m_mine, m_peer)


def split_columns(table, part):
    rows, dim = table.shape
    width = dim // 4
    flipped = table.T.reshape(2, 2, width, rows)
    mine = lax.dynamic_index_in_dim(flipped, part, axis=1, keepdims=False)
    mine = jnp.pad(mine, ((0, 0), (0, LANES - width), (0, 0)))
    return jnp.transpose(mine, (2, 0, 1)).reshape(2 * rows, LANES)


def join_columns(half, dim):
    rows = half.shape[0] // 2
    width = dim // 4
    flipped = jnp.transpose(half.reshape(rows, 2, LANES)[:, :, :width], (1, 2, 0))
    both = lax.all_gather(flipped, "data", axis=1)
    return both.reshape(dim, rows).T


def adagrad(param, state, grad, rate, dim):
    rows = state.shape[0]
    grad3 = grad.reshape(rows, 2, LANES)
    square = lax.psum(jnp.sum(grad3 * grad3, axis=(1, 2)), "data")
    state = state + square / dim
    step = rate * lax.rsqrt(state + ADA_EPS)
    param = param.reshape(rows, 2, LANES) - grad3 * step[:, None, None]
    return param.reshape(2 * rows, LANES), state


def solution(mesh):
    ent_size = mesh.shape["ent"]
    data_size = mesh.shape["data"]
    swap = [(src, data_size - 1 - src) for src in range(data_size)]

    def device_epoch(ent_table, ada_state, rel_table, head_idx, tail_idx, rel_idx, edge_mask, neg_idx):
        dim = ent_table.shape[1]
        edge_count = head_idx.shape[-1]
        negs = neg_idx.shape[-1]
        part = lax.axis_index("data")
        ent = split_columns(ent_table, part)
        rel = split_columns(rel_table, part)
        state = ada_state
        rel_state = jnp.zeros((rel_table.shape[0],), jnp.float32)

        local = jnp.concatenate(
            [2 * head_idx[0, 0], 2 * tail_idx[0, 0], 2 * rel_idx[0, 0], edge_mask[0, 0], 2 * neg_idx[0, 0]], axis=1)
        both = lax.all_gather(local, "data")
        blocks = data_size * edge_count // BLOCK

        def field(slot, round_idx):
            return both[:, round_idx, slot * edge_count:(slot + 1) * edge_count].reshape(blocks, 1, BLOCK)

        losses = []
        for round_idx in range(ent_size):
            head_ids, tail_ids, rel_ids = (field(slot, round_idx) for slot in range(3))
            weight = field(3, round_idx).astype(jnp.float32)
            neg_ids = both[:, round_idx, 4 * edge_count:].reshape(data_size, 1, negs)
            table = ent.astype(jnp.bfloat16)
            if round_idx:
                fetch = [((dest + round_idx) % ent_size, dest) for dest in range(ent_size)]
                table = lax.ppermute(table, "ent", fetch)
            a_rows, r_rows, q_mine = query_rows(ent, rel, head_ids, rel_ids)
            q_peer = lax.ppermute(q_mine, "data", swap)
            c_rows, p_mine = tail_rows(table, tail_ids, a_rows, r_rows)
            m_mine = jnp.take(table.reshape(-1, 2, LANES), neg_ids.reshape(-1) // 2, axis=0)
            m_mine = m_mine.reshape(data_size, negs, 2 * LANES)
            m_mine = jnp.pad(m_mine, ((0, 0), (0, 2 * LANES - negs), (0, 0)))
            m_peer = lax.ppermute(m_mine, "data", swap)
            p_peer = lax.ppermute(p_mine, "data", swap)
            g_head, g_tail, g_rel, loss = bucket_grads(
                (head_ids, tail_ids, rel_ids), neg_ids, (a_rows, r_rows, c_rows), q_peer, p_mine, p_peer, weight,
                m_mine, m_peer, ent.shape, rel.shape, negs)
            if round_idx:
                back = [(src, (src + round_idx) % ent_size) for src in range(ent_size)]
                g_tail = lax.ppermute(g_tail, "ent", back)
            g_rel = lax.psum(g_rel, "ent")
            ent, state = adagrad(ent, state, g_head + g_tail, LEARN_ENT, dim)
            rel, rel_state = adagrad(rel, rel_state, g_rel, LEARN_REL, dim)
            losses.append(lax.dynamic_index_in_dim(loss, part, axis=0, keepdims=False)[0, 0] / edge_count)
        ent_out = join_columns(ent, dim)
        rel_out = join_columns(rel, dim)
        return ent_out, state, rel_out, jnp.stack(losses)[None, None, :]

    ent_spec = P(("sweep", "ent"), None)
    row_spec = P(("sweep", "ent"))
    rel_spec = P("sweep", None)
    edge_spec = P(("sweep", "ent"), "data", None, None)
    loss_spec = P(("sweep", "ent"), "data", None)
    return jax.shard_map(
        device_epoch, mesh=mesh,
        in_specs=(ent_spec, row_spec, rel_spec, edge_spec, edge_spec, edge_spec, edge_spec, edge_spec),
        out_specs=(ent_spec, row_spec, rel_spec, loss_spec),
        check_vma=False)
```

time: 6750 us -> 4910 us (0.73)
  waiting for transfers between devices: 3890 us -> 2650 us
  Pallas kernels: 0 us -> 1190 us
  other arithmetic: 1530 us -> 437 us
  local copies, waits for them, and re-layouts: 1170 us -> 542 us
  matrix products: 104 us -> 0 us
    psum x8, waiting for transfers between devices: 3190 us -> 1590 us  [the longest x4 1540 us: device_epoch(): g_rel = lax.psum(g_rel, 'ent')]
    pallas_call x0 -> x12, Pallas kernels: none -> 1190 us  [the longest x4 769 us: bucket_grads(): pl.pallas_call(functools.partial(grad_kernel, per_bucket, negs), grid=(bl...]
    gather x28 -> x4, local copies, waits for them, and re-layouts: 735 us -> 18.2 us  [device_epoch(): jnp.take(table.reshape(-1, 2, LANES), neg_ids.reshape(-1) // 2, axis=0)]
    scatter-add x8 -> x0, other arithmetic: 698 us -> none  [the longest x4 453 us: device_epoch(): jax.ops.segment_sum(jnp.concatenate([head_grad, back_rows], axis=0), jnp....]
    all_gather x0 -> x3, waiting for transfers between devices: none -> 481 us  [the longest x2 481 us: join_columns(): both = lax.all_gather(flipped, 'data', axis=1)]
    concatenate x8 -> x0, local copies, waits for them, and re-layouts: 185 us -> none  [the longest x4 122 us: device_epoch(): jnp.concatenate([head_grad, back_rows], axis=0)]
    sub x0 -> x3, local copies, waits for them, and re-layouts: none -> 145 us  [adagrad(): param = param.reshape(rows, 2, LANES) - grad3 * step[:, None, None]]
    concatenate x18 -> x1, other arithmetic: 142 us -> 0.7 us  [device_epoch(): jnp.concatenate([2 * head_idx[0, 0], 2 * tail_idx[0, 0], 2 * rel_idx[0, 0...]
  transfers between devices with their start and end apart: 17 -> 29, of which waited for: 11 -> 19; matrix products, arithmetic and copies ran while one was open for 25% -> 14% of each run, Pallas kernels for 0% -> 7%
where the time goes in v1:
time: 4910 us; the launch traced here: 4890 us
  waiting for transfers between devices  2650 us (54%)
  Pallas kernels  1190 us (24%)
  local copies, waits for them, and re-layouts  542 us (11%)
  other arithmetic  437 us (9%)
    psum x4, waiting for transfers between devices, device_epoch(): g_rel = lax.psum(g_rel, 'ent')  1540 us
    pallas_call x4, Pallas kernels, bucket_grads(): pl.pallas_call(functools.partial(grad_kernel, per_bucket, negs), grid=(bl...  769 us
    all_gather x2, waiting for transfers between devices, join_columns(): both = lax.all_gather(flipped, 'data', axis=1)  481 us
    ppermute x4, waiting for transfers between devices, device_epoch(): p_peer = lax.ppermute(p_mine, 'data', swap)  243 us
    pallas_call x4, Pallas kernels, tail_rows(): pl.pallas_call(tail_kernel, grid=(blocks,), in_specs=[smem_block(BLOCK),...  212 us
    pallas_call x4, Pallas kernels, query_rows(): pl.pallas_call(query_kernel, grid=(blocks,), in_specs=[smem_block(BLOCK),...  208 us
    sub x6, other arithmetic, adagrad(): param = param.reshape(rows, 2, LANES) - grad3 * step[:, None, None]  190 us
    ppermute x4, waiting for transfers between devices, device_epoch(): q_peer = lax.ppermute(q_mine, 'data', swap)  177 us
  transfers between devices with their start and end apart: 29, of which 19 were waited for; matrix products, arithmetic and copies ran while one was open for 14% of the time, Pallas kernels for 7%

profile of v1, /device:TPU:0, one launch (start us, length us, event | category | flops | bytes accessed | tf_op | source)
XLA Modules:
  0.0 4886.8 jit_solution(915750503730941360)
XLA Ops:
  186.0 53.3 %query_rows.4 = (f32[32768,128]{1,0:T(8,128)}, f32[32768,128]{1,0:T(8,128)}, bf16[16384,256]{1,0:T(8,128)(2,1)}) custom-call(s32[64,1,256]{2,1,0:T(1,128)} %bitcast.138, s32[64,1,256]{2,1,0:T(1,128)} %bitcast.134, f32[32768,128]{1,0:T(8,128)} %bitcast.97, f32[29648,128]{1,0:T(8,128)} %bitcast.107), custom_call_target="tpu_custom_call" | custom-call | flops 200000000 | bytes 80000000 | tf_op jit(solution)/shard_map/query_rows/pallas_call | solution.py:206
  269.7 52.9 %tail_rows.4 = (f32[32768,128]{1,0:T(8,128)}, f32[64,1,256]{2,1,0:T(1,128)}) custom-call(s32[64,1,256]{2,1,0:T(1,128)} %bitcast.136, f32[32768,128]{1,0:T(8,128)} %get-tuple-element.41.a_ref, f32[32768,128]{1,0:T(8,128)} %get-tuple-element.42.r_ref, bf16[32768,128]{1,0:T(8,128)(2,1)} %convert_element_type.43.tab_hbm), custom_call_target="tpu_custom_call" | custom-call | flops 200000000 | bytes 60000000 | tf_op jit(solution)/shard_map/tail_rows/pallas_call | solution.py:230
  324.6 105.5 %collective-permute-done.1.pp_ref = f32[64,1,256]{2,1,0:T(1,128)S(1)} collective-permute-done((f32[64,1,256]{2,1,0:T(1,128)}, f32[64,1,256]{2,1,0:T(1,128)S(1)}, u32[]{:S(2)}, u32[]{:S(2)}) %collective-permute-start.1) | collective-permute-done | bytes 65568 | tf_op jit(solution)/shard_map/ppermute | solution.py:354
  430.8 192.2 %bucket_grads.4 = (f32[32768,128]{1,0:T(8,128)}, f32[32768,128]{1,0:T(8,128)}, f32[29648,128]{1,0:T(8,128)}, f32[2,1,128]{2,1,0:T(1,128)}) custom-call(s32[64,1,256]{2,1,0:T(1,128)} %bitcast.139, s32[64,1,256]{2,1,0:T(1,128)} %bitcast.137, s32[64,1,256]{2,1,0:T(1,128)} %bitcast.135, s32[2,1,200]{2,1,0:T(1,128)} %get-tuple-element.120.neg_ref, ...), custom_call_target="tpu_custom_call" | custom-call | flops 500000000 | bytes 110000000 | tf_op jit(solution)/shard_map/bucket_grads/pallas_call | solution.py:257
  734.0 279.7 %all-reduce.17.cloned.1.call-done = f32[29648,128]{1,0:T(8,128)} async-done(((f32[29648,128]{1,0:T(8,128)}), f32[29648,128]{1,0:T(8,128)}) %all-reduce.17.cloned.1.call-update) | async-done | bytes 15179792 | tf_op jit(solution)/shard_map/psum | solution.py:361
  1108.0 51.7 %query_rows.5 = (f32[32768,128]{1,0:T(8,128)}, f32[32768,128]{1,0:T(8,128)}, bf16[16384,256]{1,0:T(8,128)(2,1)}) custom-call(s32[64,1,256]{2,1,0:T(1,128)} %bitcast.132, s32[64,1,256]{2,1,0:T(1,128)} %bitcast.128, f32[32768,128]{1,0:T(8,128)} %bitcast.94, f32[29648,128]{1,0:T(8,128)} %bitcast.108), custom_call_target="tpu_custom_call" | custom-call | flops 200000000 | bytes 80000000 | tf_op jit(solution)/shard_map/query_rows/pallas_call | solution.py:206
  1168.1 52.9 %tail_rows.5 = (f32[32768,128]{1,0:T(8,128)}, f32[64,1,256]{2,1,0:T(1,128)}) custom-call(s32[64,1,256]{2,1,0:T(1,128)} %bitcast.130, f32[32768,128]{1,0:T(8,128)} %get-tuple-element.49.a_ref, f32[32768,128]{1,0:T(8,128)} %get-tuple-element.50.r_ref, bf16[32768,128]{1,0:T(8,128)(2,1)} %collective-permute-done.3.tab_hbm), custom_call_target="tpu_custom_call" | custom-call | flops 200000000 | bytes 60000000 | tf_op jit(solution)/shard_map/tail_rows/pallas_call | solution.py:230
  1221.5 125.5 %collective-permute-done.5.pp_ref = f32[64,1,256]{2,1,0:T(1,128)S(1)} collective-permute-done((f32[64,1,256]{2,1,0:T(1,128)}, f32[64,1,256]{2,1,0:T(1,128)S(1)}, u32[]{:S(2)}, u32[]{:S(2)}) %collective-permute-start.5) | collective-permute-done | bytes 65568 | tf_op jit(solution)/shard_map/ppermute | solution.py:354
  1347.7 192.2 %bucket_grads.5 = (f32[32768,128]{1,0:T(8,128)}, f32[32768,128]{1,0:T(8,128)}, f32[29648,128]{1,0:T(8,128)}, f32[2,1,128]{2,1,0:T(1,128)}) custom-call(s32[64,1,256]{2,1,0:T(1,128)} %bitcast.133, s32[64,1,256]{2,1,0:T(1,128)} %bitcast.131, s32[64,1,256]{2,1,0:T(1,128)} %bitcast.129, s32[2,1,200]{2,1,0:T(1,128)} %get-tuple-element.119.neg_ref, ...), custom_call_target="tpu_custom_call" | custom-call | flops 500000000 | bytes 110000000 | tf_op jit(solution)/shard_map/bucket_grads/pallas_call | solution.py:257
  1540.0 380.2 %all-reduce.21.cloned.1.call-done = f32[29648,128]{1,0:T(8,128)} async-done(((f32[29648,128]{1,0:T(8,128)}), f32[29648,128]{1,0:T(8,128)}) %all-reduce.21.cloned.1.call-update) | async-done | bytes 15179792 | tf_op jit(solution)/shard_map/psum | solution.py:361
  2137.0 51.6 %query_rows.6 = (f32[32768,128]{1,0:T(8,128)}, f32[32768,128]{1,0:T(8,128)}, bf16[16384,256]{1,0:T(8,128)(2,1)}) custom-call(s32[64,1,256]{2,1,0:T(1,128)} %bitcast.126, s32[64,1,256]{2,1,0:T(1,128)} %bitcast.122, f32[32768,128]{1,0:T(8,128)} %bitcast.96, f32[29648,128]{1,0:T(8,128)} %bitcast.109), custom_call_target="tpu_custom_call" | custom-call | flops 200000000 | bytes 80000000 | tf_op jit(solution)/shard_map/query_rows/pallas_call | solution.py:206
  2189.4 65.8 %collective-permute-done.8.tab_hbm = bf16[32768,128]{1,0:T(8,128)(2,1)} collective-permute-done((bf16[32768,128]{1,0:T(8,128)(2,1)}, bf16[32768,128]{1,0:T(8,128)(2,1)}, u32[]{:S(2)}, u32[]{:S(2)}) %collective-permute-start.8) | collective-permute-done | bytes 8388640 | tf_op jit(solution)/shard_map/ppermute | solution.py:346
  2261.5 52.9 %tail_rows.6 = (f32[32768,128]{1,0:T(8,128)}, f32[64,1,256]{2,1,0:T(1,128)}) custom-call(s32[64,1,256]{2,1,0:T(1,128)} %bitcast.124, f32[32768,128]{1,0:T(8,128)} %get-tuple-element.57.a_ref, f32[32768,128]{1,0:T(8,128)} %get-tuple-element.58.r_ref, bf16[32768,128]{1,0:T(8,128)(2,1)} %collective-permute-done.8.tab_hbm), custom_call_target="tpu_custom_call" | custom-call | flops 200000000 | bytes 60000000 | tf_op jit(solution)/shard_map/tail_rows/pallas_call | solution.py:230
  2316.2 55.8 %collective-permute-done.9.qp_ref = bf16[16384,256]{1,0:T(8,128)(2,1)} collective-permute-done((bf16[16384,256]{1,0:T(8,128)(2,1)}, bf16[16384,256]{1,0:T(8,128)(2,1)}, u32[]{:S(2)}, u32[]{:S(2)}) %collective-permute-start.9) | collective-permute-done | bytes 8388640 | tf_op jit(solution)/shard_map/ppermute | solution.py:348
  2377.9 192.2 %bucket_grads.6 = (f32[32768,128]{1,0:T(8,128)}, f32[32768,128]{1,0:T(8,128)}, f32[29648,128]{1,0:T(8,128)}, f32[2,1,128]{2,1,0:T(1,128)}) custom-call(s32[64,1,256]{2,1,0:T(1,128)} %bitcast.127, s32[64,1,256]{2,1,0:T(1,128)} %bitcast.125, s32[64,1,256]{2,1,0:T(1,128)} %bitcast.123, s32[2,1,200]{2,1,0:T(1,128)} %get-tuple-element.118.neg_ref, ...), custom_call_target="tpu_custom_call" | custom-call | flops 500000000 | bytes 110000000 | tf_op jit(solution)/shard_map/bucket_grads/pallas_call | solution.py:257
  2570.8 502.2 %all-reduce.25.cloned.1.call-done = f32[29648,128]{1,0:T(8,128)} async-done(((f32[29648,128]{1,0:T(8,128)}), f32[29648,128]{1,0:T(8,128)}) %all-reduce.25.cloned.1.call-update) | async-done | bytes 15179792 | tf_op jit(solution)/shard_map/psum | solution.py:361
  3105.1 69.7 %collective-permute-done.12 = f32[32768,128]{1,0:T(8,128)} collective-permute-done((f32[32768,128]{1,0:T(8,128)}, f32[32768,128]{1,0:T(8,128)}, u32[]{:S(2)}, u32[]{:S(2)}) %collective-permute-start.12) | collective-permute-done | bytes 16777248 | tf_op jit(solution)/shard_map/ppermute | solution.py:360
  3343.3 51.6 %query_rows.7 = (f32[32768,128]{1,0:T(8,128)}, f32[32768,128]{1,0:T(8,128)}, bf16[16384,256]{1,0:T(8,128)(2,1)}) custom-call(s32[64,1,256]{2,1,0:T(1,128)} %bitcast.120, s32[64,1,256]{2,1,0:T(1,128)} %bitcast.116, f32[32768,128]{1,0:T(8,128)} %bitcast.92, f32[29648,128]{1,0:T(8,128)} %bitcast.110), custom_call_target="tpu_custom_call" | custom-call | flops 200000000 | bytes 80000000 | tf_op jit(solution)/shard_map/query_rows/pallas_call | solution.py:206
  3403.3 52.9 %tail_rows.7 = (f32[32768,128]{1,0:T(8,128)}, f32[64,1,256]{2,1,0:T(1,128)}) custom-call(s32[64,1,256]{2,1,0:T(1,128)} %bitcast.118, f32[32768,128]{1,0:T(8,128)} %get-tuple-element.65.a_ref, f32[32768,128]{1,0:T(8,128)} %get-tuple-element.66.r_ref, bf16[32768,128]{1,0:T(8,128)(2,1)} %collective-permute-done.13.tab_hbm), custom_call_target="tpu_custom_call" | custom-call | flops 200000000 | bytes 60000000 | tf_op jit(solution)/shard_map/tail_rows/pallas_call | solution.py:230
  3456.3 121.4 %collective-permute-done.14.qp_ref = bf16[16384,256]{1,0:T(8,128)(2,1)} collective-permute-done((bf16[16384,256]{1,0:T(8,128)(2,1)}, bf16[16384,256]{1,0:T(8,128)(2,1)}, u32[]{:S(2)}, u32[]{:S(2)}) %collective-permute-start.14) | collective-permute-done | bytes 8388640 | tf_op jit(solution)/shard_map/ppermute | solution.py:348
  3585.5 192.2 %bucket_grads.7 = (f32[32768,128]{1,0:T(8,128)}, f32[32768,128]{1,0:T(8,128)}, f32[29648,128]{1,0:T(8,128)}, f32[2,1,128]{2,1,0:T(1,128)}) custom-call(s32[64,1,256]{2,1,0:T(1,128)} %bitcast.121, s32[64,1,256]{2,1,0:T(1,128)} %bitcast.119, s32[64,1,256]{2,1,0:T(1,128)} %bitcast.117, s32[2,1,200]{2,1,0:T(1,128)} %get-tuple-element.117.neg_ref, ...), custom_call_target="tpu_custom_call" | custom-call | flops 500000000 | bytes 110000000 | tf_op jit(solution)/shard_map/bucket_grads/pallas_call | solution.py:257
  3779.0 379.3 %all-reduce.29.cloned.1.call-done = f32[29648,128]{1,0:T(8,128)} async-done(((f32[29648,128]{1,0:T(8,128)}), f32[29648,128]{1,0:T(8,128)}) %all-reduce.29.cloned.1.call-update) | async-done | bytes 15179792 | tf_op jit(solution)/shard_map/psum | solution.py:361
  4356.9 194.4 %all-gather.10.cloned.1.call-done = f32[2,200,14824]{2,0,1:T(2,128)} async-done(((f32[2,100,14824]{2,0,1:T(2,128)}), f32[2,200,14824]{2,0,1:T(2,128)}) %all-gather.10.cloned.1.call-update) | async-done | bytes 23718416 | tf_op jit(solution)/shard_map/all_gather | solution.py:301
  4571.9 286.5 %all-gather.8.cloned.1.call-done = f32[2,200,16384]{2,0,1:T(2,128)} async-done(((f32[2,100,16384]{2,0,1:T(2,128)}), f32[2,200,16384]{2,0,1:T(2,128)}) %all-gather.8.cloned.1.call-update) | async-done | bytes 26214416 | tf_op jit(solution)/shard_map/all_gather | solution.py:301
  (227 shorter events, 1116.9 us)
Async XLA Ops:
  7.2 174.3 %all-gather.12.cloned.1.call-start = ((), (), s32[]{:S(2)}) async-start(), calls=%async_computation.10 | async-start | bytes 1585152 | tf_op jit(solution)/shard_map/all_gather | solution.py:332
  12.5 659.8 %all-reduce.15.cloned.1.call-start = ((), (), s32[]{:S(2)}) async-start(), calls=%async_computation | async-start | bytes 131072 | tf_op jit(solution)/shard_map/psum | solution.py:308
  239.3 190.8 %collective-permute-start = (bf16[16384,256]{1,0:T(8,128)(2,1)}, bf16[16384,256]{1,0:T(8,128)(2,1)}, u32[]{:S(2)}, u32[]{:S(2)}) collective-permute-start(bf16[16384,256]{1,0:T(8,128)(2,1)} %get-tuple-element.44), channel_id=1, source_target_pairs={{0,4},{4,0},{1,5},{5,1},{2,6},{6,2},{3,7},{7,3}} | collective-permute-start | bytes 25165832 | tf_op jit(solution)/shard_map/ppermute | solution.py:348
  260.7 169.4 %collective-permute-start.2 = (bf16[2,256,256]{2,1,0:T(8,128)(2,1)S(1)}, bf16[2,256,256]{2,1,0:T(8,128)(2,1)S(1)}, u32[]{:S(2)}, u32[]{:S(2)}) collective-permute-start(bf16[2,256,256]{2,1,0:T(8,128)(2,1)S(1)} %pad.23.mm_ref), channel_id=1, source_target_pairs={{0,4},{4,0},{1,5},{5,1},{2,6},{6,2},{3,7},{7,3}} | collective-permute-start | bytes 786440 | tf_op jit(solution)/shard_map/ppermute | solution.py:353
  655.6 358.1 %all-reduce.17.cloned.1.call-start = ((), (), s32[]{:S(2)}) async-start(), calls=%async_computation.1 | async-start | bytes 30359552 | tf_op jit(solution)/shard_map/psum | solution.py:361
  656.4 1263.9 %all-reduce.21.cloned.1.call-start = ((), (), s32[]{:S(2)}) async-start(), calls=%async_computation.3 | async-start | bytes 30359552 | tf_op jit(solution)/shard_map/psum | solution.py:361
  733.6 426.9 %collective-permute-start.3 = (bf16[32768,128]{1,0:T(8,128)(2,1)}, bf16[32768,128]{1,0:T(8,128)(2,1)}, u32[]{:S(2)}, u32[]{:S(2)}) collective-permute-start(bf16[32768,128]{1,0:T(8,128)(2,1)} %convert_element_type.47), channel_id=1, source_target_pairs={{1,0},{2,1},{3,2},{0,3},{5,4},{6,5},{7,6},{4,7}} | collective-permute-start | bytes 25165832 | tf_op jit(solution)/shard_map/ppermute | solution.py:346
  1159.8 187.2 %collective-permute-start.4 = (bf16[16384,256]{1,0:T(8,128)(2,1)}, bf16[16384,256]{1,0:T(8,128)(2,1)}, u32[]{:S(2)}, u32[]{:S(2)}) collective-permute-start(bf16[16384,256]{1,0:T(8,128)(2,1)} %get-tuple-element.52), channel_id=1, source_target_pairs={{0,4},{4,0},{1,5},{5,1},{2,6},{6,2},{3,7},{7,3}} | collective-permute-start | bytes 25165832 | tf_op jit(solution)/shard_map/ppermute | solution.py:348
  1166.6 180.4 %collective-permute-start.6 = (bf16[2,256,256]{2,1,0:T(8,128)(2,1)S(1)}, bf16[2,256,256]{2,1,0:T(8,128)(2,1)S(1)}, u32[]{:S(2)}, u32[]{:S(2)}) collective-permute-start(bf16[2,256,256]{2,1,0:T(8,128)(2,1)S(1)} %pad.24.mm_ref), channel_id=1, source_target_pairs={{0,4},{4,0},{1,5},{5,1},{2,6},{6,2},{3,7},{7,3}} | collective-permute-start | bytes 786440 | tf_op jit(solution)/shard_map/ppermute | solution.py:353
  1539.9 427.0 %collective-permute-start.7 = (f32[32768,128]{1,0:T(8,128)}, f32[32768,128]{1,0:T(8,128)}, u32[]{:S(2)}, u32[]{:S(2)}) collective-permute-start(f32[32768,128]{1,0:T(8,128)} %get-tuple-element.55), channel_id=1, source_target_pairs={{0,1},{1,2},{2,3},{3,0},{4,5},{5,6},{6,7},{7,4}} | collective-permute-start | bytes 50331656 | tf_op jit(solution)/shard_map/ppermute | solution.py:360
  1540.0 474.1 %all-reduce.19.cloned.1.call-start = ((), (), s32[]{:S(2)}) async-start(), calls=%async_computation.2 | async-start | bytes 131072 | tf_op jit(solution)/shard_map/psum | solution.py:308
  1999.6 1073.4 %all-reduce.25.cloned.1.call-start = ((), (), s32[]{:S(2)}) async-start(), calls=%async_computation.5 | async-start | bytes 30359552 | tf_op jit(solution)/shard_map/psum | solution.py:361
  2073.4 181.8 %collective-permute-start.8 = (bf16[32768,128]{1,0:T(8,128)(2,1)}, bf16[32768,128]{1,0:T(8,128)(2,1)}, u32[]{:S(2)}, u32[]{:S(2)}) collective-permute-start(bf16[32768,128]{1,0:T(8,128)(2,1)} %convert_element_type.50), channel_id=1, source_target_pairs={{2,0},{3,1},{0,2},{1,3},{6,4},{7,5},{4,6},{5,7}} | collective-permute-start | bytes 25165832 | tf_op jit(solution)/shard_map/ppermute | solution.py:346
  2188.7 183.3 %collective-permute-start.9 = (bf16[16384,256]{1,0:T(8,128)(2,1)}, bf16[16384,256]{1,0:T(8,128)(2,1)}, u32[]{:S(2)}, u32[]{:S(2)}) collective-permute-start(bf16[16384,256]{1,0:T(8,128)(2,1)} %get-tuple-element.60), channel_id=1, source_target_pairs={{0,4},{4,0},{1,5},{5,1},{2,6},{6,2},{3,7},{7,3}} | collective-permute-start | bytes 25165832 | tf_op jit(solution)/shard_map/ppermute | solution.py:348
  2570.1 604.7 %collective-permute-start.12 = (f32[32768,128]{1,0:T(8,128)}, f32[32768,128]{1,0:T(8,128)}, u32[]{:S(2)}, u32[]{:S(2)}) collective-permute-start(f32[32768,128]{1,0:T(8,128)} %get-tuple-element.63), channel_id=1, source_target_pairs={{0,2},{1,3},{2,0},{3,1},{4,6},{5,7},{6,4},{7,5}} | collective-permute-start | bytes 50331656 | tf_op jit(solution)/shard_map/ppermute | solution.py:360
  2570.7 651.2 %all-reduce.23.cloned.1.call-start = ((), (), s32[]{:S(2)}) async-start(), calls=%async_computation.4 | async-start | bytes 131072 | tf_op jit(solution)/shard_map/psum | solution.py:308
  3207.4 950.9 %all-reduce.29.cloned.1.call-start = ((), (), s32[]{:S(2)}) async-start(), calls=%async_computation.7 | async-start | bytes 30359552 | tf_op jit(solution)/shard_map/psum | solution.py:361
  3395.0 182.7 %collective-permute-start.14 = (bf16[16384,256]{1,0:T(8,128)(2,1)}, bf16[16384,256]{1,0:T(8,128)(2,1)}, u32[]{:S(2)}, u32[]{:S(2)}) collective-permute-start(bf16[16384,256]{1,0:T(8,128)(2,1)} %get-tuple-element.68), channel_id=1, source_target_pairs={{0,4},{4,0},{1,5},{5,1},{2,6},{6,2},{3,7},{7,3}} | collective-permute-start | bytes 25165832 | tf_op jit(solution)/shard_map/ppermute | solution.py:348
  3401.3 183.4 %collective-permute-start.16 = (bf16[2,256,256]{2,1,0:T(8,128)(2,1)S(1)}, bf16[2,256,256]{2,1,0:T(8,128)(2,1)S(1)}, u32[]{:S(2)}, u32[]{:S(2)}) collective-permute-start(bf16[2,256,256]{2,1,0:T(8,128)(2,1)S(1)} %pad.26.mm_ref), channel_id=1, source_target_pairs={{0,4},{4,0},{1,5},{5,1},{2,6},{6,2},{3,7},{7,3}} | collective-permute-start | bytes 786440 | tf_op jit(solution)/shard_map/ppermute | solution.py:353
  3456.1 128.6 %collective-permute-start.15 = (f32[64,1,256]{2,1,0:T(1,128)}, f32[64,1,256]{2,1,0:T(1,128)S(1)}, u32[]{:S(2)}, u32[]{:S(2)}) collective-permute-start(f32[64,1,256]{2,1,0:T(1,128)} %get-tuple-element.69.pm_ref), channel_id=1, source_target_pairs={{0,4},{4,0},{1,5},{5,1},{2,6},{6,2},{3,7},{7,3}} | collective-permute-start | bytes 196616 | tf_op jit(solution)/shard_map/ppermute | solution.py:354
  3777.7 426.0 %collective-permute-start.17 = (f32[32768,128]{1,0:T(8,128)}, f32[32768,128]{1,0:T(8,128)}, u32[]{:S(2)}, u32[]{:S(2)}) collective-permute-start(f32[32768,128]{1,0:T(8,128)} %get-tuple-element.71), channel_id=1, source_target_pairs={{0,3},{1,0},{2,1},{3,2},{4,7},{5,4},{6,5},{7,6}} | collective-permute-start | bytes 50331656 | tf_op jit(solution)/shard_map/ppermute | solution.py:360
  3779.0 496.3 %all-reduce.27.cloned.1.call-start = ((), (), s32[]{:S(2)}) async-start(), calls=%async_computation.6 | async-start | bytes 131072 | tf_op jit(solution)/shard_map/psum | solution.py:308
  4236.4 315.0 %all-gather.10.cloned.1.call-start = ((), (), s32[]{:S(2)}) async-start(), calls=%async_computation.9 | async-start | bytes 35635200 | tf_op jit(solution)/shard_map/all_gather | solution.py:301
  4275.2 583.2 %all-gather.8.cloned.1.call-start = ((), (), s32[]{:S(2)}) async-start(), calls=%async_computation.8 | async-start | bytes 39321600 | tf_op jit(solution)/shard_map/all_gather | solution.py:301
  (37 other events, 1448.2 us)
Sparse Core Ops, SparseCore 0:
  12.6 21.0 all-gather.11
  655.8 16.4 all-reduce.14
  674.8 338.9 all-reduce.16
  1540.1 380.1 all-reduce.20
  1999.7 14.3 all-reduce.18
  2570.9 502.0 all-reduce.24
  3207.5 14.3 all-reduce.22
  3779.1 379.2 all-reduce.28
  4236.5 15.7 all-reduce.26
  4275.3 276.0 all-gather.9
  4553.5 304.8 all-gather.7

commit v2 on v1

v2 whole, which is shorter than its diff:
```python
import functools

import jax
import jax.numpy as jnp
from jax import lax
from jax.experimental import pallas as pl
from jax.experimental.pallas import tpu as pltpu
from jax.sharding import PartitionSpec as P


LEARN_ENT = 0.1
LEARN_REL = 0.05
ADA_EPS = 1e-6
LANES = 128
BLOCK = 256
WIDE_ROWS = 512
VMEM_CAP = 66_000_000


def pair_at(row):
    return pl.ds(pl.multiple_of(row, 2), 2)


def halves(ref):
    count = ref.shape[0] // 2
    return ref[pl.ds(0, count, stride=2), :], ref[pl.ds(1, count, stride=2), :]


def put_halves(ref, real, imag):
    count = ref.shape[0] // 2
    ref[pl.ds(0, count, stride=2), :] = real
    ref[pl.ds(1, count, stride=2), :] = imag


def split_kernel(width, part_ref, in_ref, out_ref, *bf_refs):
    second = part_ref[0] != 0
    lane = lax.broadcasted_iota(jnp.int32, (out_ref.shape[0] // 2, LANES), 1)

    def pick(start):
        last = in_ref.shape[0] - LANES
        shift = max(start - last, 0)
        rows = in_ref[pl.ds(start - shift, LANES), :].T
        if shift:
            rows = pltpu.roll(rows, LANES - shift, 1)
        return jnp.where(lane < width, rows, 0.0)

    real = jnp.where(second, pick(width), pick(0))
    imag = jnp.where(second, pick(3 * width), pick(2 * width))
    put_halves(out_ref, real, imag)
    for ref in bf_refs:
        ref[...] = out_ref[...].astype(jnp.bfloat16)


def split_columns(table, part, with_bf):
    rows, dim = table.shape
    pairs = pl.BlockSpec((2 * WIDE_ROWS, LANES), lambda b: (b, 0))
    kinds = [jnp.float32, jnp.bfloat16] if with_bf else [jnp.float32]
    return pl.pallas_call(
        functools.partial(split_kernel, dim // 4),
        grid=(pl.cdiv(rows, WIDE_ROWS),),
        in_specs=[pl.BlockSpec(memory_space=pltpu.SMEM), pl.BlockSpec((dim, WIDE_ROWS), lambda b: (0, b))],
        out_specs=[pairs] * len(kinds),
        out_shape=[jax.ShapeDtypeStruct((2 * rows, LANES), kind) for kind in kinds],
        compiler_params=pltpu.CompilerParams(dimension_semantics=("arbitrary",)),
        cost_estimate=pl.CostEstimate(flops=20_000_000, bytes_accessed=45_000_000, transcendentals=0),
        name="split_columns",
    )(part[None], table.T)


def flip_kernel(in_ref, out_ref):
    real, imag = halves(in_ref)
    width = out_ref.shape[1]
    out_ref[0] = real.T[:width, :]
    out_ref[1] = imag.T[:width, :]


def flip_half(half, dim):
    rows = half.shape[0] // 2
    return pl.pallas_call(
        flip_kernel,
        grid=(pl.cdiv(rows, WIDE_ROWS),),
        in_specs=[pl.BlockSpec((2 * WIDE_ROWS, LANES), lambda b: (b, 0))],
        out_specs=pl.BlockSpec((2, dim // 4, WIDE_ROWS), lambda b: (0, 0, b)),
        out_shape=jax.ShapeDtypeStruct((2, dim // 4, rows), jnp.float32),
        compiler_params=pltpu.CompilerParams(dimension_semantics=("arbitrary",)),
        cost_estimate=pl.CostEstimate(flops=20_000_000, bytes_accessed=30_000_000, transcendentals=0),
        name="flip_half",
    )(half)


def query_kernel(core_ref, head_ref, rel_ref, ent_hbm, relm_hbm, relo_hbm, a_ref, r_ref, q_ref, ent_v, rel_v, sems):
    @pl.when(pl.program_id(0) == 0)
    def _():
        half = relm_hbm.shape[0]
        core = core_ref[0]
        mine = pl.ds(pl.multiple_of(core * half, 8), half)
        other = pl.ds(pl.multiple_of((1 - core) * half, 8), half)
        copies = [
            pltpu.make_async_copy(ent_hbm, ent_v, sems.at[0]),
            pltpu.make_async_copy(relm_hbm, rel_v.at[mine], sems.at[1]),
            pltpu.make_async_copy(relo_hbm, rel_v.at[other], sems.at[2]),
        ]
        for copy in copies:
            copy.start()
        for copy in copies:
            copy.wait()

    unroll = 32

    def some(step, carry):
        for sub in range(unroll):
            edge = step * unroll + sub
            a_ref[pair_at(2 * edge), :] = ent_v[pair_at(head_ref[0, 0, edge]), :]
            r_ref[pair_at(2 * edge), :] = rel_v[pair_at(rel_ref[0, 0, edge]), :]
        return carry

    lax.fori_loop(0, BLOCK // unroll, some, 0)
    a_re, a_im = halves(a_ref)
    r_re, r_im = halves(r_ref)
    q_ref[:, :LANES] = (a_re * r_re - a_im * r_im).astype(jnp.bfloat16)
    q_ref[:, LANES:] = (a_re * r_im + a_im * r_re).astype(jnp.bfloat16)


def tail_kernel(negs, tail_ref, neg_ref, a_ref, r_ref, tab_hbm, c_ref, p_ref, m_ref, tab_bf, tab_v, neg_v, sem):
    @pl.when(pl.program_id(0) == 0)
    def _():
        copy = pltpu.make_async_copy(tab_hbm, tab_bf, sem)
        copy.start()
        copy.wait()
        rows = 512

        def widen(step, carry):
            at = pl.ds(pl.multiple_of(step * rows, rows), rows)
            tab_v[at, :] = tab_bf[at, :].astype(jnp.float32)
            return carry

        lax.fori_loop(0, tab_v.shape[0] // rows, widen, 0)
        neg_v[...] = jnp.zeros_like(neg_v)
        small = 8

        def pick(step, carry):
            for sub in range(small):
                row = step * small + sub
                neg_v[pair_at(2 * row), :] = tab_v[pair_at(neg_ref[0, 0, row]), :]
            return carry

        lax.fori_loop(0, negs // small, pick, 0)
        m_re, m_im = halves(neg_v)
        m_ref[:, :LANES] = m_re.astype(jnp.bfloat16)
        m_ref[:, LANES:] = m_im.astype(jnp.bfloat16)

    unroll = 32

    def some(step, carry):
        for sub in range(unroll):
            edge = step * unroll + sub
            c_ref[pair_at(2 * edge), :] = tab_v[pair_at(tail_ref[0, 0, edge]), :]
        return carry

    lax.fori_loop(0, BLOCK // unroll, some, 0)
    a_re, a_im = halves(a_ref)
    r_re, r_im = halves(r_ref)
    c_re, c_im = halves(c_ref)
    prod = (a_re * r_re - a_im * r_im) * c_re + (a_re * r_im + a_im * r_re) * c_im
    p_ref[0] = jnp.sum(prod.T, axis=0, keepdims=True)


def column(row):
    return jnp.broadcast_to(row, (LANES, row.shape[-1])).T


def grad_kernel(
    last, negs,
    core_ref, head_ref, tail_ref, rel_ref, neg_ref, a_ref, r_ref, c_ref, qm_ref, qp_ref, pm_ref, pp_ref, w_ref, mm_ref, mp_ref,
    *rest,
):
    before, rest = rest[:3 * last], rest[3 * last:]
    outs, (loss_ref, acc_h, acc_t, acc_r, blk_h, blk_t, blk_r, neg_acc, sems) = rest[:3 + last], rest[3 + last:]
    block = pl.program_id(0)
    accs = (acc_h, acc_t, acc_r)

    @pl.when(block == 0)
    def _():
        neg_acc[...] = jnp.zeros_like(neg_acc)
        loss_ref[...] = jnp.zeros_like(loss_ref)
        if last:
            copies = [pltpu.make_async_copy(src, acc, sems.at[slot]) for slot, (src, acc) in enumerate(zip(before, accs))]
            for copy in copies:
                copy.start()
            for copy in copies:
                copy.wait()
        else:
            rows = 16
            for acc in accs:
                def clear(step, carry, acc=acc):
                    acc[pl.ds(pl.multiple_of(step * rows, rows), rows), :] = jnp.zeros((rows, LANES), jnp.float32)
                    return carry

                lax.fori_loop(0, acc.shape[0] // rows, clear, 0)

    a_re, a_im = halves(a_ref)
    r_re, r_im = halves(r_ref)
    c_re, c_im = halves(c_ref)
    q_re = a_re * r_re - a_im * r_im
    q_im = a_re * r_im + a_im * r_re
    q_bf = qm_ref[...]
    m_mine = mm_ref[...]
    nt = (((1,), (1,)), ((), ()))
    score = lax.dot_general(q_bf, m_mine, nt, preferred_element_type=jnp.float32)
    score = score + lax.dot_general(qp_ref[...], mp_ref[...], nt, preferred_element_type=jnp.float32)
    lane = lax.broadcasted_iota(jnp.int32, score.shape, 1)
    score = jnp.where(lane < negs, score, -jnp.inf)
    pos = column(pm_ref[0] + pp_ref[0])
    weight = column(w_ref[0])
    low, high = score[:, :LANES], score[:, LANES:]
    top = jnp.maximum(pos, jnp.max(jnp.maximum(low, high), axis=1, keepdims=True))
    pos_exp = jnp.exp(pos - top)
    low_exp, high_exp = jnp.exp(low - top), jnp.exp(high - top)
    norm = pos_exp + jnp.sum(low_exp + high_exp, axis=1, keepdims=True)
    loss_ref[...] += jnp.sum(weight * (top + jnp.log(norm) - pos), axis=0, keepdims=True)
    alpha = weight * (pos_exp / norm - 1.0)
    scale = weight / norm
    beta = jnp.concatenate([(scale * low_exp).astype(jnp.bfloat16), (scale * high_exp).astype(jnp.bfloat16)], axis=1)
    nn = (((1,), (0,)), ((), ()))
    mixed = lax.dot_general(beta, m_mine, nn, preferred_element_type=jnp.float32)
    tn = (((0,), (0,)), ((), ()))
    neg_acc[...] += lax.dot_general(beta, q_bf, tn, preferred_element_type=jnp.float32)
    d_re = alpha * c_re + mixed[:, :LANES]
    d_im = alpha * c_im + mixed[:, LANES:]
    put_halves(blk_t, alpha * q_re, alpha * q_im)
    put_halves(blk_h, d_re * r_re + d_im * r_im, d_im * r_re - d_re * r_im)
    put_halves(blk_r, d_re * a_re + d_im * a_im, d_im * a_re - d_re * a_im)

    unroll = 16

    def some(step, carry):
        for sub in range(unroll):
            edge = step * unroll + sub
            here = pair_at(2 * edge)
            at_h, at_t, at_r = (pair_at(ref[0, 0, edge]) for ref in (head_ref, tail_ref, rel_ref))
            acc_h[at_h, :] = acc_h[at_h, :] + blk_h[here, :]
            acc_t[at_t, :] = acc_t[at_t, :] + blk_t[here, :]
            acc_r[at_r, :] = acc_r[at_r, :] + blk_r[here, :]
        return carry

    lax.fori_loop(0, BLOCK // unroll, some, 0)

    @pl.when(block == pl.num_programs(0) - 1)
    def _():
        put_halves(blk_t, neg_acc[:, :LANES], neg_acc[:, LANES:])
        small = 8

        def more(step, carry):
            for sub in range(small):
                row = step * small + sub
                at_t = pair_at(neg_ref[0, 0, row])
                acc_t[at_t, :] = acc_t[at_t, :] + blk_t[pair_at(2 * row), :]
            return carry

        lax.fori_loop(0, negs // small, more, 0)
        sources = list(accs)
        if last:
            half = acc_r.shape[0] // 2
            core = core_ref[0]
            sources[2:] = [acc_r.at[pl.ds(pl.multiple_of(at * half, 8), half)] for at in (core, 1 - core)]
        copies = [pltpu.make_async_copy(src, out, sems.at[slot]) for slot, (src, out) in enumerate(zip(sources, outs))]
        for copy in copies:
            copy.start()
        for copy in copies:
            copy.wait()


def smem_block(width):
    return pl.BlockSpec((1, 1, width), lambda b: (b, 0, 0), memory_space=pltpu.SMEM)


PAIRS = pl.BlockSpec((2 * BLOCK, LANES), lambda b: (b, 0))
WIDE = pl.BlockSpec((BLOCK, 2 * LANES), lambda b: (b, 0))
ROW = pl.BlockSpec((1, 1, BLOCK), lambda b: (b, 0, 0))
NEGS = pl.BlockSpec((2 * LANES, 2 * LANES), lambda b: (0, 0))
ANYWHERE = pl.BlockSpec(memory_space=pl.ANY)
SCALARS = pl.BlockSpec(memory_space=pltpu.SMEM)
PARAMS = dict(dimension_semantics=("arbitrary",), vmem_limit_bytes=VMEM_CAP)


def query_rows(core, ent, rel_mine, rel_other, head_ids, rel_ids):
    blocks = head_ids.shape[0]
    edges = blocks * BLOCK
    return pl.pallas_call(
        query_kernel,
        grid=(blocks,),
        in_specs=[SCALARS, smem_block(BLOCK), smem_block(BLOCK), ANYWHERE, ANYWHERE, ANYWHERE],
        out_specs=[PAIRS, PAIRS, WIDE],
        out_shape=[
            jax.ShapeDtypeStruct((2 * edges, LANES), jnp.float32),
            jax.ShapeDtypeStruct((2 * edges, LANES), jnp.float32),
            jax.ShapeDtypeStruct((edges, 2 * LANES), jnp.bfloat16),
        ],
        scratch_shapes=[
            pltpu.VMEM(ent.shape, jnp.float32),
            pltpu.VMEM((2 * rel_mine.shape[0], LANES), jnp.float32),
            pltpu.SemaphoreType.DMA((3,)),
        ],
        compiler_params=pltpu.CompilerParams(**PARAMS),
        cost_estimate=pl.CostEstimate(flops=100_000_000, bytes_accessed=80_000_000, transcendentals=0),
        name="query_rows",
    )(core, head_ids, rel_ids, ent, rel_mine, rel_other)


def tail_rows(table, tail_ids, neg_ids, a_rows, r_rows):
    blocks = tail_ids.shape[0]
    edges = blocks * BLOCK
    negs = neg_ids.shape[-1]
    return pl.pallas_call(
        functools.partial(tail_kernel, negs),
        grid=(blocks,),
        in_specs=[smem_block(BLOCK), SCALARS, PAIRS, PAIRS, ANYWHERE],
        out_specs=[PAIRS, ROW, NEGS],
        out_shape=[
            jax.ShapeDtypeStruct((2 * edges, LANES), jnp.float32),
            jax.ShapeDtypeStruct((blocks, 1, BLOCK), jnp.float32),
            jax.ShapeDtypeStruct((2 * LANES, 2 * LANES), jnp.bfloat16),
        ],
        scratch_shapes=[
            pltpu.VMEM(table.shape, jnp.bfloat16),
            pltpu.VMEM(table.shape, jnp.float32),
            pltpu.VMEM((4 * LANES, LANES), jnp.float32),
            pltpu.SemaphoreType.DMA,
        ],
        compiler_params=pltpu.CompilerParams(**PARAMS),
        cost_estimate=pl.CostEstimate(flops=100_000_000, bytes_accessed=60_000_000, transcendentals=0),
        name="tail_rows",
    )(tail_ids, neg_ids, a_rows, r_rows, table)


def bucket_grads(core, ids, neg_ids, rows, queries, scores, weight, negatives, before, ent_shape, rel_shape):
    blocks = ids[0].shape[0]
    last = before is not None
    before = before or ()
    half_shape = (rel_shape[0] // 2, LANES)
    shapes = [ent_shape, ent_shape] + ([half_shape, half_shape] if last else [rel_shape])
    return pl.pallas_call(
        functools.partial(grad_kernel, int(last), neg_ids.shape[-1]),
        grid=(blocks,),
        in_specs=[SCALARS] + [smem_block(BLOCK)] * 3 + [SCALARS] + [PAIRS] * 3 + [WIDE] * 2 + [ROW] * 3 + [NEGS] * 2
        + [ANYWHERE] * len(before),
        out_specs=[ANYWHERE] * len(shapes) + [pl.BlockSpec((1, LANES), lambda b: (0, 0))],
        out_shape=[jax.ShapeDtypeStruct(shape, jnp.float32) for shape in shapes + [(1, LANES)]],
        scratch_shapes=[
            pltpu.VMEM(ent_shape, jnp.float32),
            pltpu.VMEM(ent_shape, jnp.float32),
            pltpu.VMEM(rel_shape, jnp.float32),
            pltpu.VMEM((2 * BLOCK, LANES), jnp.float32),
            pltpu.VMEM((2 * BLOCK, LANES), jnp.float32),
            pltpu.VMEM((2 * BLOCK, LANES), jnp.float32),
            pltpu.VMEM((2 * LANES, 2 * LANES), jnp.float32),
            pltpu.SemaphoreType.DMA((4,)),
        ],
        compiler_params=pltpu.CompilerParams(**PARAMS),
        cost_estimate=pl.CostEstimate(flops=300_000_000, bytes_accessed=200_000_000, transcendentals=2_000_000),
        name="bucket_grads",
    )(core, *ids, neg_ids, *rows, *queries, *scores, weight, *negatives, *before)


def square_kernel(one_ref, two_ref, *rest):
    g_ref, sum_ref = rest[-2:]
    g_ref[...] = one_ref[...] + two_ref[...]
    real, imag = halves(g_ref)
    sum_ref[0] = jnp.sum((real * real + imag * imag).T, axis=0, keepdims=True)


def step_kernel(rate, dim, par_ref, g_ref, state_ref, sm_ref, sp_ref, out_ref, new_ref, *bf_refs):
    state = state_ref[0] + (sm_ref[0] + sp_ref[0]) / dim
    new_ref[0] = state
    scale = column(rate / jnp.sqrt(state + ADA_EPS))
    p_re, p_im = halves(par_ref)
    g_re, g_im = halves(g_ref)
    put_halves(out_ref, p_re - g_re * scale, p_im - g_im * scale)
    for ref in bf_refs:
        ref[...] = out_ref[...].astype(jnp.bfloat16)


def adagrad(param, state, one, two, rate, dim, swap, with_bf, after=()):
    blocks = state.shape[0]
    pairs = pl.BlockSpec((2 * WIDE_ROWS, LANES), lambda b: (b, 0))
    row = pl.BlockSpec((1, 1, WIDE_ROWS), lambda b: (b, 0, 0))
    wide = jax.ShapeDtypeStruct(param.shape, jnp.float32)
    narrow = jax.ShapeDtypeStruct(state.shape, jnp.float32)
    params = pltpu.CompilerParams(dimension_semantics=("arbitrary",))
    size = 4 * param.size
    grad, sums = pl.pallas_call(
        square_kernel,
        grid=(blocks,),
        in_specs=[pairs, pairs] + [ANYWHERE] * len(after),
        out_specs=[pairs, row],
        out_shape=[wide, narrow],
        compiler_params=params,
        cost_estimate=pl.CostEstimate(flops=4 * param.size, bytes_accessed=3 * size, transcendentals=0),
        name="square_sums",
    )(one, two, *after)
    sums_peer = lax.ppermute(sums, "data", swap)
    bf_shapes = [jax.ShapeDtypeStruct(param.shape, jnp.bfloat16)] if with_bf else []
    return pl.pallas_call(
        functools.partial(step_kernel, rate, dim),
        grid=(blocks,),
        in_specs=[pairs, pairs, row, row, row],
        out_specs=[pairs, row] + [pairs] * len(bf_shapes),
        out_shape=[wide, narrow] + bf_shapes,
        compiler_params=params,
        cost_estimate=pl.CostEstimate(flops=4 * param.size, bytes_accessed=3 * size, transcendentals=0),
        name="adagrad_step",
    )(param, grad, state, sums, sums_peer)


def solution(mesh):
    ent_size = mesh.shape["ent"]
    data_size = mesh.shape["data"]
    swap = [(src, data_size - 1 - src) for src in range(data_size)]
    core_swap = [(src, src ^ 1) for src in range(ent_size)]
    chip_swap = [(src, src ^ 2) for src in range(ent_size)]

    def device_epoch(ent_table, ada_state, rel_table, head_idx, tail_idx, rel_idx, edge_mask, neg_idx):
        _, dim = ent_table.shape
        rel_rows = rel_table.shape[0]
        edge_count = head_idx.shape[-1]
        negs = neg_idx.shape[-1]
        part = lax.axis_index("data")
        core = lax.rem(lax.axis_index("ent"), 2)
        core_at = core[None]
        ent, table = split_columns(ent_table, part, True)
        rel = split_columns(rel_table, part, False)[0]
        ent_shape, rel_shape = ent.shape, rel.shape
        rel_mine = lax.dynamic_slice_in_dim(rel, core * rel_rows, rel_rows, axis=0)
        rel_other = lax.dynamic_slice_in_dim(rel, (1 - core) * rel_rows, rel_rows, axis=0)
        state = ada_state.reshape(-1, 1, WIDE_ROWS)
        rel_state = jnp.zeros((pl.cdiv(rel_rows // 2, WIDE_ROWS), 1, WIDE_ROWS), jnp.float32)

        local = jnp.concatenate(
            [2 * head_idx[0, 0], 2 * tail_idx[0, 0], 2 * rel_idx[0, 0], edge_mask[0, 0], 2 * neg_idx[0, 0]], axis=1)
        both = lax.all_gather(local, "data")
        blocks = edge_count // BLOCK

        def field(slot, bucket, round_idx):
            return both[bucket, round_idx, slot * edge_count:(slot + 1) * edge_count].reshape(blocks, 1, BLOCK)

        losses = []
        for round_idx in range(ent_size):
            if round_idx:
                fetch = [((dest + round_idx) % ent_size, dest) for dest in range(ent_size)]
                table = lax.ppermute(table, "ent", fetch)
            ids = [[field(slot, bucket, round_idx) for slot in range(3)] for bucket in range(data_size)]
            asked = [query_rows(core_at, ent, rel_mine, rel_other, ids[bucket][0], ids[bucket][2]) for bucket in range(data_size)]
            before = None
            sums = []
            for bucket in range(data_size):
                a_rows, r_rows, q_mine = asked[bucket]
                q_peer = lax.ppermute(q_mine, "data", swap)
                neg_ids = both[bucket, round_idx, 4 * edge_count:].reshape(1, 1, negs)
                c_rows, p_mine, m_mine = tail_rows(table, ids[bucket][1], neg_ids, a_rows, r_rows)
                m_peer = lax.ppermute(m_mine, "data", swap)
                p_peer = lax.ppermute(p_mine, "data", swap)
                *before, loss = bucket_grads(
                    core_at, ids[bucket], neg_ids, (a_rows, r_rows, c_rows), (q_mine, q_peer), (p_mine, p_peer),
                    field(3, bucket, round_idx).astype(jnp.float32), (m_mine, m_peer), before, ent_shape, rel_shape)
                sums.append(loss[0, 0])
            g_head, g_tail, keep, give = before
            if round_idx:
                back = [(src, (src + round_idx) % ent_size) for src in range(ent_size)]
                g_tail = lax.ppermute(g_tail, "ent", back)
            chip_sum = keep + lax.ppermute(give, "ent", core_swap)
            chip_other = lax.ppermute(chip_sum, "ent", chip_swap)
            ent, state, table = adagrad(ent, state, g_head, g_tail, LEARN_ENT, dim, swap, True)
            rel_mine, rel_state = adagrad(rel_mine, rel_state, chip_sum, chip_other, LEARN_REL, dim, swap, False, (state,))
            if round_idx < ent_size - 1:
                rel_other = lax.ppermute(rel_mine, "ent", core_swap)
            losses.append(jnp.where(part == 0, sums[0], sums[1]) / edge_count)

        def join(half):
            flipped = flip_half(half, dim)
            peer = lax.ppermute(flipped, "data", swap)
            first = jnp.where(part == 0, flipped, peer)
            second = jnp.where(part == 0, peer, flipped)
            return jnp.stack([first, second], axis=1).reshape(dim, -1)

        ent_out = join(ent).T
        rel_cols = join(rel_mine)
        rel_cols_other = lax.ppermute(rel_cols, "ent", core_swap)
        rel_out = jnp.concatenate(
            [jnp.where(core == 0, rel_cols, rel_cols_other), jnp.where(core == 0, rel_cols_other, rel_cols)], axis=1).T
        return ent_out, state.reshape(-1), rel_out, jnp.stack(losses)[None, None, :]

    ent_spec = P(("sweep", "ent"), None)
    row_spec = P(("sweep", "ent"))
    rel_spec = P("sweep", None)
    edge_spec = P(("sweep", "ent"), "data", None, None)
    loss_spec = P(("sweep", "ent"), "data", None)
    return jax.shard_map(
        device_epoch, mesh=mesh,
        in_specs=(ent_spec, row_spec, rel_spec, edge_spec, edge_spec, edge_spec, edge_spec, edge_spec),
        out_specs=(ent_spec, row_spec, rel_spec, loss_spec),
        check_vma=False)
```

time: 4910 us -> 3970 us (0.81)
  waiting for transfers between devices: 2650 us -> 1840 us
  Pallas kernels: 1190 us -> 1830 us
  local copies, waits for them, and re-layouts: 542 us -> 105 us
  other arithmetic: 437 us -> 97.1 us
  starting transfers between devices: 17 us -> 66.3 us
    psum x8 -> x0, waiting for transfers between devices: 1590 us -> none  [the longest x4 1540 us: device_epoch(): g_rel = lax.psum(g_rel, 'ent')]
    ppermute x3, waiting for transfers between devices: 97.8 us -> 784 us  [device_epoch(): g_tail = lax.ppermute(g_tail, 'ent', back)]
    ppermute x0 -> x22, waiting for transfers between devices: none -> 669 us  [the longest x2 307 us: join(): peer = lax.ppermute(flipped, 'data', swap)]
    pallas_call x12 -> x44, Pallas kernels: 1190 us -> 1830 us  [the longest x8 887 us: bucket_grads(): pl.pallas_call(functools.partial(grad_kernel, int(last), neg_ids.shape[-1...]
    all_gather x2 -> x0, waiting for transfers between devices: 481 us -> none  [join_columns(): both = lax.all_gather(flipped, 'data', axis=1)]
    sub x6 -> x0, other arithmetic: 190 us -> none  [adagrad(): param = param.reshape(rows, 2, LANES) - grad3 * step[:, None, None]]
    ppermute x4 -> x8, waiting for transfers between devices: 177 us -> 0.02 us  [device_epoch(): q_peer = lax.ppermute(q_mine, 'data', swap)]
    sub x3 -> x0, local copies, waits for them, and re-layouts: 145 us -> none  [adagrad(): param = param.reshape(rows, 2, LANES) - grad3 * step[:, None, None]]
  transfers between devices with their start and end apart: 29 -> 53, of which waited for: 19 -> 30; matrix products, arithmetic and copies ran while one was open for 14% -> 4% of each run, Pallas kernels for 7% -> 32%
where the time goes in v2:
time: 3970 us; the launch traced here: 3950 us
  waiting for transfers between devices  1840 us (46%)
  Pallas kernels  1830 us (46%)
  local copies, waits for them, and re-layouts  105 us (3%)
  other arithmetic  97.1 us (2%)
  starting transfers between devices  66.3 us (2%)
    pallas_call x8, Pallas kernels, bucket_grads(): pl.pallas_call(functools.partial(grad_kernel, int(last), neg_ids.shape[-1...  887 us
    ppermute x3, waiting for transfers between devices, device_epoch(): g_tail = lax.ppermute(g_tail, 'ent', back)  784 us
    ppermute x2, waiting for transfers between devices, join(): peer = lax.ppermute(flipped, 'data', swap)  307 us
    pallas_call x8, Pallas kernels, query_rows(): pl.pallas_call(query_kernel, grid=(blocks,), in_specs=[SCALARS, smem_bloc...  255 us
    ppermute x8, waiting for transfers between devices, device_epoch(): p_peer = lax.ppermute(p_mine, 'data', swap)  248 us
    pallas_call x8, Pallas kernels, tail_rows(): pl.pallas_call(functools.partial(tail_kernel, negs), grid=(blocks,), in_s...  238 us
    ppermute x4, waiting for transfers between devices, device_epoch(): chip_other = lax.ppermute(chip_sum, 'ent', chip_swap)  211 us
    pallas_call x8, Pallas kernels, adagrad(): pl.pallas_call(functools.partial(step_kernel, rate, dim), grid=(blocks,),...  189 us
  transfers between devices with their start and end apart: 53, of which 30 were waited for; matrix products, arithmetic and copies ran while one was open for 4% of the time, Pallas kernels for 32%

profile of v2, /device:TPU:0, one launch (start us, length us, event | category | flops | bytes accessed | tf_op | source)
XLA Modules:
  0.0 3951.0 jit_solution(3050034208465578835)
XLA Ops:
  218.8 89.8 %collective-permute-done.4.pp_ref = f32[32,1,256]{2,1,0:T(1,128)S(1)} collective-permute-done((f32[32,1,256]{2,1,0:T(1,128)S(1)}, f32[32,1,256]{2,1,0:T(1,128)S(1)}, u32[]{:S(2)}, u32[]{:S(2)}) %collective-permute-start.4) | collective-permute-done | bytes 32800 | tf_op jit(solution)/shard_map/ppermute | solution.py:461
  311.0 120.3 %bucket_grads.8 = (f32[32768,128]{1,0:T(8,128)}, f32[32768,128]{1,0:T(8,128)}, f32[29648,128]{1,0:T(8,128)}, f32[1,128]{1,0:T(1,128)}) custom-call(s32[1]{0:T(128)} %bitcast.2.core_ref, s32[32,1,256]{2,1,0:T(1,128)} %bitcast.133, s32[32,1,256]{2,1,0:T(1,128)} %bitcast.117, s32[32,1,256]{2,1,0:T(1,128)} %bitcast.131, ...), custom_call_target="tpu_custom_call" | custom-call | flops 300000000 | bytes 200000000 | tf_op jit(solution)/shard_map/bucket_grads/pallas_call | solution.py:342
  432.1 101.3 %bucket_grads.9 = (f32[32768,128]{1,0:T(8,128)}, f32[32768,128]{1,0:T(8,128)}, f32[14824,128]{1,0:T(8,128)}, f32[14824,128]{1,0:T(8,128)}, f32[1,128]{1,0:T(1,128)}) custom-call(s32[1]{0:T(128)} %bitcast.2.core_ref, s32[32,1,256]{2,1,0:T(1,128)} %bitcast.109, s32[32,1,256]{2,1,0:T(1,128)} %bitcast.93, s32[32,1,256]{2,1,0:T(1,128)} %bitcast.107, ...), custom_call_target="tpu_custom_call" | custom-call | flops 300000000 | bytes 200000000 | tf_op jit(solution)/shard_map/bucket_grads/pallas_call | solution.py:342
  584.6 33.5 adagrad_step.8
  618.1 98.8 %collective-permute-done.8.two_ref = f32[14824,128]{1,0:T(8,128)} collective-permute-done((f32[14824,128]{1,0:T(8,128)}, f32[14824,128]{1,0:T(8,128)}, u32[]{:S(2)}, u32[]{:S(2)}) %collective-permute-start.8) | collective-permute-done | bytes 7589920 | tf_op jit(solution)/shard_map/ppermute | solution.py:471
  905.1 78.3 %collective-permute-done.16.pp_ref = f32[32,1,256]{2,1,0:T(1,128)S(1)} collective-permute-done((f32[32,1,256]{2,1,0:T(1,128)S(1)}, f32[32,1,256]{2,1,0:T(1,128)S(1)}, u32[]{:S(2)}, u32[]{:S(2)}) %collective-permute-start.16) | collective-permute-done | bytes 32800 | tf_op jit(solution)/shard_map/ppermute | solution.py:461
  984.3 120.3 %bucket_grads.10 = (f32[32768,128]{1,0:T(8,128)}, f32[32768,128]{1,0:T(8,128)}, f32[29648,128]{1,0:T(8,128)}, f32[1,128]{1,0:T(1,128)}) custom-call(s32[1]{0:T(128)} %bitcast.2.core_ref, s32[32,1,256]{2,1,0:T(1,128)} %bitcast.129, s32[32,1,256]{2,1,0:T(1,128)} %bitcast.115, s32[32,1,256]{2,1,0:T(1,128)} %bitcast.127, ...), custom_call_target="tpu_custom_call" | custom-call | flops 300000000 | bytes 200000000 | tf_op jit(solution)/shard_map/bucket_grads/pallas_call | solution.py:342
  1105.3 101.4 %bucket_grads.11 = (f32[32768,128]{1,0:T(8,128)}, f32[32768,128]{1,0:T(8,128)}, f32[14824,128]{1,0:T(8,128)}, f32[14824,128]{1,0:T(8,128)}, f32[1,128]{1,0:T(1,128)}) custom-call(s32[1]{0:T(128)} %bitcast.2.core_ref, s32[32,1,256]{2,1,0:T(1,128)} %bitcast.105, s32[32,1,256]{2,1,0:T(1,128)} %bitcast.91, s32[32,1,256]{2,1,0:T(1,128)} %bitcast.103, ...), custom_call_target="tpu_custom_call" | custom-call | flops 300000000 | bytes 200000000 | tf_op jit(solution)/shard_map/bucket_grads/pallas_call | solution.py:342
  1208.5 34.0 collective-permute-done.20
  1249.8 221.3 %collective-permute-done.18.two_ref = f32[32768,128]{1,0:T(8,128)} collective-permute-done((f32[32768,128]{1,0:T(8,128)}, f32[32768,128]{1,0:T(8,128)}, u32[]{:S(2)}, u32[]{:S(2)}) %collective-permute-start.18) | collective-permute-done | bytes 16777248 | tf_op jit(solution)/shard_map/ppermute | solution.py:469
  1502.9 33.4 adagrad_step.10
  1662.0 104.8 %collective-permute-done.24.tab_hbm = bf16[32768,128]{1,0:T(8,128)(2,1)} collective-permute-done((bf16[32768,128]{1,0:T(8,128)(2,1)}, bf16[32768,128]{1,0:T(8,128)(2,1)}, u32[]{:S(2)}, u32[]{:S(2)}) %collective-permute-start.24) | collective-permute-done | bytes 8388640 | tf_op jit(solution)/shard_map/ppermute | solution.py:450
  1834.7 120.5 %bucket_grads.12 = (f32[32768,128]{1,0:T(8,128)}, f32[32768,128]{1,0:T(8,128)}, f32[29648,128]{1,0:T(8,128)}, f32[1,128]{1,0:T(1,128)}) custom-call(s32[1]{0:T(128)} %bitcast.2.core_ref, s32[32,1,256]{2,1,0:T(1,128)} %bitcast.125, s32[32,1,256]{2,1,0:T(1,128)} %bitcast.113, s32[32,1,256]{2,1,0:T(1,128)} %bitcast.123, ...), custom_call_target="tpu_custom_call" | custom-call | flops 300000000 | bytes 200000000 | tf_op jit(solution)/shard_map/bucket_grads/pallas_call | solution.py:342
  1955.9 101.3 %bucket_grads.13 = (f32[32768,128]{1,0:T(8,128)}, f32[32768,128]{1,0:T(8,128)}, f32[14824,128]{1,0:T(8,128)}, f32[14824,128]{1,0:T(8,128)}, f32[1,128]{1,0:T(1,128)}) custom-call(s32[1]{0:T(128)} %bitcast.2.core_ref, s32[32,1,256]{2,1,0:T(1,128)} %bitcast.101, s32[32,1,256]{2,1,0:T(1,128)} %bitcast.89, s32[32,1,256]{2,1,0:T(1,128)} %bitcast.99, ...), custom_call_target="tpu_custom_call" | custom-call | flops 300000000 | bytes 200000000 | tf_op jit(solution)/shard_map/bucket_grads/pallas_call | solution.py:342
  2077.1 343.6 %collective-permute-done.31.two_ref = f32[32768,128]{1,0:T(8,128)} collective-permute-done((f32[32768,128]{1,0:T(8,128)}, f32[32768,128]{1,0:T(8,128)}, u32[]{:S(2)}, u32[]{:S(2)}) %collective-permute-start.31) | collective-permute-done | bytes 16777248 | tf_op jit(solution)/shard_map/ppermute | solution.py:469
  2452.6 33.5 adagrad_step.12
  2486.0 93.7 %collective-permute-done.34.two_ref = f32[14824,128]{1,0:T(8,128)} collective-permute-done((f32[14824,128]{1,0:T(8,128)}, f32[14824,128]{1,0:T(8,128)}, u32[]{:S(2)}, u32[]{:S(2)}) %collective-permute-start.34) | collective-permute-done | bytes 7589920 | tf_op jit(solution)/shard_map/ppermute | solution.py:471
  2769.4 76.7 %collective-permute-done.42.pp_ref = f32[32,1,256]{2,1,0:T(1,128)S(1)} collective-permute-done((f32[32,1,256]{2,1,0:T(1,128)S(1)}, f32[32,1,256]{2,1,0:T(1,128)S(1)}, u32[]{:S(2)}, u32[]{:S(2)}) %collective-permute-start.42) | collective-permute-done | bytes 32800 | tf_op jit(solution)/shard_map/ppermute | solution.py:461
  2848.5 120.2 %bucket_grads.14 = (f32[32768,128]{1,0:T(8,128)}, f32[32768,128]{1,0:T(8,128)}, f32[29648,128]{1,0:T(8,128)}, f32[1,128]{1,0:T(1,128)}) custom-call(s32[1]{0:T(128)} %bitcast.2.core_ref, s32[32,1,256]{2,1,0:T(1,128)} %bitcast.121, s32[32,1,256]{2,1,0:T(1,128)} %bitcast.111, s32[32,1,256]{2,1,0:T(1,128)} %bitcast.119, ...), custom_call_target="tpu_custom_call" | custom-call | flops 300000000 | bytes 200000000 | tf_op jit(solution)/shard_map/bucket_grads/pallas_call | solution.py:342
  2969.5 101.3 %bucket_grads.15 = (f32[32768,128]{1,0:T(8,128)}, f32[32768,128]{1,0:T(8,128)}, f32[14824,128]{1,0:T(8,128)}, f32[14824,128]{1,0:T(8,128)}, f32[1,128]{1,0:T(1,128)}) custom-call(s32[1]{0:T(128)} %bitcast.2.core_ref, s32[32,1,256]{2,1,0:T(1,128)} %bitcast.97, s32[32,1,256]{2,1,0:T(1,128)} %bitcast.87, s32[32,1,256]{2,1,0:T(1,128)} %bitcast.95, ...), custom_call_target="tpu_custom_call" | custom-call | flops 300000000 | bytes 200000000 | tf_op jit(solution)/shard_map/bucket_grads/pallas_call | solution.py:342
  3071.3 35.7 collective-permute-done.47
  3114.1 219.3 %collective-permute-done.44.two_ref = f32[32768,128]{1,0:T(8,128)} collective-permute-done((f32[32768,128]{1,0:T(8,128)}, f32[32768,128]{1,0:T(8,128)}, u32[]{:S(2)}, u32[]{:S(2)}) %collective-permute-start.44) | collective-permute-done | bytes 16777248 | tf_op jit(solution)/shard_map/ppermute | solution.py:469
  3516.2 85.0 %collective-permute-done.50 = f32[2,100,7412]{2,0,1:T(2,128)} collective-permute-done((f32[2,100,7412]{2,0,1:T(2,128)}, f32[2,100,7412]{2,0,1:T(2,128)}, u32[]{:S(2)}, u32[]{:S(2)}) %collective-permute-start.50) | collective-permute-done | bytes 5929632 | tf_op jit(solution)/shard_map/ppermute | solution.py:480
  3640.7 222.1 %collective-permute-done.46 = f32[2,100,16384]{2,0,1:T(2,128)} collective-permute-done((f32[2,100,16384]{2,0,1:T(2,128)}, f32[2,100,16384]{2,0,1:T(2,128)}, u32[]{:S(2)}, u32[]{:S(2)}) %collective-permute-start.46) | collective-permute-done | bytes 13107232 | tf_op jit(solution)/shard_map/ppermute | solution.py:480
  (230 shorter events, 1246.0 us)
Async XLA Ops:
  118.3 192.1 %collective-permute-start.3 = (bf16[8192,256]{1,0:T(8,128)(2,1)}, bf16[8192,256]{1,0:T(8,128)(2,1)}, u32[]{:S(2)}, u32[]{:S(2)}) collective-permute-start(bf16[8192,256]{1,0:T(8,128)(2,1)} %get-tuple-element.135.qm_ref), channel_id=1, source_target_pairs={{0,4},{4,0},{1,5},{5,1},{2,6},{6,2},{3,7},{7,3}} | collective-permute-start | bytes 12582920 | tf_op jit(solution)/shard_map/ppermute | solution.py:457
  153.6 277.9 %collective-permute-start = (bf16[8192,256]{1,0:T(8,128)(2,1)}, bf16[8192,256]{1,0:T(8,128)(2,1)}, u32[]{:S(2)}, u32[]{:S(2)}) collective-permute-start(bf16[8192,256]{1,0:T(8,128)(2,1)} %get-tuple-element.129.qm_ref), channel_id=1, source_target_pairs={{0,4},{4,0},{1,5},{5,1},{2,6},{6,2},{3,7},{7,3}} | collective-permute-start | bytes 12582920 | tf_op jit(solution)/shard_map/ppermute | solution.py:457
  185.0 125.4 %collective-permute-start.5 = (bf16[256,256]{1,0:T(8,128)(2,1)}, bf16[256,256]{1,0:T(8,128)(2,1)S(1)}, u32[]{:S(2)}, u32[]{:S(2)}) collective-permute-start(bf16[256,256]{1,0:T(8,128)(2,1)} %get-tuple-element.137.mm_ref), channel_id=1, source_target_pairs={{0,4},{4,0},{1,5},{5,1},{2,6},{6,2},{3,7},{7,3}} | collective-permute-start | bytes 393224 | tf_op jit(solution)/shard_map/ppermute | solution.py:460
  216.8 214.7 %collective-permute-start.2 = (bf16[256,256]{1,0:T(8,128)(2,1)}, bf16[256,256]{1,0:T(8,128)(2,1)S(1)}, u32[]{:S(2)}, u32[]{:S(2)}) collective-permute-start(bf16[256,256]{1,0:T(8,128)(2,1)} %get-tuple-element.131.mm_ref), channel_id=1, source_target_pairs={{0,4},{4,0},{1,5},{5,1},{2,6},{6,2},{3,7},{7,3}} | collective-permute-start | bytes 393224 | tf_op jit(solution)/shard_map/ppermute | solution.py:460
  551.2 165.7 %collective-permute-start.8 = (f32[14824,128]{1,0:T(8,128)}, f32[14824,128]{1,0:T(8,128)}, u32[]{:S(2)}, u32[]{:S(2)}) collective-permute-start(f32[14824,128]{1,0:T(8,128)} %add.20.one_ref), channel_id=1, source_target_pairs={{0,2},{1,3},{2,0},{3,1},{4,6},{5,7},{6,4},{7,5}} | collective-permute-start | bytes 22769672 | tf_op jit(solution)/shard_map/ppermute | solution.py:471
  794.3 189.3 %collective-permute-start.15 = (bf16[8192,256]{1,0:T(8,128)(2,1)}, bf16[8192,256]{1,0:T(8,128)(2,1)}, u32[]{:S(2)}, u32[]{:S(2)}) collective-permute-start(bf16[8192,256]{1,0:T(8,128)(2,1)} %get-tuple-element.162.qm_ref), channel_id=1, source_target_pairs={{0,4},{4,0},{1,5},{5,1},{2,6},{6,2},{3,7},{7,3}} | collective-permute-start | bytes 12582920 | tf_op jit(solution)/shard_map/ppermute | solution.py:457
  826.5 278.1 %collective-permute-start.12 = (bf16[8192,256]{1,0:T(8,128)(2,1)}, bf16[8192,256]{1,0:T(8,128)(2,1)}, u32[]{:S(2)}, u32[]{:S(2)}) collective-permute-start(bf16[8192,256]{1,0:T(8,128)(2,1)} %get-tuple-element.156.qm_ref), channel_id=1, source_target_pairs={{0,4},{4,0},{1,5},{5,1},{2,6},{6,2},{3,7},{7,3}} | collective-permute-start | bytes 12582920 | tf_op jit(solution)/shard_map/ppermute | solution.py:457
  903.1 201.5 %collective-permute-start.14 = (bf16[256,256]{1,0:T(8,128)(2,1)}, bf16[256,256]{1,0:T(8,128)(2,1)S(1)}, u32[]{:S(2)}, u32[]{:S(2)}) collective-permute-start(bf16[256,256]{1,0:T(8,128)(2,1)} %get-tuple-element.158.mm_ref), channel_id=1, source_target_pairs={{0,4},{4,0},{1,5},{5,1},{2,6},{6,2},{3,7},{7,3}} | collective-permute-start | bytes 393224 | tf_op jit(solution)/shard_map/ppermute | solution.py:460
  1206.7 264.4 %collective-permute-start.18 = (f32[32768,128]{1,0:T(8,128)}, f32[32768,128]{1,0:T(8,128)}, u32[]{:S(2)}, u32[]{:S(2)}) collective-permute-start(f32[32768,128]{1,0:T(8,128)} %get-tuple-element.169), channel_id=1, source_target_pairs={{0,1},{1,2},{2,3},{3,0},{4,5},{5,6},{6,7},{7,4}} | collective-permute-start | bytes 50331656 | tf_op jit(solution)/shard_map/ppermute | solution.py:469
  1248.1 288.3 %collective-permute-start.21 = (f32[14824,128]{1,0:T(8,128)}, f32[14824,128]{1,0:T(8,128)}, u32[]{:S(2)}, u32[]{:S(2)}) collective-permute-start(f32[14824,128]{1,0:T(8,128)} %add.21.one_ref), channel_id=1, source_target_pairs={{0,2},{1,3},{2,0},{3,1},{4,6},{5,7},{6,4},{7,5}} | collective-permute-start | bytes 22769672 | tf_op jit(solution)/shard_map/ppermute | solution.py:471
  1584.1 182.7 %collective-permute-start.24 = (bf16[32768,128]{1,0:T(8,128)(2,1)}, bf16[32768,128]{1,0:T(8,128)(2,1)}, u32[]{:S(2)}, u32[]{:S(2)}) collective-permute-start(bf16[32768,128]{1,0:T(8,128)(2,1)} %get-tuple-element.182), channel_id=1, source_target_pairs={{2,0},{3,1},{0,2},{1,3},{6,4},{7,5},{4,6},{5,7}} | collective-permute-start | bytes 25165832 | tf_op jit(solution)/shard_map/ppermute | solution.py:450
  1628.0 206.1 %collective-permute-start.28 = (bf16[8192,256]{1,0:T(8,128)(2,1)}, bf16[8192,256]{1,0:T(8,128)(2,1)}, u32[]{:S(2)}, u32[]{:S(2)}) collective-permute-start(bf16[8192,256]{1,0:T(8,128)(2,1)} %get-tuple-element.190.qm_ref), channel_id=1, source_target_pairs={{0,4},{4,0},{1,5},{5,1},{2,6},{6,2},{3,7},{7,3}} | collective-permute-start | bytes 12582920 | tf_op jit(solution)/shard_map/ppermute | solution.py:457
  1661.7 293.6 %collective-permute-start.25 = (bf16[8192,256]{1,0:T(8,128)(2,1)}, bf16[8192,256]{1,0:T(8,128)(2,1)}, u32[]{:S(2)}, u32[]{:S(2)}) collective-permute-start(bf16[8192,256]{1,0:T(8,128)(2,1)} %get-tuple-element.184.qm_ref), channel_id=1, source_target_pairs={{0,4},{4,0},{1,5},{5,1},{2,6},{6,2},{3,7},{7,3}} | collective-permute-start | bytes 12582920 | tf_op jit(solution)/shard_map/ppermute | solution.py:457
  1828.1 127.1 %collective-permute-start.27 = (bf16[256,256]{1,0:T(8,128)(2,1)}, bf16[256,256]{1,0:T(8,128)(2,1)S(1)}, u32[]{:S(2)}, u32[]{:S(2)}) collective-permute-start(bf16[256,256]{1,0:T(8,128)(2,1)} %get-tuple-element.186.mm_ref), channel_id=1, source_target_pairs={{0,4},{4,0},{1,5},{5,1},{2,6},{6,2},{3,7},{7,3}} | collective-permute-start | bytes 393224 | tf_op jit(solution)/shard_map/ppermute | solution.py:460
  2057.3 363.4 %collective-permute-start.31 = (f32[32768,128]{1,0:T(8,128)}, f32[32768,128]{1,0:T(8,128)}, u32[]{:S(2)}, u32[]{:S(2)}) collective-permute-start(f32[32768,128]{1,0:T(8,128)} %get-tuple-element.197), channel_id=1, source_target_pairs={{0,2},{1,3},{2,0},{3,1},{4,6},{5,7},{6,4},{7,5}} | collective-permute-start | bytes 50331656 | tf_op jit(solution)/shard_map/ppermute | solution.py:469
  2076.6 503.1 %collective-permute-start.34 = (f32[14824,128]{1,0:T(8,128)}, f32[14824,128]{1,0:T(8,128)}, u32[]{:S(2)}, u32[]{:S(2)}) collective-permute-start(f32[14824,128]{1,0:T(8,128)} %add.22.one_ref), channel_id=1, source_target_pairs={{0,2},{1,3},{2,0},{3,1},{4,6},{5,7},{6,4},{7,5}} | collective-permute-start | bytes 22769672 | tf_op jit(solution)/shard_map/ppermute | solution.py:471
  2657.1 190.8 %collective-permute-start.41 = (bf16[8192,256]{1,0:T(8,128)(2,1)}, bf16[8192,256]{1,0:T(8,128)(2,1)}, u32[]{:S(2)}, u32[]{:S(2)}) collective-permute-start(bf16[8192,256]{1,0:T(8,128)(2,1)} %get-tuple-element.218.qm_ref), channel_id=1, source_target_pairs={{0,4},{4,0},{1,5},{5,1},{2,6},{6,2},{3,7},{7,3}} | collective-permute-start | bytes 12582920 | tf_op jit(solution)/shard_map/ppermute | solution.py:457
  2690.8 278.1 %collective-permute-start.38 = (bf16[8192,256]{1,0:T(8,128)(2,1)}, bf16[8192,256]{1,0:T(8,128)(2,1)}, u32[]{:S(2)}, u32[]{:S(2)}) collective-permute-start(bf16[8192,256]{1,0:T(8,128)(2,1)} %get-tuple-element.212.qm_ref), channel_id=1, source_target_pairs={{0,4},{4,0},{1,5},{5,1},{2,6},{6,2},{3,7},{7,3}} | collective-permute-start | bytes 12582920 | tf_op jit(solution)/shard_map/ppermute | solution.py:457
  2767.4 201.4 %collective-permute-start.40 = (bf16[256,256]{1,0:T(8,128)(2,1)}, bf16[256,256]{1,0:T(8,128)(2,1)S(1)}, u32[]{:S(2)}, u32[]{:S(2)}) collective-permute-start(bf16[256,256]{1,0:T(8,128)(2,1)} %get-tuple-element.214.mm_ref), channel_id=1, source_target_pairs={{0,4},{4,0},{1,5},{5,1},{2,6},{6,2},{3,7},{7,3}} | collective-permute-start | bytes 393224 | tf_op jit(solution)/shard_map/ppermute | solution.py:460
  3070.8 262.6 %collective-permute-start.44 = (f32[32768,128]{1,0:T(8,128)}, f32[32768,128]{1,0:T(8,128)}, u32[]{:S(2)}, u32[]{:S(2)}) collective-permute-start(f32[32768,128]{1,0:T(8,128)} %get-tuple-element.225), channel_id=1, source_target_pairs={{0,3},{1,0},{2,1},{3,2},{4,7},{5,4},{6,5},{7,6}} | collective-permute-start | bytes 50331656 | tf_op jit(solution)/shard_map/ppermute | solution.py:469
  3112.6 304.0 %collective-permute-start.48 = (f32[14824,128]{1,0:T(8,128)}, f32[14824,128]{1,0:T(8,128)}, u32[]{:S(2)}, u32[]{:S(2)}) collective-permute-start(f32[14824,128]{1,0:T(8,128)} %add.23.one_ref), channel_id=1, source_target_pairs={{0,2},{1,3},{2,0},{3,1},{4,6},{5,7},{6,4},{7,5}} | collective-permute-start | bytes 22769672 | tf_op jit(solution)/shard_map/ppermute | solution.py:471
  3470.0 131.2 %collective-permute-start.50 = (f32[2,100,7412]{2,0,1:T(2,128)}, f32[2,100,7412]{2,0,1:T(2,128)}, u32[]{:S(2)}, u32[]{:S(2)}) collective-permute-start(f32[2,100,7412]{2,0,1:T(2,128)} %copy.128), channel_id=1, source_target_pairs={{0,4},{4,0},{1,5},{5,1},{2,6},{6,2},{3,7},{7,3}} | collective-permute-start | bytes 17788808 | tf_op jit(solution)/shard_map/ppermute | solution.py:480
  3514.7 348.1 %collective-permute-start.46 = (f32[2,100,16384]{2,0,1:T(2,128)}, f32[2,100,16384]{2,0,1:T(2,128)}, u32[]{:S(2)}, u32[]{:S(2)}) collective-permute-start(f32[2,100,16384]{2,0,1:T(2,128)} %copy.124), channel_id=1, source_target_pairs={{0,4},{4,0},{1,5},{5,1},{2,6},{6,2},{3,7},{7,3}} | collective-permute-start | bytes 39321608 | tf_op jit(solution)/shard_map/ppermute | solution.py:480
  3639.9 286.0 %collective-permute-start.51 = (f32[400,7412]{1,0:T(8,128)}, f32[400,7412]{1,0:T(8,128)}, u32[]{:S(2)}, u32[]{:S(2)}) collective-permute-start(f32[400,7412]{1,0:T(8,128)} %reshape.135), channel_id=1, source_target_pairs={{0,1},{1,0},{2,3},{3,2},{4,5},{5,4},{6,7},{7,6}} | collective-permute-start | bytes 35577608 | tf_op jit(solution)/shard_map/ppermute | solution.py:487
  (67 other events, 1702.0 us)
Sparse Core Ops, SparseCore 0:
  12.6 21.3 all-gather.3

commit v3 on v2

--- a/solution.py
+++ b/solution.py
@@ -69,9 +69,9 @@
 
 def flip_kernel(in_ref, out_ref):
     real, imag = halves(in_ref)
-    width = out_ref.shape[1]
-    out_ref[0] = real.T[:width, :]
-    out_ref[1] = imag.T[:width, :]
+    width = out_ref.shape[0] // 2
+    out_ref[pl.ds(0, width), :] = real.T[:width, :]
+    out_ref[pl.ds(width, width), :] = imag.T[:width, :]
 
 
 def flip_half(half, dim):
@@ -80,8 +80,8 @@
         flip_kernel,
         grid=(pl.cdiv(rows, WIDE_ROWS),),
         in_specs=[pl.BlockSpec((2 * WIDE_ROWS, LANES), lambda b: (b, 0))],
-        out_specs=pl.BlockSpec((2, dim // 4, WIDE_ROWS), lambda b: (0, 0, b)),
-        out_shape=jax.ShapeDtypeStruct((2, dim // 4, rows), jnp.float32),
+        out_specs=pl.BlockSpec((dim // 2, WIDE_ROWS), lambda b: (0, b)),
+        out_shape=jax.ShapeDtypeStruct((dim // 2, rows), jnp.float32),
         compiler_params=pltpu.CompilerParams(dimension_semantics=("arbitrary",)),
         cost_estimate=pl.CostEstimate(flops=20_000_000, bytes_accessed=30_000_000, transcendentals=0),
         name="flip_half",
@@ -171,13 +171,13 @@
 
 def grad_kernel(
     last, negs,
-    core_ref, head_ref, tail_ref, rel_ref, neg_ref, a_ref, r_ref, c_ref, qm_ref, qp_ref, pm_ref, pp_ref, w_ref, mm_ref, mp_ref,
+    core_ref, head_ref, rel_ref, a_ref, r_ref, c_ref, qm_ref, qp_ref, pm_ref, pp_ref, w_ref, mm_ref, mp_ref,
     *rest,
 ):
-    before, rest = rest[:3 * last], rest[3 * last:]
-    outs, (loss_ref, acc_h, acc_t, acc_r, blk_h, blk_t, blk_r, neg_acc, sems) = rest[:3 + last], rest[3 + last:]
+    before, rest = rest[:2 * last], rest[2 * last:]
+    outs, (t_ref, n_ref, loss_ref, acc_h, acc_r, blk_h, blk_r, neg_acc, sems) = rest[:2 + last], rest[2 + last:]
     block = pl.program_id(0)
-    accs = (acc_h, acc_t, acc_r)
+    accs = (acc_h, acc_r)
 
     @pl.when(block == 0)
     def _():
@@ -190,9 +190,10 @@
             for copy in copies:
                 copy.wait()
         else:
-            rows = 16
             for acc in accs:
-                def clear(step, carry, acc=acc):
+                rows = max(size for size in range(8, 513, 8) if acc.shape[0] % size == 0)
+
+                def clear(step, carry, acc=acc, rows=rows):
                     acc[pl.ds(pl.multiple_of(step * rows, rows), rows), :] = jnp.zeros((rows, LANES), jnp.float32)
                     return carry
 
@@ -227,7 +228,7 @@
     neg_acc[...] += lax.dot_general(beta, q_bf, tn, preferred_element_type=jnp.float32)
     d_re = alpha * c_re + mixed[:, :LANES]
     d_im = alpha * c_im + mixed[:, LANES:]
-    put_halves(blk_t, alpha * q_re, alpha * q_im)
+    put_halves(t_ref, alpha * q_re, alpha * q_im)
     put_halves(blk_h, d_re * r_re + d_im * r_im, d_im * r_re - d_re * r_im)
     put_halves(blk_r, d_re * a_re + d_im * a_im, d_im * a_re - d_re * a_im)
 
@@ -237,9 +238,8 @@
         for sub in range(unroll):
             edge = step * unroll + sub
             here = pair_at(2 * edge)
-            at_h, at_t, at_r = (pair_at(ref[0, 0, edge]) for ref in (head_ref, tail_ref, rel_ref))
+            at_h, at_r = (pair_at(ref[0, 0, edge]) for ref in (head_ref, rel_ref))
             acc_h[at_h, :] = acc_h[at_h, :] + blk_h[here, :]
-            acc_t[at_t, :] = acc_t[at_t, :] + blk_t[here, :]
             acc_r[at_r, :] = acc_r[at_r, :] + blk_r[here, :]
         return carry
 
@@ -247,22 +247,12 @@
 
     @pl.when(block == pl.num_programs(0) - 1)
     def _():
-        put_halves(blk_t, neg_acc[:, :LANES], neg_acc[:, LANES:])
-        small = 8
-
-        def more(step, carry):
-            for sub in range(small):
-                row = step * small + sub
-                at_t = pair_at(neg_ref[0, 0, row])
-                acc_t[at_t, :] = acc_t[at_t, :] + blk_t[pair_at(2 * row), :]
-            return carry
-
-        lax.fori_loop(0, negs // small, more, 0)
+        put_halves(n_ref, neg_acc[:, :LANES], neg_acc[:, LANES:])
         sources = list(accs)
         if last:
             half = acc_r.shape[0] // 2
             core = core_ref[0]
-            sources[2:] = [acc_r.at[pl.ds(pl.multiple_of(at * half, 8), half)] for at in (core, 1 - core)]
+            sources[1:] = [acc_r.at[pl.ds(pl.multiple_of(at * half, 8), half)] for at in (core, 1 - core)]
         copies = [pltpu.make_async_copy(src, out, sems.at[slot]) for slot, (src, out) in enumerate(zip(sources, outs))]
         for copy in copies:
             copy.start()
@@ -333,33 +323,101 @@
     )(tail_ids, neg_ids, a_rows, r_rows, table)
 
 
-def bucket_grads(core, ids, neg_ids, rows, queries, scores, weight, negatives, before, ent_shape, rel_shape):
+def bucket_grads(core, ids, negs, rows, queries, scores, weight, negatives, before, ent_shape, rel_shape):
     blocks = ids[0].shape[0]
     last = before is not None
     before = before or ()
     half_shape = (rel_shape[0] // 2, LANES)
-    shapes = [ent_shape, ent_shape] + ([half_shape, half_shape] if last else [rel_shape])
-    return pl.pallas_call(
-        functools.partial(grad_kernel, int(last), neg_ids.shape[-1]),
+    shapes = [ent_shape] + ([half_shape, half_shape] if last else [rel_shape])
+    neg_pairs = (4 * LANES, LANES)
+    flat = lambda b: (0, 0)
+    return pl.pallas_call(
+        functools.partial(grad_kernel, int(last), negs),
         grid=(blocks,),
-        in_specs=[SCALARS] + [smem_block(BLOCK)] * 3 + [SCALARS] + [PAIRS] * 3 + [WIDE] * 2 + [ROW] * 3 + [NEGS] * 2
+        in_specs=[SCALARS] + [smem_block(BLOCK)] * 2 + [PAIRS] * 3 + [WIDE] * 2 + [ROW] * 3 + [NEGS] * 2
         + [ANYWHERE] * len(before),
-        out_specs=[ANYWHERE] * len(shapes) + [pl.BlockSpec((1, LANES), lambda b: (0, 0))],
-        out_shape=[jax.ShapeDtypeStruct(shape, jnp.float32) for shape in shapes + [(1, LANES)]],
+        out_specs=[ANYWHERE] * len(shapes) + [PAIRS, pl.BlockSpec(neg_pairs, flat), pl.BlockSpec((1, LANES), flat)],
+        out_shape=[
+            jax.ShapeDtypeStruct(shape, jnp.float32)
+            for shape in shapes + [(2 * blocks * BLOCK, LANES), neg_pairs, (1, LANES)]
+        ],
         scratch_shapes=[
-            pltpu.VMEM(ent_shape, jnp.float32),
             pltpu.VMEM(ent_shape, jnp.float32),
             pltpu.VMEM(rel_shape, jnp.float32),
             pltpu.VMEM((2 * BLOCK, LANES), jnp.float32),
             pltpu.VMEM((2 * BLOCK, LANES), jnp.float32),
-            pltpu.VMEM((2 * BLOCK, LANES), jnp.float32),
             pltpu.VMEM((2 * LANES, 2 * LANES), jnp.float32),
-            pltpu.SemaphoreType.DMA((4,)),
+            pltpu.SemaphoreType.DMA((3,)),
         ],
         compiler_params=pltpu.CompilerParams(**PARAMS),
         cost_estimate=pl.CostEstimate(flops=300_000_000, bytes_accessed=200_000_000, transcendentals=2_000_000),
         name="bucket_grads",
-    )(core, *ids, neg_ids, *rows, *queries, *scores, weight, *negatives, *before)
+    )(core, *ids, *rows, *queries, *scores, weight, *negatives, *before)
+
+
+def add_kernel(negs, tail_ref, neg_ref, rows_ref, n_ref, base_hbm, g_hbm, *rest):
+    sum_refs, (acc, sem) = rest[:-2], rest[-2:]
+    block = pl.program_id(0)
+
+    @pl.when(block == 0)
+    def _():
+        copy = pltpu.make_async_copy(base_hbm, acc, sem)
+        copy.start()
+        copy.wait()
+        small = 8
+
+        def more(step, carry):
+            for sub in range(small):
+                row = step * small + sub
+                at = pair_at(neg_ref[0, 0, row])
+                acc[at, :] = acc[at, :] + n_ref[pair_at(2 * row), :]
+            return carry
+
+        lax.fori_loop(0, negs // small, more, 0)
+
+    unroll = 16
+
+    def some(step, carry):
+        for sub in range(unroll):
+            edge = step * unroll + sub
+            at = pair_at(tail_ref[0, 0, edge])
+            acc[at, :] = acc[at, :] + rows_ref[pair_at(2 * edge), :]
+        return carry
+
+    lax.fori_loop(0, BLOCK // unroll, some, 0)
+
+    @pl.when(block == pl.num_programs(0) - 1)
+    def _():
+        copy = pltpu.make_async_copy(acc, g_hbm, sem)
+        copy.start()
+        for sum_ref in sum_refs:
+            width = sum_ref.shape[-1]
+
+            def square(step, carry):
+                start = pl.multiple_of(step * 2 * width, 2 * width)
+                real = acc[pl.ds(start, width, stride=2), :]
+                imag = acc[pl.ds(start + 1, width, stride=2), :]
+                sum_ref[step] = jnp.sum((real * real + imag * imag).T, axis=0, keepdims=True)
+                return carry
+
+            lax.fori_loop(0, sum_ref.shape[0], square, 0)
+        copy.wait()
+
+
+def add_rows(base, tail_ids, neg_ids, rows, neg_rows, sum_shape):
+    blocks = tail_ids.shape[0]
+    sums = [] if sum_shape is None else [sum_shape]
+    return pl.pallas_call(
+        functools.partial(add_kernel, neg_ids.shape[-1]),
+        grid=(blocks,),
+        in_specs=[smem_block(BLOCK), SCALARS, PAIRS, pl.BlockSpec(neg_rows.shape, lambda b: (0, 0)), ANYWHERE],
+        out_specs=[ANYWHERE] + [pl.BlockSpec(shape, lambda b: (0, 0, 0)) for shape in sums],
+        out_shape=[jax.ShapeDtypeStruct(shape, jnp.float32) for shape in [base.shape] + sums],
+        scratch_shapes=[pltpu.VMEM(base.shape, jnp.float32), pltpu.SemaphoreType.DMA],
+        compiler_params=pltpu.CompilerParams(**PARAMS),
+        cost_estimate=pl.CostEstimate(flops=100_000_000, bytes_accessed=100_000_000, transcendentals=0),
+        name="add_rows",
+    )(tail_ids, neg_ids, rows, neg_rows, base)
 
 
 def square_kernel(one_ref, two_ref, *rest):
@@ -380,36 +438,64 @@
         ref[...] = out_ref[...].astype(jnp.bfloat16)
 
 
-def adagrad(param, state, one, two, rate, dim, swap, with_bf, after=()):
-    blocks = state.shape[0]
-    pairs = pl.BlockSpec((2 * WIDE_ROWS, LANES), lambda b: (b, 0))
-    row = pl.BlockSpec((1, 1, WIDE_ROWS), lambda b: (b, 0, 0))
-    wide = jax.ShapeDtypeStruct(param.shape, jnp.float32)
-    narrow = jax.ShapeDtypeStruct(state.shape, jnp.float32)
-    params = pltpu.CompilerParams(dimension_semantics=("arbitrary",))
-    size = 4 * param.size
-    grad, sums = pl.pallas_call(
+PAIR_ROWS = pl.BlockSpec((2 * WIDE_ROWS, LANES), lambda b: (b, 0))
+WIDE_ROW = pl.BlockSpec((1, 1, WIDE_ROWS), lambda b: (b, 0, 0))
+
+
+def square_sums(one, two, blocks, after):
+    return pl.pallas_call(
         square_kernel,
         grid=(blocks,),
-        in_specs=[pairs, pairs] + [ANYWHERE] * len(after),
-        out_specs=[pairs, row],
-        out_shape=[wide, narrow],
-        compiler_params=params,
-        cost_estimate=pl.CostEstimate(flops=4 * param.size, bytes_accessed=3 * size, transcendentals=0),
+        in_specs=[PAIR_ROWS, PAIR_ROWS] + [ANYWHERE] * len(after),
+        out_specs=[PAIR_ROWS, WIDE_ROW],
+        out_shape=[
+            jax.ShapeDtypeStruct(one.shape, jnp.float32),
+            jax.ShapeDtypeStruct((blocks, 1, WIDE_ROWS), jnp.float32),
+        ],
+        compiler_params=pltpu.CompilerParams(dimension_semantics=("arbitrary",)),
+        cost_estimate=pl.CostEstimate(flops=4 * one.size, bytes_accessed=12 * one.size, transcendentals=0),
         name="square_sums",
     )(one, two, *after)
+
+
+def adagrad_step(param, state, grad, sums, rate, dim, swap, with_bf):
     sums_peer = lax.ppermute(sums, "data", swap)
-    bf_shapes = [jax.ShapeDtypeStruct(param.shape, jnp.bfloat16)] if with_bf else []
+    kinds = [jnp.float32, jnp.bfloat16] if with_bf else [jnp.float32]
+    wide = [jax.ShapeDtypeStruct(param.shape, kind) for kind in kinds]
     return pl.pallas_call(
         functools.partial(step_kernel, rate, dim),
-        grid=(blocks,),
-        in_specs=[pairs, pairs, row, row, row],
-        out_specs=[pairs, row] + [pairs] * len(bf_shapes),
-        out_shape=[wide, narrow] + bf_shapes,
-        compiler_params=params,
-        cost_estimate=pl.CostEstimate(flops=4 * param.size, bytes_accessed=3 * size, transcendentals=0),
+        grid=(state.shape[0],),
+        in_specs=[PAIR_ROWS, PAIR_ROWS, WIDE_ROW, WIDE_ROW, WIDE_ROW],
+        out_specs=[PAIR_ROWS, WIDE_ROW] + [PAIR_ROWS] * (len(kinds) - 1),
+        out_shape=[wide[0], jax.ShapeDtypeStruct(state.shape, jnp.float32)] + wide[1:],
+        compiler_params=pltpu.CompilerParams(dimension_semantics=("arbitrary",)),
+        cost_estimate=pl.CostEstimate(flops=4 * param.size, bytes_accessed=12 * param.size, transcendentals=0),
         name="adagrad_step",
     )(param, grad, state, sums, sums_peer)
+
+
+def join_kernel(part_ref, mine_ref, peer_ref, out_ref):
+    second = part_ref[0] != 0
+    width = mine_ref.shape[0] // 2
+    for side in range(2):
+        mine, peer = (ref[pl.ds(side * width, width), :] for ref in (mine_ref, peer_ref))
+        out_ref[pl.ds(2 * side * width, width), :] = jnp.where(second, peer, mine)
+        out_ref[pl.ds((2 * side + 1) * width, width), :] = jnp.where(second, mine, peer)
+
+
+def join_columns(part, mine, peer):
+    width, rows = mine.shape
+    half = pl.BlockSpec((width, WIDE_ROWS), lambda b: (0, b))
+    return pl.pallas_call(
+        join_kernel,
+        grid=(pl.cdiv(rows, WIDE_ROWS),),
+        in_specs=[SCALARS, half, half],
+        out_specs=pl.BlockSpec((2 * width, WIDE_ROWS), lambda b: (0, b)),
+        out_shape=jax.ShapeDtypeStruct((2 * width, rows), jnp.float32),
+        compiler_params=pltpu.CompilerParams(dimension_semantics=("arbitrary",)),
+        cost_estimate=pl.CostEstimate(flops=mine.size, bytes_accessed=16 * mine.size, transcendentals=0),
+        name="join_columns",
+    )(part[None], mine, peer)
 
 
 def solution(mesh):
@@ -443,6 +529,16 @@
         def field(slot, bucket, round_idx):
             return both[bucket, round_idx, slot * edge_count:(slot + 1) * edge_count].reshape(blocks, 1, BLOCK)
 
+        def owned(round_idx):
+            mine = jnp.concatenate(
+                [both[:, round_idx, edge_count:2 * edge_count], both[:, round_idx, 4 * edge_count:]], axis=1)
+            if round_idx:
+                mine = lax.ppermute(mine, "ent", [(src, (src + round_idx) % ent_size) for src in range(ent_size)])
+            return [
+                (mine[bucket, :edge_count].reshape(blocks, 1, BLOCK), mine[bucket, edge_count:].reshape(1, 1, negs))
+                for bucket in range(data_size)
+            ]
+
         losses = []
         for round_idx in range(ent_size):
             if round_idx:
@@ -450,8 +546,10 @@
                 table = lax.ppermute(table, "ent", fetch)
             ids = [[field(slot, bucket, round_idx) for slot in range(3)] for bucket in range(data_size)]
             asked = [query_rows(core_at, ent, rel_mine, rel_other, ids[bucket][0], ids[bucket][2]) for bucket in range(data_size)]
+            back = [(src, (src + round_idx) % ent_size) for src in range(ent_size)]
+            targets = owned(round_idx)
             before = None
-            sums = []
+            sums, returned = [], []
             for bucket in range(data_size):
                 a_rows, r_rows, q_mine = asked[bucket]
                 q_peer = lax.ppermute(q_mine, "data", swap)
@@ -459,34 +557,44 @@
                 c_rows, p_mine, m_mine = tail_rows(table, ids[bucket][1], neg_ids, a_rows, r_rows)
                 m_peer = lax.ppermute(m_mine, "data", swap)
                 p_peer = lax.ppermute(p_mine, "data", swap)
-                *before, loss = bucket_grads(
-                    core_at, ids[bucket], neg_ids, (a_rows, r_rows, c_rows), (q_mine, q_peer), (p_mine, p_peer),
-                    field(3, bucket, round_idx).astype(jnp.float32), (m_mine, m_peer), before, ent_shape, rel_shape)
+                *before, t_rows, n_rows, loss = bucket_grads(
+                    core_at, (ids[bucket][0], ids[bucket][2]), negs, (a_rows, r_rows, c_rows), (q_mine, q_peer),
+                    (p_mine, p_peer), field(3, bucket, round_idx).astype(jnp.float32), (m_mine, m_peer), before,
+                    ent_shape, rel_shape)
                 sums.append(loss[0, 0])
-            g_head, g_tail, keep, give = before
-            if round_idx:
-                back = [(src, (src + round_idx) % ent_size) for src in range(ent_size)]
-                g_tail = lax.ppermute(g_tail, "ent", back)
+                if round_idx:
+                    t_rows = lax.ppermute(t_rows, "ent", back)
+                    n_rows = lax.ppermute(n_rows, "ent", back)
+                returned.append((t_rows, n_rows))
+            g_ent, keep, give = before
             chip_sum = keep + lax.ppermute(give, "ent", core_swap)
             chip_other = lax.ppermute(chip_sum, "ent", chip_swap)
-            ent, state, table = adagrad(ent, state, g_head, g_tail, LEARN_ENT, dim, swap, True)
-            rel_mine, rel_state = adagrad(rel_mine, rel_state, chip_sum, chip_other, LEARN_REL, dim, swap, False, (state,))
+            for bucket in range(data_size):
+                shape = state.shape if bucket == data_size - 1 else None
+                g_ent, *ent_sums = add_rows(g_ent, *targets[bucket], *returned[bucket], shape)
+            ent, state, table = adagrad_step(ent, state, g_ent, ent_sums[0], LEARN_ENT, dim, swap, True)
+            after = state
+            if round_idx == ent_size - 1:
+                ent_cols = after = flip_half(ent, dim)
+                ent_cols_peer = lax.ppermute(ent_cols, "data", swap)
+            g_rel, rel_sums = square_sums(chip_sum, chip_other, rel_state.shape[0], (after,))
+            rel_mine, rel_state = adagrad_step(rel_mine, rel_state, g_rel, rel_sums, LEARN_REL, dim, swap, False)
             if round_idx < ent_size - 1:
                 rel_other = lax.ppermute(rel_mine, "ent", core_swap)
             losses.append(jnp.where(part == 0, sums[0], sums[1]) / edge_count)
 
-        def join(half):
-            flipped = flip_half(half, dim)
-            peer = lax.ppermute(flipped, "data", swap)
-            first = jnp.where(part == 0, flipped, peer)
-            second = jnp.where(part == 0, peer, flipped)
-            return jnp.stack([first, second], axis=1).reshape(dim, -1)
-
-        ent_out = join(ent).T
-        rel_cols = join(rel_mine)
-        rel_cols_other = lax.ppermute(rel_cols, "ent", core_swap)
+        ent_out = join_columns(part, ent_cols, ent_cols_peer).T
+        rel_cols = flip_half(rel_mine, dim)
+        quarter = rel_cols.shape[-1] // 2
+        chip = lax.axis_index("ent") // 2
+        piece = lax.ppermute(lax.dynamic_slice_in_dim(rel_cols, chip * quarter, quarter, axis=1), "data", swap)
+        piece_other = lax.ppermute(piece, "ent", chip_swap)
+        rel_peer = jnp.concatenate(
+            [jnp.where(chip == 0, piece, piece_other), jnp.where(chip == 0, piece_other, piece)], axis=1)
+        rel_all = join_columns(part, rel_cols, rel_peer)
+        rel_other = lax.ppermute(rel_all, "ent", core_swap)
         rel_out = jnp.concatenate(
-            [jnp.where(core == 0, rel_cols, rel_cols_other), jnp.where(core == 0, rel_cols_other, rel_cols)], axis=1).T
+            [jnp.where(core == 0, rel_all, rel_other), jnp.where(core == 0, rel_other, rel_all)], axis=1).T
         return ent_out, state.reshape(-1), rel_out, jnp.stack(losses)[None, None, :]
 
     ent_spec = P(("sweep", "ent"), None)

time: 3970 us -> 4090 us (1.030)
  waiting for transfers between devices: 1840 us -> 2010 us
  local copies, waits for them, and re-layouts: 105 us -> 38 us
  Pallas kernels: 1830 us -> 1880 us
  other arithmetic: 97.1 us -> 54.1 us
    ppermute x14 -> x27, waiting for transfers between devices: 1120 us -> 1510 us  [the longest x3 1150 us: owned(): lax.ppermute(mine, 'ent', [(src, (src + round_idx) % ent_size) for src in...]
    ppermute x4, waiting for transfers between devices: 211 us -> 46.7 us  [device_epoch(): chip_other = lax.ppermute(chip_sum, 'ent', chip_swap)]
    pallas_call x24 -> x30, Pallas kernels: 1240 us -> 1290 us  [the longest x8 684 us: bucket_grads(): pl.pallas_call(functools.partial(grad_kernel, int(last), negs), grid=(blo...]
    ppermute x4, waiting for transfers between devices: 94.2 us -> 43.3 us  [device_epoch(): chip_sum = keep + lax.ppermute(give, 'ent', core_swap)]
    another operation x4 -> x0, other arithmetic: 48.6 us -> none  [join(): return jnp.stack([first, second], axis=1).reshape(dim, -1)]
  transfers between devices with their start and end apart: 53 -> 66, of which waited for: 30 -> 31; matrix products, arithmetic and copies ran while one was open for 4% -> 1% of each run, Pallas kernels for 32% -> 34%
where the time goes in v3:
time: 4090 us; the launch traced here: 4070 us
  waiting for transfers between devices  2010 us (49%)
  Pallas kernels  1880 us (46%)
  starting transfers between devices  60.8 us (1%)
  other arithmetic  54.1 us (1%)
    ppermute x3, waiting for transfers between devices, owned(): lax.ppermute(mine, 'ent', [(src, (src + round_idx) % ent_size) for src in...  1150 us
    pallas_call x8, Pallas kernels, bucket_grads(): pl.pallas_call(functools.partial(grad_kernel, int(last), negs), grid=(blo...  684 us
    pallas_call x8, Pallas kernels, add_rows(): pl.pallas_call(functools.partial(add_kernel, neg_ids.shape[-1]), grid=(bl...  316 us
    pallas_call x8, Pallas kernels, query_rows(): pl.pallas_call(query_kernel, grid=(blocks,), in_specs=[SCALARS, smem_bloc...  255 us
    ppermute x8, waiting for transfers between devices, device_epoch(): p_peer = lax.ppermute(p_mine, 'data', swap)  249 us
    pallas_call x8, Pallas kernels, tail_rows(): pl.pallas_call(functools.partial(tail_kernel, negs), grid=(blocks,), in_s...  238 us
    ppermute x1, waiting for transfers between devices, device_epoch(): ent_cols_peer = lax.ppermute(ent_cols, 'data', swap)  198 us
    pallas_call x8, Pallas kernels, adagrad_step(): pl.pallas_call(functools.partial(step_kernel, rate, dim), grid=(state.sha...  189 us
  transfers between devices with their start and end apart: 66, of which 31 were waited for; matrix products, arithmetic and copies ran while one was open for 1% of the time, Pallas kernels for 34%

profile of v3, /device:TPU:0, one launch (start us, length us, event | category | flops | bytes accessed | tf_op | source)
XLA Modules:
  0.0 4065.4 jit_solution(4626935622674210842)
XLA Ops:
  218.6 89.8 %collective-permute-done.4.pp_ref = f32[32,1,256]{2,1,0:T(1,128)S(1)} collective-permute-done((f32[32,1,256]{2,1,0:T(1,128)S(1)}, f32[32,1,256]{2,1,0:T(1,128)S(1)}, u32[]{:S(2)}, u32[]{:S(2)}) %collective-permute-start.4) | collective-permute-done | bytes 32800 | tf_op jit(solution)/shard_map/ppermute | solution.py:559
  310.9 81.4 %bucket_grads.8 = (f32[32768,128]{1,0:T(8,128)}, f32[29648,128]{1,0:T(8,128)}, f32[16384,128]{1,0:T(8,128)}, f32[512,128]{1,0:T(8,128)}, f32[1,128]{1,0:T(1,128)}) custom-call(s32[1]{0:T(128)} %bitcast.9.core_ref, s32[32,1,256]{2,1,0:T(1,128)} %bitcast.149, s32[32,1,256]{2,1,0:T(1,128)} %bitcast.147, f32[16384,128]{1,0:T(8,128)} %get-tuple-element.140.a_ref, ...), custom_call_target="tpu_custom_call" | custom-call | flops 300000000 | bytes 200000000 | tf_op jit(solution)/shard_map/bucket_grads/pallas_call | solution.py:334
  393.0 89.5 %bucket_grads.9 = (f32[32768,128]{1,0:T(8,128)}, f32[14824,128]{1,0:T(8,128)}, f32[14824,128]{1,0:T(8,128)}, f32[16384,128]{1,0:T(8,128)}, f32[512,128]{1,0:T(8,128)}, /*index=5*/f32[1,128]{1,0:T(1,128)}) custom-call(s32[1]{0:T(128)} %bitcast.9.core_ref, s32[32,1,256]{2,1,0:T(1,128)} %bitcast.133, s32[32,1,256]{2,1,0:T(1,128)} %bitcast.131, ...), custom_call_target="tpu_custom_call" | custom-call | flops 300000000 | bytes 200000000 | tf_op jit(solution)/shard_map/bucket_grads/pallas_call | solution.py:334
  501.8 39.3 add_rows.8.base_hbm
  541.0 39.7 add_rows.9
  619.3 46.7 %collective-permute-done.9.two_ref = f32[14824,128]{1,0:T(8,128)} collective-permute-done((f32[14824,128]{1,0:T(8,128)}, f32[14824,128]{1,0:T(8,128)}, u32[]{:S(2)}, u32[]{:S(2)}) %collective-permute-start.9) | collective-permute-done | bytes 7589920 | tf_op jit(solution)/shard_map/ppermute | solution.py:571
  854.3 78.3 %collective-permute-done.17.pp_ref = f32[32,1,256]{2,1,0:T(1,128)S(1)} collective-permute-done((f32[32,1,256]{2,1,0:T(1,128)S(1)}, f32[32,1,256]{2,1,0:T(1,128)S(1)}, u32[]{:S(2)}, u32[]{:S(2)}) %collective-permute-start.17) | collective-permute-done | bytes 32800 | tf_op jit(solution)/shard_map/ppermute | solution.py:559
  933.6 81.4 %bucket_grads.10 = (f32[32768,128]{1,0:T(8,128)}, f32[29648,128]{1,0:T(8,128)}, f32[16384,128]{1,0:T(8,128)}, f32[512,128]{1,0:T(8,128)}, f32[1,128]{1,0:T(1,128)}) custom-call(s32[1]{0:T(128)} %bitcast.9.core_ref, s32[32,1,256]{2,1,0:T(1,128)} %bitcast.145, s32[32,1,256]{2,1,0:T(1,128)} %bitcast.143, f32[16384,128]{1,0:T(8,128)} %get-tuple-element.169.a_ref, ...), custom_call_target="tpu_custom_call" | custom-call | flops 300000000 | bytes 200000000 | tf_op jit(solution)/shard_map/bucket_grads/pallas_call | solution.py:334
  1015.8 89.6 %bucket_grads.11 = (f32[32768,128]{1,0:T(8,128)}, f32[14824,128]{1,0:T(8,128)}, f32[14824,128]{1,0:T(8,128)}, f32[16384,128]{1,0:T(8,128)}, f32[512,128]{1,0:T(8,128)}, /*index=5*/f32[1,128]{1,0:T(1,128)}) custom-call(s32[1]{0:T(128)} %bitcast.9.core_ref, s32[32,1,256]{2,1,0:T(1,128)} %bitcast.127, s32[32,1,256]{2,1,0:T(1,128)} %bitcast.125, ...), custom_call_target="tpu_custom_call" | custom-call | flops 300000000 | bytes 200000000 | tf_op jit(solution)/shard_map/bucket_grads/pallas_call | solution.py:334
  1128.8 323.0 %collective-permute-done.7 = s32[2,8392]{1,0:T(2,128)S(1)} collective-permute-done((s32[2,8392]{1,0:T(2,128)S(1)}, s32[2,8392]{1,0:T(2,128)S(1)}, u32[]{:S(2)}, u32[]{:S(2)}) %collective-permute-start.7) | collective-permute-done | bytes 67168 | tf_op jit(solution)/shard_map/ppermute | solution.py:536
  1495.4 39.7 add_rows.11
  1684.9 104.7 %collective-permute-done.29.tab_hbm = bf16[32768,128]{1,0:T(8,128)(2,1)} collective-permute-done((bf16[32768,128]{1,0:T(8,128)(2,1)}, bf16[32768,128]{1,0:T(8,128)(2,1)}, u32[]{:S(2)}, u32[]{:S(2)}) %collective-permute-start.29) | collective-permute-done | bytes 8388640 | tf_op jit(solution)/shard_map/ppermute | solution.py:546
  1857.6 81.5 %bucket_grads.12 = (f32[32768,128]{1,0:T(8,128)}, f32[29648,128]{1,0:T(8,128)}, f32[16384,128]{1,0:T(8,128)}, f32[512,128]{1,0:T(8,128)}, f32[1,128]{1,0:T(1,128)}) custom-call(s32[1]{0:T(128)} %bitcast.9.core_ref, s32[32,1,256]{2,1,0:T(1,128)} %bitcast.141, s32[32,1,256]{2,1,0:T(1,128)} %bitcast.139, f32[16384,128]{1,0:T(8,128)} %get-tuple-element.199.a_ref, ...), custom_call_target="tpu_custom_call" | custom-call | flops 300000000 | bytes 200000000 | tf_op jit(solution)/shard_map/bucket_grads/pallas_call | solution.py:334
  1939.9 89.5 %bucket_grads.13 = (f32[32768,128]{1,0:T(8,128)}, f32[14824,128]{1,0:T(8,128)}, f32[14824,128]{1,0:T(8,128)}, f32[16384,128]{1,0:T(8,128)}, f32[512,128]{1,0:T(8,128)}, /*index=5*/f32[1,128]{1,0:T(1,128)}) custom-call(s32[1]{0:T(128)} %bitcast.9.core_ref, s32[32,1,256]{2,1,0:T(1,128)} %bitcast.123, s32[32,1,256]{2,1,0:T(1,128)} %bitcast.121, ...), custom_call_target="tpu_custom_call" | custom-call | flops 300000000 | bytes 200000000 | tf_op jit(solution)/shard_map/bucket_grads/pallas_call | solution.py:334
  2051.0 505.9 %collective-permute-done.24 = s32[2,8392]{1,0:T(2,128)S(1)} collective-permute-done((s32[2,8392]{1,0:T(2,128)S(1)}, s32[2,8392]{1,0:T(2,128)S(1)}, u32[]{:S(2)}, u32[]{:S(2)}) %collective-permute-start.24) | collective-permute-done | bytes 67168 | tf_op jit(solution)/shard_map/ppermute | solution.py:536
  2603.2 39.7 add_rows.13
  2870.7 76.8 %collective-permute-done.51.pp_ref = f32[32,1,256]{2,1,0:T(1,128)S(1)} collective-permute-done((f32[32,1,256]{2,1,0:T(1,128)S(1)}, f32[32,1,256]{2,1,0:T(1,128)S(1)}, u32[]{:S(2)}, u32[]{:S(2)}) %collective-permute-start.51) | collective-permute-done | bytes 32800 | tf_op jit(solution)/shard_map/ppermute | solution.py:559
  2949.8 81.4 %bucket_grads.14 = (f32[32768,128]{1,0:T(8,128)}, f32[29648,128]{1,0:T(8,128)}, f32[16384,128]{1,0:T(8,128)}, f32[512,128]{1,0:T(8,128)}, f32[1,128]{1,0:T(1,128)}) custom-call(s32[1]{0:T(128)} %bitcast.9.core_ref, s32[32,1,256]{2,1,0:T(1,128)} %bitcast.137, s32[32,1,256]{2,1,0:T(1,128)} %bitcast.135, f32[16384,128]{1,0:T(8,128)} %get-tuple-element.229.a_ref, ...), custom_call_target="tpu_custom_call" | custom-call | flops 300000000 | bytes 200000000 | tf_op jit(solution)/shard_map/bucket_grads/pallas_call | solution.py:334
  3031.9 89.6 %bucket_grads.15 = (f32[32768,128]{1,0:T(8,128)}, f32[14824,128]{1,0:T(8,128)}, f32[14824,128]{1,0:T(8,128)}, f32[16384,128]{1,0:T(8,128)}, f32[512,128]{1,0:T(8,128)}, /*index=5*/f32[1,128]{1,0:T(1,128)}) custom-call(s32[1]{0:T(128)} %bitcast.9.core_ref, s32[32,1,256]{2,1,0:T(1,128)} %bitcast.119, s32[32,1,256]{2,1,0:T(1,128)} %bitcast.117, ...), custom_call_target="tpu_custom_call" | custom-call | flops 300000000 | bytes 200000000 | tf_op jit(solution)/shard_map/bucket_grads/pallas_call | solution.py:334
  3141.5 326.0 %collective-permute-done.41 = s32[2,8392]{1,0:T(2,128)S(1)} collective-permute-done((s32[2,8392]{1,0:T(2,128)S(1)}, s32[2,8392]{1,0:T(2,128)S(1)}, u32[]{:S(2)}, u32[]{:S(2)}) %collective-permute-start.41) | collective-permute-done | bytes 67168 | tf_op jit(solution)/shard_map/ppermute | solution.py:536
  3511.4 39.7 add_rows.15
  3662.6 64.4 %collective-permute-done.62 = f32[200,3706]{1,0:T(8,128)S(1)} collective-permute-done((f32[200,3706]{1,0:T(8,128)S(1)}, f32[200,3706]{1,0:T(8,128)S(1)}, u32[]{:S(2)}, u32[]{:S(2)}) %collective-permute-start.62) | collective-permute-done | bytes 2964832 | tf_op jit(solution)/shard_map/ppermute | solution.py:590
  3728.5 62.5 %collective-permute-done.63 = f32[200,3706]{1,0:T(8,128)} collective-permute-done((f32[200,3706]{1,0:T(8,128)S(1)}, f32[200,3706]{1,0:T(8,128)}, u32[]{:S(2)}, u32[]{:S(2)}) %collective-permute-start.63) | collective-permute-done | bytes 2964832 | tf_op jit(solution)/shard_map/ppermute | solution.py:591
  3812.3 197.7 %collective-permute-done.58.peer_ref = f32[200,16384]{1,0:T(8,128)} collective-permute-done((f32[200,16384]{1,0:T(8,128)}, f32[200,16384]{1,0:T(8,128)}, u32[]{:S(2)}, u32[]{:S(2)}) %collective-permute-start.58) | collective-permute-done | bytes 13107232 | tf_op jit(solution)/shard_map/ppermute | solution.py:579
  (300 shorter events, 1292.4 us)
Async XLA Ops:
  118.1 192.1 %collective-permute-start.3 = (bf16[8192,256]{1,0:T(8,128)(2,1)}, bf16[8192,256]{1,0:T(8,128)(2,1)}, u32[]{:S(2)}, u32[]{:S(2)}) collective-permute-start(bf16[8192,256]{1,0:T(8,128)(2,1)} %get-tuple-element.143.qm_ref), channel_id=1, source_target_pairs={{0,4},{4,0},{1,5},{5,1},{2,6},{6,2},{3,7},{7,3}} | collective-permute-start | bytes 12582920 | tf_op jit(solution)/shard_map/ppermute | solution.py:555
  153.4 238.9 %collective-permute-start = (bf16[8192,256]{1,0:T(8,128)(2,1)}, bf16[8192,256]{1,0:T(8,128)(2,1)}, u32[]{:S(2)}, u32[]{:S(2)}) collective-permute-start(bf16[8192,256]{1,0:T(8,128)(2,1)} %get-tuple-element.137.qm_ref), channel_id=1, source_target_pairs={{0,4},{4,0},{1,5},{5,1},{2,6},{6,2},{3,7},{7,3}} | collective-permute-start | bytes 12582920 | tf_op jit(solution)/shard_map/ppermute | solution.py:555
  775.9 239.2 %collective-permute-start.13 = (bf16[8192,256]{1,0:T(8,128)(2,1)}, bf16[8192,256]{1,0:T(8,128)(2,1)}, u32[]{:S(2)}, u32[]{:S(2)}) collective-permute-start(bf16[8192,256]{1,0:T(8,128)(2,1)} %get-tuple-element.166.qm_ref), channel_id=1, source_target_pairs={{0,4},{4,0},{1,5},{5,1},{2,6},{6,2},{3,7},{7,3}} | collective-permute-start | bytes 12582920 | tf_op jit(solution)/shard_map/ppermute | solution.py:555
  1105.4 349.2 %collective-permute-start.21 = (f32[16384,128]{1,0:T(8,128)}, f32[16384,128]{1,0:T(8,128)}, u32[]{:S(2)}, u32[]{:S(2)}) collective-permute-start(f32[16384,128]{1,0:T(8,128)} %get-tuple-element.179), channel_id=1, source_target_pairs={{0,1},{1,2},{2,3},{3,0},{4,5},{5,6},{6,7},{7,4}} | collective-permute-start | bytes 25165832 | tf_op jit(solution)/shard_map/ppermute | solution.py:566
  1105.9 388.7 %collective-permute-start.19 = (f32[16384,128]{1,0:T(8,128)}, f32[16384,128]{1,0:T(8,128)}, u32[]{:S(2)}, u32[]{:S(2)}) collective-permute-start(f32[16384,128]{1,0:T(8,128)} %get-tuple-element.177), channel_id=1, source_target_pairs={{0,1},{1,2},{2,3},{3,0},{4,5},{5,6},{6,7},{7,4}} | collective-permute-start | bytes 25165832 | tf_op jit(solution)/shard_map/ppermute | solution.py:566
  1123.1 450.3 %collective-permute-start.26 = (f32[14824,128]{1,0:T(8,128)}, f32[14824,128]{1,0:T(8,128)}, u32[]{:S(2)}, u32[]{:S(2)}) collective-permute-start(f32[14824,128]{1,0:T(8,128)} %add.25.one_ref), channel_id=1, source_target_pairs={{0,2},{1,3},{2,0},{3,1},{4,6},{5,7},{6,4},{7,5}} | collective-permute-start | bytes 22769672 | tf_op jit(solution)/shard_map/ppermute | solution.py:571
  1128.3 323.5 %collective-permute-start.7 = (s32[2,8392]{1,0:T(2,128)S(1)}, s32[2,8392]{1,0:T(2,128)S(1)}, u32[]{:S(2)}, u32[]{:S(2)}) collective-permute-start(s32[2,8392]{1,0:T(2,128)S(1)} %pad_add_fusion), channel_id=1, source_target_pairs={{0,1},{1,2},{2,3},{3,0},{4,5},{5,6},{6,7},{7,4}} | collective-permute-start | bytes 201416 | tf_op jit(solution)/shard_map/ppermute | solution.py:536
  1128.4 326.3 %collective-permute-start.22 = (f32[512,128]{1,0:T(8,128)S(1)}, f32[512,128]{1,0:T(8,128)S(1)}, u32[]{:S(2)}, u32[]{:S(2)}) collective-permute-start(f32[512,128]{1,0:T(8,128)S(1)} %copy-done.46), channel_id=1, source_target_pairs={{0,1},{1,2},{2,3},{3,0},{4,5},{5,6},{6,7},{7,4}} | collective-permute-start | bytes 786440 | tf_op jit(solution)/shard_map/ppermute | solution.py:567
  1650.9 206.1 %collective-permute-start.33 = (bf16[8192,256]{1,0:T(8,128)(2,1)}, bf16[8192,256]{1,0:T(8,128)(2,1)}, u32[]{:S(2)}, u32[]{:S(2)}) collective-permute-start(bf16[8192,256]{1,0:T(8,128)(2,1)} %get-tuple-element.202.qm_ref), channel_id=1, source_target_pairs={{0,4},{4,0},{1,5},{5,1},{2,6},{6,2},{3,7},{7,3}} | collective-permute-start | bytes 12582920 | tf_op jit(solution)/shard_map/ppermute | solution.py:555
  1684.5 254.7 %collective-permute-start.30 = (bf16[8192,256]{1,0:T(8,128)(2,1)}, bf16[8192,256]{1,0:T(8,128)(2,1)}, u32[]{:S(2)}, u32[]{:S(2)}) collective-permute-start(bf16[8192,256]{1,0:T(8,128)(2,1)} %get-tuple-element.196.qm_ref), channel_id=1, source_target_pairs={{0,4},{4,0},{1,5},{5,1},{2,6},{6,2},{3,7},{7,3}} | collective-permute-start | bytes 12582920 | tf_op jit(solution)/shard_map/ppermute | solution.py:555
  2029.5 533.0 %collective-permute-start.38 = (f32[16384,128]{1,0:T(8,128)}, f32[16384,128]{1,0:T(8,128)}, u32[]{:S(2)}, u32[]{:S(2)}) collective-permute-start(f32[16384,128]{1,0:T(8,128)} %get-tuple-element.209), channel_id=1, source_target_pairs={{0,2},{1,3},{2,0},{3,1},{4,6},{5,7},{6,4},{7,5}} | collective-permute-start | bytes 25165832 | tf_op jit(solution)/shard_map/ppermute | solution.py:566
  2031.1 571.4 %collective-permute-start.36 = (f32[16384,128]{1,0:T(8,128)}, f32[16384,128]{1,0:T(8,128)}, u32[]{:S(2)}, u32[]{:S(2)}) collective-permute-start(f32[16384,128]{1,0:T(8,128)} %get-tuple-element.207), channel_id=1, source_target_pairs={{0,2},{1,3},{2,0},{3,1},{4,6},{5,7},{6,4},{7,5}} | collective-permute-start | bytes 25165832 | tf_op jit(solution)/shard_map/ppermute | solution.py:566
  2047.2 633.9 %collective-permute-start.43 = (f32[14824,128]{1,0:T(8,128)}, f32[14824,128]{1,0:T(8,128)}, u32[]{:S(2)}, u32[]{:S(2)}) collective-permute-start(f32[14824,128]{1,0:T(8,128)} %add.26.one_ref), channel_id=1, source_target_pairs={{0,2},{1,3},{2,0},{3,1},{4,6},{5,7},{6,4},{7,5}} | collective-permute-start | bytes 22769672 | tf_op jit(solution)/shard_map/ppermute | solution.py:571
  2049.0 507.9 %collective-permute-start.24 = (s32[2,8392]{1,0:T(2,128)S(1)}, s32[2,8392]{1,0:T(2,128)S(1)}, u32[]{:S(2)}, u32[]{:S(2)}) collective-permute-start(s32[2,8392]{1,0:T(2,128)S(1)} %pad_add_fusion.1), channel_id=1, source_target_pairs={{0,2},{1,3},{2,0},{3,1},{4,6},{5,7},{6,4},{7,5}} | collective-permute-start | bytes 201416 | tf_op jit(solution)/shard_map/ppermute | solution.py:536
  2049.4 513.1 %collective-permute-start.39 = (f32[512,128]{1,0:T(8,128)S(1)}, f32[512,128]{1,0:T(8,128)S(1)}, u32[]{:S(2)}, u32[]{:S(2)}) collective-permute-start(f32[512,128]{1,0:T(8,128)S(1)} %copy-done.48), channel_id=1, source_target_pairs={{0,2},{1,3},{2,0},{3,1},{4,6},{5,7},{6,4},{7,5}} | collective-permute-start | bytes 786440 | tf_op jit(solution)/shard_map/ppermute | solution.py:567
  2758.4 190.7 %collective-permute-start.50 = (bf16[8192,256]{1,0:T(8,128)(2,1)}, bf16[8192,256]{1,0:T(8,128)(2,1)}, u32[]{:S(2)}, u32[]{:S(2)}) collective-permute-start(bf16[8192,256]{1,0:T(8,128)(2,1)} %get-tuple-element.232.qm_ref), channel_id=1, source_target_pairs={{0,4},{4,0},{1,5},{5,1},{2,6},{6,2},{3,7},{7,3}} | collective-permute-start | bytes 12582920 | tf_op jit(solution)/shard_map/ppermute | solution.py:555
  2792.0 239.2 %collective-permute-start.47 = (bf16[8192,256]{1,0:T(8,128)(2,1)}, bf16[8192,256]{1,0:T(8,128)(2,1)}, u32[]{:S(2)}, u32[]{:S(2)}) collective-permute-start(bf16[8192,256]{1,0:T(8,128)(2,1)} %get-tuple-element.226.qm_ref), channel_id=1, source_target_pairs={{0,4},{4,0},{1,5},{5,1},{2,6},{6,2},{3,7},{7,3}} | collective-permute-start | bytes 12582920 | tf_op jit(solution)/shard_map/ppermute | solution.py:555
  3121.5 349.2 %collective-permute-start.55 = (f32[16384,128]{1,0:T(8,128)}, f32[16384,128]{1,0:T(8,128)}, u32[]{:S(2)}, u32[]{:S(2)}) collective-permute-start(f32[16384,128]{1,0:T(8,128)} %get-tuple-element.239), channel_id=1, source_target_pairs={{0,3},{1,0},{2,1},{3,2},{4,7},{5,4},{6,5},{7,6}} | collective-permute-start | bytes 25165832 | tf_op jit(solution)/shard_map/ppermute | solution.py:566
  3123.1 387.6 %collective-permute-start.53 = (f32[16384,128]{1,0:T(8,128)}, f32[16384,128]{1,0:T(8,128)}, u32[]{:S(2)}, u32[]{:S(2)}) collective-permute-start(f32[16384,128]{1,0:T(8,128)} %get-tuple-element.237), channel_id=1, source_target_pairs={{0,3},{1,0},{2,1},{3,2},{4,7},{5,4},{6,5},{7,6}} | collective-permute-start | bytes 25165832 | tf_op jit(solution)/shard_map/ppermute | solution.py:566
  3139.3 474.6 %collective-permute-start.60 = (f32[14824,128]{1,0:T(8,128)}, f32[14824,128]{1,0:T(8,128)}, u32[]{:S(2)}, u32[]{:S(2)}) collective-permute-start(f32[14824,128]{1,0:T(8,128)} %add.27.one_ref), channel_id=1, source_target_pairs={{0,2},{1,3},{2,0},{3,1},{4,6},{5,7},{6,4},{7,5}} | collective-permute-start | bytes 22769672 | tf_op jit(solution)/shard_map/ppermute | solution.py:571
  3140.8 326.7 %collective-permute-start.41 = (s32[2,8392]{1,0:T(2,128)S(1)}, s32[2,8392]{1,0:T(2,128)S(1)}, u32[]{:S(2)}, u32[]{:S(2)}) collective-permute-start(s32[2,8392]{1,0:T(2,128)S(1)} %pad_add_fusion.2), channel_id=1, source_target_pairs={{0,3},{1,0},{2,1},{3,2},{4,7},{5,4},{6,5},{7,6}} | collective-permute-start | bytes 201416 | tf_op jit(solution)/shard_map/ppermute | solution.py:536
  3140.9 329.8 %collective-permute-start.56 = (f32[512,128]{1,0:T(8,128)S(1)}, f32[512,128]{1,0:T(8,128)S(1)}, u32[]{:S(2)}, u32[]{:S(2)}) collective-permute-start(f32[512,128]{1,0:T(8,128)S(1)} %copy-done.47), channel_id=1, source_target_pairs={{0,3},{1,0},{2,1},{3,2},{4,7},{5,4},{6,5},{7,6}} | collective-permute-start | bytes 786440 | tf_op jit(solution)/shard_map/ppermute | solution.py:567
  3728.2 281.8 %collective-permute-start.58 = (f32[200,16384]{1,0:T(8,128)}, f32[200,16384]{1,0:T(8,128)}, u32[]{:S(2)}, u32[]{:S(2)}) collective-permute-start(f32[200,16384]{1,0:T(8,128)} %flip_half.2.mine_ref.rest_0_), channel_id=1, source_target_pairs={{0,4},{4,0},{1,5},{5,1},{2,6},{6,2},{3,7},{7,3}} | collective-permute-start | bytes 39321608 | tf_op jit(solution)/shard_map/ppermute | solution.py:579
  3811.5 228.7 %collective-permute-start.64 = (f32[400,7412]{1,0:T(8,128)}, f32[400,7412]{1,0:T(8,128)}, u32[]{:S(2)}, u32[]{:S(2)}) collective-permute-start(f32[400,7412]{1,0:T(8,128)} %join_columns.3), channel_id=1, source_target_pairs={{0,1},{1,0},{2,3},{3,2},{4,5},{5,4},{6,7},{7,6}} | collective-permute-start | bytes 35577608 | tf_op jit(solution)/shard_map/ppermute | solution.py:595
  (94 other events, 4249.6 us)
Sparse Core Ops, SparseCore 0:
  12.6 21.3 all-gather.3

commit v4 on v3

--- a/solution.py
+++ b/solution.py
@@ -14,6 +14,7 @@
 LANES = 128
 BLOCK = 256
 WIDE_ROWS = 512
+PIECES = 4
 VMEM_CAP = 66_000_000
 
 
@@ -74,12 +75,13 @@
     out_ref[pl.ds(width, width), :] = imag.T[:width, :]
 
 
-def flip_half(half, dim):
-    rows = half.shape[0] // 2
+def flip_half(half, dim, start=0, rows=None):
+    rows = half.shape[0] // 2 if rows is None else rows
+    skip = start // WIDE_ROWS
     return pl.pallas_call(
         flip_kernel,
         grid=(pl.cdiv(rows, WIDE_ROWS),),
-        in_specs=[pl.BlockSpec((2 * WIDE_ROWS, LANES), lambda b: (b, 0))],
+        in_specs=[pl.BlockSpec((2 * WIDE_ROWS, LANES), lambda b: (b + skip, 0))],
         out_specs=pl.BlockSpec((dim // 2, WIDE_ROWS), lambda b: (0, b)),
         out_shape=jax.ShapeDtypeStruct((dim // 2, rows), jnp.float32),
         compiler_params=pltpu.CompilerParams(dimension_semantics=("arbitrary",)),
@@ -474,7 +476,8 @@
     )(param, grad, state, sums, sums_peer)
 
 
-def join_kernel(part_ref, mine_ref, peer_ref, out_ref):
+def join_kernel(part_ref, mine_ref, peer_ref, *rest):
+    out_ref = rest[-1]
     second = part_ref[0] != 0
     width = mine_ref.shape[0] // 2
     for side in range(2):
@@ -483,19 +486,21 @@
         out_ref[pl.ds((2 * side + 1) * width, width), :] = jnp.where(second, mine, peer)
 
 
-def join_columns(part, mine, peer):
+def join_columns(part, mine, peer, start=0, total=None, whole=()):
     width, rows = mine.shape
+    skip = start // WIDE_ROWS
     half = pl.BlockSpec((width, WIDE_ROWS), lambda b: (0, b))
     return pl.pallas_call(
         join_kernel,
         grid=(pl.cdiv(rows, WIDE_ROWS),),
-        in_specs=[SCALARS, half, half],
-        out_specs=pl.BlockSpec((2 * width, WIDE_ROWS), lambda b: (0, b)),
-        out_shape=jax.ShapeDtypeStruct((2 * width, rows), jnp.float32),
+        in_specs=[SCALARS, half, half] + [ANYWHERE] * len(whole),
+        out_specs=pl.BlockSpec((2 * width, WIDE_ROWS), lambda b: (0, b + skip)),
+        out_shape=jax.ShapeDtypeStruct((2 * width, total or rows), jnp.float32),
+        input_output_aliases={3: 0} if whole else {},
         compiler_params=pltpu.CompilerParams(dimension_semantics=("arbitrary",)),
         cost_estimate=pl.CostEstimate(flops=mine.size, bytes_accessed=16 * mine.size, transcendentals=0),
         name="join_columns",
-    )(part[None], mine, peer)
+    )(part[None], mine, peer, *whole)
 
 
 def solution(mesh):
@@ -506,7 +511,7 @@
     chip_swap = [(src, src ^ 2) for src in range(ent_size)]
 
     def device_epoch(ent_table, ada_state, rel_table, head_idx, tail_idx, rel_idx, edge_mask, neg_idx):
-        _, dim = ent_table.shape
+        ent_rows, dim = ent_table.shape
         rel_rows = rel_table.shape[0]
         edge_count = head_idx.shape[-1]
         negs = neg_idx.shape[-1]
@@ -545,7 +550,9 @@
                 fetch = [((dest + round_idx) % ent_size, dest) for dest in range(ent_size)]
                 table = lax.ppermute(table, "ent", fetch)
             ids = [[field(slot, bucket, round_idx) for slot in range(3)] for bucket in range(data_size)]
-            asked = [query_rows(core_at, ent, rel_mine, rel_other, ids[bucket][0], ids[bucket][2]) for bucket in range(data_size)]
+            asked = []
+            for bucket in range(data_size):
+                asked.append(query_rows(core_at, ent, rel_mine, rel_other, ids[bucket][0], ids[bucket][2]))
             back = [(src, (src + round_idx) % ent_size) for src in range(ent_size)]
             targets = owned(round_idx)
             before = None
@@ -575,15 +582,22 @@
             ent, state, table = adagrad_step(ent, state, g_ent, ent_sums[0], LEARN_ENT, dim, swap, True)
             after = state
             if round_idx == ent_size - 1:
-                ent_cols = after = flip_half(ent, dim)
-                ent_cols_peer = lax.ppermute(ent_cols, "data", swap)
+                size = ent_rows // PIECES
+                ent_cols = [flip_half(ent, dim, piece * size, size) for piece in range(PIECES)]
+                after = ent_cols[0]
+                ent_peer = []
+                for piece in range(PIECES):
+                    ent_peer.append(lax.ppermute(ent_cols[piece], "data", swap))
             g_rel, rel_sums = square_sums(chip_sum, chip_other, rel_state.shape[0], (after,))
             rel_mine, rel_state = adagrad_step(rel_mine, rel_state, g_rel, rel_sums, LEARN_REL, dim, swap, False)
             if round_idx < ent_size - 1:
                 rel_other = lax.ppermute(rel_mine, "ent", core_swap)
             losses.append(jnp.where(part == 0, sums[0], sums[1]) / edge_count)
 
-        ent_out = join_columns(part, ent_cols, ent_cols_peer).T
+        ent_out = ()
+        for piece in range(PIECES):
+            ent_out = (join_columns(part, ent_cols[piece], ent_peer[piece], piece * size, ent_rows, ent_out),)
+        ent_out = ent_out[0].T
         rel_cols = flip_half(rel_mine, dim)
         quarter = rel_cols.shape[-1] // 2
         chip = lax.axis_index("ent") // 2

time: 4090 us -> 4140 us (1.012)
    ppermute x1 -> x4, waiting for transfers between devices: 198 us -> 234 us  [device_epoch(): ent_peer.append(lax.ppermute(ent_cols[piece], 'data', swap))]
  transfers between devices with their start and end apart: 66 -> 69, of which waited for: 31 -> 33; matrix products, arithmetic and copies ran while one was open for 1% -> 1% of each run, Pallas kernels for 34% -> 33%
where the time goes in v4:
time: 4140 us; the launch traced here: 4110 us
  waiting for transfers between devices  2050 us (50%)
  Pallas kernels  1890 us (46%)
  starting transfers between devices  64.5 us (2%)
  other arithmetic  54.1 us (1%)
    ppermute x3, waiting for transfers between devices, owned(): lax.ppermute(mine, 'ent', [(src, (src + round_idx) % ent_size) for src in...  1150 us
    pallas_call x8, Pallas kernels, bucket_grads(): pl.pallas_call(functools.partial(grad_kernel, int(last), negs), grid=(blo...  684 us
    pallas_call x8, Pallas kernels, add_rows(): pl.pallas_call(functools.partial(add_kernel, neg_ids.shape[-1]), grid=(bl...  316 us
    pallas_call x8, Pallas kernels, query_rows(): pl.pallas_call(query_kernel, grid=(blocks,), in_specs=[SCALARS, smem_bloc...  255 us
    ppermute x8, waiting for transfers between devices, device_epoch(): p_peer = lax.ppermute(p_mine, 'data', swap)  249 us
    pallas_call x8, Pallas kernels, tail_rows(): pl.pallas_call(functools.partial(tail_kernel, negs), grid=(blocks,), in_s...  238 us
    ppermute x4, waiting for transfers between devices, device_epoch(): ent_peer.append(lax.ppermute(ent_cols[piece], 'data', swap))  234 us
    pallas_call x8, Pallas kernels, adagrad_step(): pl.pallas_call(functools.partial(step_kernel, rate, dim), grid=(state.sha...  189 us
  transfers between devices with their start and end apart: 69, of which 33 were waited for; matrix products, arithmetic and copies ran while one was open for 1% of the time, Pallas kernels for 33%

profile of v4, /device:TPU:0, one launch (start us, length us, event | category | flops | bytes accessed | tf_op | source)
XLA Modules:
  0.0 4111.5 jit_solution(1364263527121762544)
XLA Ops:
  218.6 89.9 %collective-permute-done.4.pp_ref = f32[32,1,256]{2,1,0:T(1,128)S(1)} collective-permute-done((f32[32,1,256]{2,1,0:T(1,128)S(1)}, f32[32,1,256]{2,1,0:T(1,128)S(1)}, u32[]{:S(2)}, u32[]{:S(2)}) %collective-permute-start.4) | collective-permute-done | bytes 32800 | tf_op jit(solution)/shard_map/ppermute | solution.py:566
  310.9 81.4 %bucket_grads.8 = (f32[32768,128]{1,0:T(8,128)}, f32[29648,128]{1,0:T(8,128)}, f32[16384,128]{1,0:T(8,128)}, f32[512,128]{1,0:T(8,128)}, f32[1,128]{1,0:T(1,128)}) custom-call(s32[1]{0:T(128)} %bitcast.9.core_ref, s32[32,1,256]{2,1,0:T(1,128)} %bitcast.149, s32[32,1,256]{2,1,0:T(1,128)} %bitcast.147, f32[16384,128]{1,0:T(8,128)} %get-tuple-element.140.a_ref, ...), custom_call_target="tpu_custom_call" | custom-call | flops 300000000 | bytes 200000000 | tf_op jit(solution)/shard_map/bucket_grads/pallas_call | solution.py:336
  393.0 89.6 %bucket_grads.9 = (f32[32768,128]{1,0:T(8,128)}, f32[14824,128]{1,0:T(8,128)}, f32[14824,128]{1,0:T(8,128)}, f32[16384,128]{1,0:T(8,128)}, f32[512,128]{1,0:T(8,128)}, /*index=5*/f32[1,128]{1,0:T(1,128)}) custom-call(s32[1]{0:T(128)} %bitcast.9.core_ref, s32[32,1,256]{2,1,0:T(1,128)} %bitcast.133, s32[32,1,256]{2,1,0:T(1,128)} %bitcast.131, ...), custom_call_target="tpu_custom_call" | custom-call | flops 300000000 | bytes 200000000 | tf_op jit(solution)/shard_map/bucket_grads/pallas_call | solution.py:336
  541.0 39.7 add_rows.9
  619.3 46.7 %collective-permute-done.9.two_ref = f32[14824,128]{1,0:T(8,128)} collective-permute-done((f32[14824,128]{1,0:T(8,128)}, f32[14824,128]{1,0:T(8,128)}, u32[]{:S(2)}, u32[]{:S(2)}) %collective-permute-start.9) | collective-permute-done | bytes 7589920 | tf_op jit(solution)/shard_map/ppermute | solution.py:578
  854.3 78.3 %collective-permute-done.17.pp_ref = f32[32,1,256]{2,1,0:T(1,128)S(1)} collective-permute-done((f32[32,1,256]{2,1,0:T(1,128)S(1)}, f32[32,1,256]{2,1,0:T(1,128)S(1)}, u32[]{:S(2)}, u32[]{:S(2)}) %collective-permute-start.17) | collective-permute-done | bytes 32800 | tf_op jit(solution)/shard_map/ppermute | solution.py:566
  933.6 81.4 %bucket_grads.10 = (f32[32768,128]{1,0:T(8,128)}, f32[29648,128]{1,0:T(8,128)}, f32[16384,128]{1,0:T(8,128)}, f32[512,128]{1,0:T(8,128)}, f32[1,128]{1,0:T(1,128)}) custom-call(s32[1]{0:T(128)} %bitcast.9.core_ref, s32[32,1,256]{2,1,0:T(1,128)} %bitcast.145, s32[32,1,256]{2,1,0:T(1,128)} %bitcast.143, f32[16384,128]{1,0:T(8,128)} %get-tuple-element.169.a_ref, ...), custom_call_target="tpu_custom_call" | custom-call | flops 300000000 | bytes 200000000 | tf_op jit(solution)/shard_map/bucket_grads/pallas_call | solution.py:336
  1015.7 89.6 %bucket_grads.11 = (f32[32768,128]{1,0:T(8,128)}, f32[14824,128]{1,0:T(8,128)}, f32[14824,128]{1,0:T(8,128)}, f32[16384,128]{1,0:T(8,128)}, f32[512,128]{1,0:T(8,128)}, /*index=5*/f32[1,128]{1,0:T(1,128)}) custom-call(s32[1]{0:T(128)} %bitcast.9.core_ref, s32[32,1,256]{2,1,0:T(1,128)} %bitcast.127, s32[32,1,256]{2,1,0:T(1,128)} %bitcast.125, ...), custom_call_target="tpu_custom_call" | custom-call | flops 300000000 | bytes 200000000 | tf_op jit(solution)/shard_map/bucket_grads/pallas_call | solution.py:336
  1128.7 323.1 %collective-permute-done.7 = s32[2,8392]{1,0:T(2,128)S(1)} collective-permute-done((s32[2,8392]{1,0:T(2,128)S(1)}, s32[2,8392]{1,0:T(2,128)S(1)}, u32[]{:S(2)}, u32[]{:S(2)}) %collective-permute-start.7) | collective-permute-done | bytes 67168 | tf_op jit(solution)/shard_map/ppermute | solution.py:541
  1495.3 39.7 add_rows.11
  1684.8 104.8 %collective-permute-done.29.tab_hbm = bf16[32768,128]{1,0:T(8,128)(2,1)} collective-permute-done((bf16[32768,128]{1,0:T(8,128)(2,1)}, bf16[32768,128]{1,0:T(8,128)(2,1)}, u32[]{:S(2)}, u32[]{:S(2)}) %collective-permute-start.29) | collective-permute-done | bytes 8388640 | tf_op jit(solution)/shard_map/ppermute | solution.py:551
  1857.6 81.5 %bucket_grads.12 = (f32[32768,128]{1,0:T(8,128)}, f32[29648,128]{1,0:T(8,128)}, f32[16384,128]{1,0:T(8,128)}, f32[512,128]{1,0:T(8,128)}, f32[1,128]{1,0:T(1,128)}) custom-call(s32[1]{0:T(128)} %bitcast.9.core_ref, s32[32,1,256]{2,1,0:T(1,128)} %bitcast.141, s32[32,1,256]{2,1,0:T(1,128)} %bitcast.139, f32[16384,128]{1,0:T(8,128)} %get-tuple-element.199.a_ref, ...), custom_call_target="tpu_custom_call" | custom-call | flops 300000000 | bytes 200000000 | tf_op jit(solution)/shard_map/bucket_grads/pallas_call | solution.py:336
  1939.8 89.5 %bucket_grads.13 = (f32[32768,128]{1,0:T(8,128)}, f32[14824,128]{1,0:T(8,128)}, f32[14824,128]{1,0:T(8,128)}, f32[16384,128]{1,0:T(8,128)}, f32[512,128]{1,0:T(8,128)}, /*index=5*/f32[1,128]{1,0:T(1,128)}) custom-call(s32[1]{0:T(128)} %bitcast.9.core_ref, s32[32,1,256]{2,1,0:T(1,128)} %bitcast.123, s32[32,1,256]{2,1,0:T(1,128)} %bitcast.121, ...), custom_call_target="tpu_custom_call" | custom-call | flops 300000000 | bytes 200000000 | tf_op jit(solution)/shard_map/bucket_grads/pallas_call | solution.py:336
  2050.9 505.9 %collective-permute-done.24 = s32[2,8392]{1,0:T(2,128)S(1)} collective-permute-done((s32[2,8392]{1,0:T(2,128)S(1)}, s32[2,8392]{1,0:T(2,128)S(1)}, u32[]{:S(2)}, u32[]{:S(2)}) %collective-permute-start.24) | collective-permute-done | bytes 67168 | tf_op jit(solution)/shard_map/ppermute | solution.py:541
  2870.5 76.7 %collective-permute-done.51.pp_ref = f32[32,1,256]{2,1,0:T(1,128)S(1)} collective-permute-done((f32[32,1,256]{2,1,0:T(1,128)S(1)}, f32[32,1,256]{2,1,0:T(1,128)S(1)}, u32[]{:S(2)}, u32[]{:S(2)}) %collective-permute-start.51) | collective-permute-done | bytes 32800 | tf_op jit(solution)/shard_map/ppermute | solution.py:566
  2949.5 81.4 %bucket_grads.14 = (f32[32768,128]{1,0:T(8,128)}, f32[29648,128]{1,0:T(8,128)}, f32[16384,128]{1,0:T(8,128)}, f32[512,128]{1,0:T(8,128)}, f32[1,128]{1,0:T(1,128)}) custom-call(s32[1]{0:T(128)} %bitcast.9.core_ref, s32[32,1,256]{2,1,0:T(1,128)} %bitcast.137, s32[32,1,256]{2,1,0:T(1,128)} %bitcast.135, f32[16384,128]{1,0:T(8,128)} %get-tuple-element.229.a_ref, ...), custom_call_target="tpu_custom_call" | custom-call | flops 300000000 | bytes 200000000 | tf_op jit(solution)/shard_map/bucket_grads/pallas_call | solution.py:336
  3031.6 89.6 %bucket_grads.15 = (f32[32768,128]{1,0:T(8,128)}, f32[14824,128]{1,0:T(8,128)}, f32[14824,128]{1,0:T(8,128)}, f32[16384,128]{1,0:T(8,128)}, f32[512,128]{1,0:T(8,128)}, /*index=5*/f32[1,128]{1,0:T(1,128)}) custom-call(s32[1]{0:T(128)} %bitcast.9.core_ref, s32[32,1,256]{2,1,0:T(1,128)} %bitcast.119, s32[32,1,256]{2,1,0:T(1,128)} %bitcast.117, ...), custom_call_target="tpu_custom_call" | custom-call | flops 300000000 | bytes 200000000 | tf_op jit(solution)/shard_map/bucket_grads/pallas_call | solution.py:336
  3141.3 326.0 %collective-permute-done.41 = s32[2,8392]{1,0:T(2,128)S(1)} collective-permute-done((s32[2,8392]{1,0:T(2,128)S(1)}, s32[2,8392]{1,0:T(2,128)S(1)}, u32[]{:S(2)}, u32[]{:S(2)}) %collective-permute-start.41) | collective-permute-done | bytes 67168 | tf_op jit(solution)/shard_map/ppermute | solution.py:541
  3511.1 39.8 add_rows.15
  3645.2 64.4 %collective-permute-done.65 = f32[200,3706]{1,0:T(8,128)S(1)} collective-permute-done((f32[200,3706]{1,0:T(8,128)S(1)}, f32[200,3706]{1,0:T(8,128)S(1)}, u32[]{:S(2)}, u32[]{:S(2)}) %collective-permute-start.65) | collective-permute-done | bytes 2964832 | tf_op jit(solution)/shard_map/ppermute | solution.py:604
  3710.8 62.9 %collective-permute-done.66 = f32[200,3706]{1,0:T(8,128)} collective-permute-done((f32[200,3706]{1,0:T(8,128)S(1)}, f32[200,3706]{1,0:T(8,128)}, u32[]{:S(2)}, u32[]{:S(2)}) %collective-permute-start.66) | collective-permute-done | bytes 2964832 | tf_op jit(solution)/shard_map/ppermute | solution.py:605
  3820.6 47.7 %collective-permute-done.61.peer_ref = f32[200,4096]{1,0:T(8,128)} collective-permute-done((f32[200,4096]{1,0:T(8,128)S(1)}, f32[200,4096]{1,0:T(8,128)}, u32[]{:S(2)}, u32[]{:S(2)}) %collective-permute-start.61) | collective-permute-done | bytes 3276832 | tf_op jit(solution)/shard_map/ppermute | solution.py:590
  3876.2 132.5 %collective-permute-done.60.peer_ref = f32[200,4096]{1,0:T(8,128)} collective-permute-done((f32[200,4096]{1,0:T(8,128)}, f32[200,4096]{1,0:T(8,128)}, u32[]{:S(2)}, u32[]{:S(2)}) %collective-permute-start.60) | collective-permute-done | bytes 3276832 | tf_op jit(solution)/shard_map/ppermute | solution.py:590
  4024.6 53.8 %collective-permute-done.58.peer_ref = f32[200,4096]{1,0:T(8,128)} collective-permute-done((f32[200,4096]{1,0:T(8,128)}, f32[200,4096]{1,0:T(8,128)}, u32[]{:S(2)}, u32[]{:S(2)}) %collective-permute-start.58) | collective-permute-done | bytes 3276832 | tf_op jit(solution)/shard_map/ppermute | solution.py:590
  (314 shorter events, 1380.9 us)
Async XLA Ops:
  153.4 238.9 %collective-permute-start = (bf16[8192,256]{1,0:T(8,128)(2,1)}, bf16[8192,256]{1,0:T(8,128)(2,1)}, u32[]{:S(2)}, u32[]{:S(2)}) collective-permute-start(bf16[8192,256]{1,0:T(8,128)(2,1)} %get-tuple-element.137.qm_ref), channel_id=1, source_target_pairs={{0,4},{4,0},{1,5},{5,1},{2,6},{6,2},{3,7},{7,3}} | collective-permute-start | bytes 12582920 | tf_op jit(solution)/shard_map/ppermute | solution.py:562
  775.8 239.3 %collective-permute-start.13 = (bf16[8192,256]{1,0:T(8,128)(2,1)}, bf16[8192,256]{1,0:T(8,128)(2,1)}, u32[]{:S(2)}, u32[]{:S(2)}) collective-permute-start(bf16[8192,256]{1,0:T(8,128)(2,1)} %get-tuple-element.166.qm_ref), channel_id=1, source_target_pairs={{0,4},{4,0},{1,5},{5,1},{2,6},{6,2},{3,7},{7,3}} | collective-permute-start | bytes 12582920 | tf_op jit(solution)/shard_map/ppermute | solution.py:562
  1105.4 349.2 %collective-permute-start.21 = (f32[16384,128]{1,0:T(8,128)}, f32[16384,128]{1,0:T(8,128)}, u32[]{:S(2)}, u32[]{:S(2)}) collective-permute-start(f32[16384,128]{1,0:T(8,128)} %get-tuple-element.179), channel_id=1, source_target_pairs={{0,1},{1,2},{2,3},{3,0},{4,5},{5,6},{6,7},{7,4}} | collective-permute-start | bytes 25165832 | tf_op jit(solution)/shard_map/ppermute | solution.py:573
  1105.9 388.7 %collective-permute-start.19 = (f32[16384,128]{1,0:T(8,128)}, f32[16384,128]{1,0:T(8,128)}, u32[]{:S(2)}, u32[]{:S(2)}) collective-permute-start(f32[16384,128]{1,0:T(8,128)} %get-tuple-element.177), channel_id=1, source_target_pairs={{0,1},{1,2},{2,3},{3,0},{4,5},{5,6},{6,7},{7,4}} | collective-permute-start | bytes 25165832 | tf_op jit(solution)/shard_map/ppermute | solution.py:573
  1123.1 450.2 %collective-permute-start.26 = (f32[14824,128]{1,0:T(8,128)}, f32[14824,128]{1,0:T(8,128)}, u32[]{:S(2)}, u32[]{:S(2)}) collective-permute-start(f32[14824,128]{1,0:T(8,128)} %add.25.one_ref), channel_id=1, source_target_pairs={{0,2},{1,3},{2,0},{3,1},{4,6},{5,7},{6,4},{7,5}} | collective-permute-start | bytes 22769672 | tf_op jit(solution)/shard_map/ppermute | solution.py:578
  1128.2 323.5 %collective-permute-start.7 = (s32[2,8392]{1,0:T(2,128)S(1)}, s32[2,8392]{1,0:T(2,128)S(1)}, u32[]{:S(2)}, u32[]{:S(2)}) collective-permute-start(s32[2,8392]{1,0:T(2,128)S(1)} %pad_add_fusion), channel_id=1, source_target_pairs={{0,1},{1,2},{2,3},{3,0},{4,5},{5,6},{6,7},{7,4}} | collective-permute-start | bytes 201416 | tf_op jit(solution)/shard_map/ppermute | solution.py:541
  1128.3 326.3 %collective-permute-start.22 = (f32[512,128]{1,0:T(8,128)S(1)}, f32[512,128]{1,0:T(8,128)S(1)}, u32[]{:S(2)}, u32[]{:S(2)}) collective-permute-start(f32[512,128]{1,0:T(8,128)S(1)} %copy-done.47), channel_id=1, source_target_pairs={{0,1},{1,2},{2,3},{3,0},{4,5},{5,6},{6,7},{7,4}} | collective-permute-start | bytes 786440 | tf_op jit(solution)/shard_map/ppermute | solution.py:574
  1650.9 206.0 %collective-permute-start.33 = (bf16[8192,256]{1,0:T(8,128)(2,1)}, bf16[8192,256]{1,0:T(8,128)(2,1)}, u32[]{:S(2)}, u32[]{:S(2)}) collective-permute-start(bf16[8192,256]{1,0:T(8,128)(2,1)} %get-tuple-element.202.qm_ref), channel_id=1, source_target_pairs={{0,4},{4,0},{1,5},{5,1},{2,6},{6,2},{3,7},{7,3}} | collective-permute-start | bytes 12582920 | tf_op jit(solution)/shard_map/ppermute | solution.py:562
  1684.4 254.7 %collective-permute-start.30 = (bf16[8192,256]{1,0:T(8,128)(2,1)}, bf16[8192,256]{1,0:T(8,128)(2,1)}, u32[]{:S(2)}, u32[]{:S(2)}) collective-permute-start(bf16[8192,256]{1,0:T(8,128)(2,1)} %get-tuple-element.196.qm_ref), channel_id=1, source_target_pairs={{0,4},{4,0},{1,5},{5,1},{2,6},{6,2},{3,7},{7,3}} | collective-permute-start | bytes 12582920 | tf_op jit(solution)/shard_map/ppermute | solution.py:562
  2029.3 533.0 %collective-permute-start.38 = (f32[16384,128]{1,0:T(8,128)}, f32[16384,128]{1,0:T(8,128)}, u32[]{:S(2)}, u32[]{:S(2)}) collective-permute-start(f32[16384,128]{1,0:T(8,128)} %get-tuple-element.209), channel_id=1, source_target_pairs={{0,2},{1,3},{2,0},{3,1},{4,6},{5,7},{6,4},{7,5}} | collective-permute-start | bytes 25165832 | tf_op jit(solution)/shard_map/ppermute | solution.py:573
  2031.0 571.4 %collective-permute-start.36 = (f32[16384,128]{1,0:T(8,128)}, f32[16384,128]{1,0:T(8,128)}, u32[]{:S(2)}, u32[]{:S(2)}) collective-permute-start(f32[16384,128]{1,0:T(8,128)} %get-tuple-element.207), channel_id=1, source_target_pairs={{0,2},{1,3},{2,0},{3,1},{4,6},{5,7},{6,4},{7,5}} | collective-permute-start | bytes 25165832 | tf_op jit(solution)/shard_map/ppermute | solution.py:573
  2047.1 633.9 %collective-permute-start.43 = (f32[14824,128]{1,0:T(8,128)}, f32[14824,128]{1,0:T(8,128)}, u32[]{:S(2)}, u32[]{:S(2)}) collective-permute-start(f32[14824,128]{1,0:T(8,128)} %add.26.one_ref), channel_id=1, source_target_pairs={{0,2},{1,3},{2,0},{3,1},{4,6},{5,7},{6,4},{7,5}} | collective-permute-start | bytes 22769672 | tf_op jit(solution)/shard_map/ppermute | solution.py:578
  2048.8 507.9 %collective-permute-start.24 = (s32[2,8392]{1,0:T(2,128)S(1)}, s32[2,8392]{1,0:T(2,128)S(1)}, u32[]{:S(2)}, u32[]{:S(2)}) collective-permute-start(s32[2,8392]{1,0:T(2,128)S(1)} %pad_add_fusion.1), channel_id=1, source_target_pairs={{0,2},{1,3},{2,0},{3,1},{4,6},{5,7},{6,4},{7,5}} | collective-permute-start | bytes 201416 | tf_op jit(solution)/shard_map/ppermute | solution.py:541
  2049.2 513.1 %collective-permute-start.39 = (f32[512,128]{1,0:T(8,128)S(1)}, f32[512,128]{1,0:T(8,128)S(1)}, u32[]{:S(2)}, u32[]{:S(2)}) collective-permute-start(f32[512,128]{1,0:T(8,128)S(1)} %copy-done.49), channel_id=1, source_target_pairs={{0,2},{1,3},{2,0},{3,1},{4,6},{5,7},{6,4},{7,5}} | collective-permute-start | bytes 786440 | tf_op jit(solution)/shard_map/ppermute | solution.py:574
  2791.9 239.1 %collective-permute-start.47 = (bf16[8192,256]{1,0:T(8,128)(2,1)}, bf16[8192,256]{1,0:T(8,128)(2,1)}, u32[]{:S(2)}, u32[]{:S(2)}) collective-permute-start(bf16[8192,256]{1,0:T(8,128)(2,1)} %get-tuple-element.226.qm_ref), channel_id=1, source_target_pairs={{0,4},{4,0},{1,5},{5,1},{2,6},{6,2},{3,7},{7,3}} | collective-permute-start | bytes 12582920 | tf_op jit(solution)/shard_map/ppermute | solution.py:562
  3121.2 349.2 %collective-permute-start.55 = (f32[16384,128]{1,0:T(8,128)}, f32[16384,128]{1,0:T(8,128)}, u32[]{:S(2)}, u32[]{:S(2)}) collective-permute-start(f32[16384,128]{1,0:T(8,128)} %get-tuple-element.239), channel_id=1, source_target_pairs={{0,3},{1,0},{2,1},{3,2},{4,7},{5,4},{6,5},{7,6}} | collective-permute-start | bytes 25165832 | tf_op jit(solution)/shard_map/ppermute | solution.py:573
  3122.8 387.6 %collective-permute-start.53 = (f32[16384,128]{1,0:T(8,128)}, f32[16384,128]{1,0:T(8,128)}, u32[]{:S(2)}, u32[]{:S(2)}) collective-permute-start(f32[16384,128]{1,0:T(8,128)} %get-tuple-element.237), channel_id=1, source_target_pairs={{0,3},{1,0},{2,1},{3,2},{4,7},{5,4},{6,5},{7,6}} | collective-permute-start | bytes 25165832 | tf_op jit(solution)/shard_map/ppermute | solution.py:573
  3139.1 457.4 %collective-permute-start.63 = (f32[14824,128]{1,0:T(8,128)}, f32[14824,128]{1,0:T(8,128)}, u32[]{:S(2)}, u32[]{:S(2)}) collective-permute-start(f32[14824,128]{1,0:T(8,128)} %add.27.one_ref), channel_id=1, source_target_pairs={{0,2},{1,3},{2,0},{3,1},{4,6},{5,7},{6,4},{7,5}} | collective-permute-start | bytes 22769672 | tf_op jit(solution)/shard_map/ppermute | solution.py:578
  3140.6 326.6 %collective-permute-start.41 = (s32[2,8392]{1,0:T(2,128)S(1)}, s32[2,8392]{1,0:T(2,128)S(1)}, u32[]{:S(2)}, u32[]{:S(2)}) collective-permute-start(s32[2,8392]{1,0:T(2,128)S(1)} %pad_add_fusion.2), channel_id=1, source_target_pairs={{0,3},{1,0},{2,1},{3,2},{4,7},{5,4},{6,5},{7,6}} | collective-permute-start | bytes 201416 | tf_op jit(solution)/shard_map/ppermute | solution.py:541
  3140.7 329.7 %collective-permute-start.56 = (f32[512,128]{1,0:T(8,128)S(1)}, f32[512,128]{1,0:T(8,128)S(1)}, u32[]{:S(2)}, u32[]{:S(2)}) collective-permute-start(f32[512,128]{1,0:T(8,128)S(1)} %copy-done.48), channel_id=1, source_target_pairs={{0,3},{1,0},{2,1},{3,2},{4,7},{5,4},{6,5},{7,6}} | collective-permute-start | bytes 786440 | tf_op jit(solution)/shard_map/ppermute | solution.py:574
  3794.3 292.1 %collective-permute-start.67 = (f32[400,7412]{1,0:T(8,128)}, f32[400,7412]{1,0:T(8,128)}, u32[]{:S(2)}, u32[]{:S(2)}) collective-permute-start(f32[400,7412]{1,0:T(8,128)} %join_columns.9), channel_id=1, source_target_pairs={{0,1},{1,0},{2,3},{3,2},{4,5},{5,4},{6,7},{7,6}} | collective-permute-start | bytes 35577608 | tf_op jit(solution)/shard_map/ppermute | solution.py:609
  3802.0 214.7 %collective-permute-start.59 = (f32[200,4096]{1,0:T(8,128)}, f32[200,4096]{1,0:T(8,128)}, u32[]{:S(2)}, u32[]{:S(2)}) collective-permute-start(f32[200,4096]{1,0:T(8,128)} %flip_half.6.mine_ref), channel_id=1, source_target_pairs={{0,4},{4,0},{1,5},{5,1},{2,6},{6,2},{3,7},{7,3}} | collective-permute-start | bytes 9830408 | tf_op jit(solution)/shard_map/ppermute | solution.py:590
  3810.6 198.0 %collective-permute-start.60 = (f32[200,4096]{1,0:T(8,128)}, f32[200,4096]{1,0:T(8,128)}, u32[]{:S(2)}, u32[]{:S(2)}) collective-permute-start(f32[200,4096]{1,0:T(8,128)} %flip_half.7.mine_ref), channel_id=1, source_target_pairs={{0,4},{4,0},{1,5},{5,1},{2,6},{6,2},{3,7},{7,3}} | collective-permute-start | bytes 9830408 | tf_op jit(solution)/shard_map/ppermute | solution.py:590
  3818.2 260.2 %collective-permute-start.58 = (f32[200,4096]{1,0:T(8,128)}, f32[200,4096]{1,0:T(8,128)}, u32[]{:S(2)}, u32[]{:S(2)}) collective-permute-start(f32[200,4096]{1,0:T(8,128)} %flip_half.5.mine_ref), channel_id=1, source_target_pairs={{0,4},{4,0},{1,5},{5,1},{2,6},{6,2},{3,7},{7,3}} | collective-permute-start | bytes 9830408 | tf_op jit(solution)/shard_map/ppermute | solution.py:590
  (98 other events, 4676.7 us)
Sparse Core Ops, SparseCore 0:
  12.6 21.3 all-gather.3

commit v5 on v4

--- a/solution.py
+++ b/solution.py
@@ -594,10 +594,6 @@
                 rel_other = lax.ppermute(rel_mine, "ent", core_swap)
             losses.append(jnp.where(part == 0, sums[0], sums[1]) / edge_count)
 
-        ent_out = ()
-        for piece in range(PIECES):
-            ent_out = (join_columns(part, ent_cols[piece], ent_peer[piece], piece * size, ent_rows, ent_out),)
-        ent_out = ent_out[0].T
         rel_cols = flip_half(rel_mine, dim)
         quarter = rel_cols.shape[-1] // 2
         chip = lax.axis_index("ent") // 2
@@ -608,7 +604,13 @@
         rel_all = join_columns(part, rel_cols, rel_peer)
         rel_other = lax.ppermute(rel_all, "ent", core_swap)
         rel_out = jnp.concatenate(
-            [jnp.where(core == 0, rel_all, rel_other), jnp.where(core == 0, rel_other, rel_all)], axis=1).T
+            [jnp.where(core == 0, rel_all, rel_other), jnp.where(core == 0, rel_other, rel_all)], axis=1)
+        ent_out = ()
+        for piece in range(PIECES):
+            if piece == PIECES - 1:
+                ent_out = ent_out + (rel_out,)
+            ent_out = (join_columns(part, ent_cols[piece], ent_peer[piece], piece * size, ent_rows, ent_out),)
+        ent_out, rel_out = ent_out[0].T, rel_out.T
         return ent_out, state.reshape(-1), rel_out, jnp.stack(losses)[None, None, :]
 
     ent_spec = P(("sweep", "ent"), None)

time: 4140 us -> 4120 us (level)
  transfers between devices with their start and end apart: 69 -> 69, of which waited for: 33 -> 34; matrix products, arithmetic and copies ran while one was open for 1% -> 2% of each run, Pallas kernels for 33% -> 33%
where the time goes in v5:
time: 4120 us; the launch traced here: 4090 us
  waiting for transfers between devices  2030 us (49%)
  Pallas kernels  1890 us (46%)
  starting transfers between devices  64.5 us (2%)
  other arithmetic  60.9 us (1%)
    ppermute x3, waiting for transfers between devices, owned(): lax.ppermute(mine, 'ent', [(src, (src + round_idx) % ent_size) for src in...  1150 us
    pallas_call x8, Pallas kernels, bucket_grads(): pl.pallas_call(functools.partial(grad_kernel, int(last), negs), grid=(blo...  684 us
    pallas_call x8, Pallas kernels, add_rows(): pl.pallas_call(functools.partial(add_kernel, neg_ids.shape[-1]), grid=(bl...  316 us
    pallas_call x8, Pallas kernels, query_rows(): pl.pallas_call(query_kernel, grid=(blocks,), in_specs=[SCALARS, smem_bloc...  256 us
    ppermute x8, waiting for transfers between devices, device_epoch(): p_peer = lax.ppermute(p_mine, 'data', swap)  249 us
    pallas_call x8, Pallas kernels, tail_rows(): pl.pallas_call(functools.partial(tail_kernel, negs), grid=(blocks,), in_s...  238 us
    ppermute x4, waiting for transfers between devices, device_epoch(): ent_peer.append(lax.ppermute(ent_cols[piece], 'data', swap))  209 us
    pallas_call x8, Pallas kernels, adagrad_step(): pl.pallas_call(functools.partial(step_kernel, rate, dim), grid=(state.sha...  190 us
  transfers between devices with their start and end apart: 69, of which 34 were waited for; matrix products, arithmetic and copies ran while one was open for 2% of the time, Pallas kernels for 33%

profile of v5, /device:TPU:0, one launch (start us, length us, event | category | flops | bytes accessed | tf_op | source)
XLA Modules:
  0.0 4094.0 jit_solution(3107734870610458293)
XLA Ops:
  218.6 90.0 %collective-permute-done.4.pp_ref = f32[32,1,256]{2,1,0:T(1,128)S(1)} collective-permute-done((f32[32,1,256]{2,1,0:T(1,128)S(1)}, f32[32,1,256]{2,1,0:T(1,128)S(1)}, u32[]{:S(2)}, u32[]{:S(2)}) %collective-permute-start.4) | collective-permute-done | bytes 32800 | tf_op jit(solution)/shard_map/ppermute | solution.py:566
  311.0 81.4 %bucket_grads.8 = (f32[32768,128]{1,0:T(8,128)}, f32[29648,128]{1,0:T(8,128)}, f32[16384,128]{1,0:T(8,128)}, f32[512,128]{1,0:T(8,128)}, f32[1,128]{1,0:T(1,128)}) custom-call(s32[1]{0:T(128)} %bitcast.9.core_ref, s32[32,1,256]{2,1,0:T(1,128)} %bitcast.149, s32[32,1,256]{2,1,0:T(1,128)} %bitcast.147, f32[16384,128]{1,0:T(8,128)} %get-tuple-element.140.a_ref, ...), custom_call_target="tpu_custom_call" | custom-call | flops 300000000 | bytes 200000000 | tf_op jit(solution)/shard_map/bucket_grads/pallas_call | solution.py:336
  393.1 89.6 %bucket_grads.9 = (f32[32768,128]{1,0:T(8,128)}, f32[14824,128]{1,0:T(8,128)}, f32[14824,128]{1,0:T(8,128)}, f32[16384,128]{1,0:T(8,128)}, f32[512,128]{1,0:T(8,128)}, /*index=5*/f32[1,128]{1,0:T(1,128)}) custom-call(s32[1]{0:T(128)} %bitcast.9.core_ref, s32[32,1,256]{2,1,0:T(1,128)} %bitcast.133, s32[32,1,256]{2,1,0:T(1,128)} %bitcast.131, ...), custom_call_target="tpu_custom_call" | custom-call | flops 300000000 | bytes 200000000 | tf_op jit(solution)/shard_map/bucket_grads/pallas_call | solution.py:336
  541.2 39.7 add_rows.9
  619.4 46.7 %collective-permute-done.9.two_ref = f32[14824,128]{1,0:T(8,128)} collective-permute-done((f32[14824,128]{1,0:T(8,128)}, f32[14824,128]{1,0:T(8,128)}, u32[]{:S(2)}, u32[]{:S(2)}) %collective-permute-start.9) | collective-permute-done | bytes 7589920 | tf_op jit(solution)/shard_map/ppermute | solution.py:578
  854.5 78.3 %collective-permute-done.17.pp_ref = f32[32,1,256]{2,1,0:T(1,128)S(1)} collective-permute-done((f32[32,1,256]{2,1,0:T(1,128)S(1)}, f32[32,1,256]{2,1,0:T(1,128)S(1)}, u32[]{:S(2)}, u32[]{:S(2)}) %collective-permute-start.17) | collective-permute-done | bytes 32800 | tf_op jit(solution)/shard_map/ppermute | solution.py:566
  933.8 81.4 %bucket_grads.10 = (f32[32768,128]{1,0:T(8,128)}, f32[29648,128]{1,0:T(8,128)}, f32[16384,128]{1,0:T(8,128)}, f32[512,128]{1,0:T(8,128)}, f32[1,128]{1,0:T(1,128)}) custom-call(s32[1]{0:T(128)} %bitcast.9.core_ref, s32[32,1,256]{2,1,0:T(1,128)} %bitcast.145, s32[32,1,256]{2,1,0:T(1,128)} %bitcast.143, f32[16384,128]{1,0:T(8,128)} %get-tuple-element.169.a_ref, ...), custom_call_target="tpu_custom_call" | custom-call | flops 300000000 | bytes 200000000 | tf_op jit(solution)/shard_map/bucket_grads/pallas_call | solution.py:336
  1015.9 89.6 %bucket_grads.11 = (f32[32768,128]{1,0:T(8,128)}, f32[14824,128]{1,0:T(8,128)}, f32[14824,128]{1,0:T(8,128)}, f32[16384,128]{1,0:T(8,128)}, f32[512,128]{1,0:T(8,128)}, /*index=5*/f32[1,128]{1,0:T(1,128)}) custom-call(s32[1]{0:T(128)} %bitcast.9.core_ref, s32[32,1,256]{2,1,0:T(1,128)} %bitcast.127, s32[32,1,256]{2,1,0:T(1,128)} %bitcast.125, ...), custom_call_target="tpu_custom_call" | custom-call | flops 300000000 | bytes 200000000 | tf_op jit(solution)/shard_map/bucket_grads/pallas_call | solution.py:336
  1128.9 323.0 %collective-permute-done.7 = s32[2,8392]{1,0:T(2,128)S(1)} collective-permute-done((s32[2,8392]{1,0:T(2,128)S(1)}, s32[2,8392]{1,0:T(2,128)S(1)}, u32[]{:S(2)}, u32[]{:S(2)}) %collective-permute-start.7) | collective-permute-done | bytes 67168 | tf_op jit(solution)/shard_map/ppermute | solution.py:541
  1495.5 39.6 add_rows.11
  1685.5 104.7 %collective-permute-done.29.tab_hbm = bf16[32768,128]{1,0:T(8,128)(2,1)} collective-permute-done((bf16[32768,128]{1,0:T(8,128)(2,1)}, bf16[32768,128]{1,0:T(8,128)(2,1)}, u32[]{:S(2)}, u32[]{:S(2)}) %collective-permute-start.29) | collective-permute-done | bytes 8388640 | tf_op jit(solution)/shard_map/ppermute | solution.py:551
  1858.1 81.5 %bucket_grads.12 = (f32[32768,128]{1,0:T(8,128)}, f32[29648,128]{1,0:T(8,128)}, f32[16384,128]{1,0:T(8,128)}, f32[512,128]{1,0:T(8,128)}, f32[1,128]{1,0:T(1,128)}) custom-call(s32[1]{0:T(128)} %bitcast.9.core_ref, s32[32,1,256]{2,1,0:T(1,128)} %bitcast.141, s32[32,1,256]{2,1,0:T(1,128)} %bitcast.139, f32[16384,128]{1,0:T(8,128)} %get-tuple-element.199.a_ref, ...), custom_call_target="tpu_custom_call" | custom-call | flops 300000000 | bytes 200000000 | tf_op jit(solution)/shard_map/bucket_grads/pallas_call | solution.py:336
  1940.3 89.5 %bucket_grads.13 = (f32[32768,128]{1,0:T(8,128)}, f32[14824,128]{1,0:T(8,128)}, f32[14824,128]{1,0:T(8,128)}, f32[16384,128]{1,0:T(8,128)}, f32[512,128]{1,0:T(8,128)}, /*index=5*/f32[1,128]{1,0:T(1,128)}) custom-call(s32[1]{0:T(128)} %bitcast.9.core_ref, s32[32,1,256]{2,1,0:T(1,128)} %bitcast.123, s32[32,1,256]{2,1,0:T(1,128)} %bitcast.121, ...), custom_call_target="tpu_custom_call" | custom-call | flops 300000000 | bytes 200000000 | tf_op jit(solution)/shard_map/bucket_grads/pallas_call | solution.py:336
  2051.4 505.9 %collective-permute-done.24 = s32[2,8392]{1,0:T(2,128)S(1)} collective-permute-done((s32[2,8392]{1,0:T(2,128)S(1)}, s32[2,8392]{1,0:T(2,128)S(1)}, u32[]{:S(2)}, u32[]{:S(2)}) %collective-permute-start.24) | collective-permute-done | bytes 67168 | tf_op jit(solution)/shard_map/ppermute | solution.py:541
  2871.1 76.8 %collective-permute-done.51.pp_ref = f32[32,1,256]{2,1,0:T(1,128)S(1)} collective-permute-done((f32[32,1,256]{2,1,0:T(1,128)S(1)}, f32[32,1,256]{2,1,0:T(1,128)S(1)}, u32[]{:S(2)}, u32[]{:S(2)}) %collective-permute-start.51) | collective-permute-done | bytes 32800 | tf_op jit(solution)/shard_map/ppermute | solution.py:566
  2950.3 81.4 %bucket_grads.14 = (f32[32768,128]{1,0:T(8,128)}, f32[29648,128]{1,0:T(8,128)}, f32[16384,128]{1,0:T(8,128)}, f32[512,128]{1,0:T(8,128)}, f32[1,128]{1,0:T(1,128)}) custom-call(s32[1]{0:T(128)} %bitcast.9.core_ref, s32[32,1,256]{2,1,0:T(1,128)} %bitcast.137, s32[32,1,256]{2,1,0:T(1,128)} %bitcast.135, f32[16384,128]{1,0:T(8,128)} %get-tuple-element.229.a_ref, ...), custom_call_target="tpu_custom_call" | custom-call | flops 300000000 | bytes 200000000 | tf_op jit(solution)/shard_map/bucket_grads/pallas_call | solution.py:336
  3032.3 89.6 %bucket_grads.15 = (f32[32768,128]{1,0:T(8,128)}, f32[14824,128]{1,0:T(8,128)}, f32[14824,128]{1,0:T(8,128)}, f32[16384,128]{1,0:T(8,128)}, f32[512,128]{1,0:T(8,128)}, /*index=5*/f32[1,128]{1,0:T(1,128)}) custom-call(s32[1]{0:T(128)} %bitcast.9.core_ref, s32[32,1,256]{2,1,0:T(1,128)} %bitcast.119, s32[32,1,256]{2,1,0:T(1,128)} %bitcast.117, ...), custom_call_target="tpu_custom_call" | custom-call | flops 300000000 | bytes 200000000 | tf_op jit(solution)/shard_map/bucket_grads/pallas_call | solution.py:336
  3142.0 326.0 %collective-permute-done.41 = s32[2,8392]{1,0:T(2,128)S(1)} collective-permute-done((s32[2,8392]{1,0:T(2,128)S(1)}, s32[2,8392]{1,0:T(2,128)S(1)}, u32[]{:S(2)}, u32[]{:S(2)}) %collective-permute-start.41) | collective-permute-done | bytes 67168 | tf_op jit(solution)/shard_map/ppermute | solution.py:541
  3511.9 39.8 add_rows.15
  3645.9 64.3 %collective-permute-done.65 = f32[200,3706]{1,0:T(8,128)S(1)} collective-permute-done((f32[200,3706]{1,0:T(8,128)S(1)}, f32[200,3706]{1,0:T(8,128)S(1)}, u32[]{:S(2)}, u32[]{:S(2)}) %collective-permute-start.65) | collective-permute-done | bytes 2964832 | tf_op jit(solution)/shard_map/ppermute | solution.py:600
  3711.5 62.8 %collective-permute-done.66 = f32[200,3706]{1,0:T(8,128)} collective-permute-done((f32[200,3706]{1,0:T(8,128)S(1)}, f32[200,3706]{1,0:T(8,128)}, u32[]{:S(2)}, u32[]{:S(2)}) %collective-permute-start.66) | collective-permute-done | bytes 2964832 | tf_op jit(solution)/shard_map/ppermute | solution.py:601
  3821.3 47.7 %collective-permute-done.61.peer_ref = f32[200,4096]{1,0:T(8,128)} collective-permute-done((f32[200,4096]{1,0:T(8,128)S(1)}, f32[200,4096]{1,0:T(8,128)}, u32[]{:S(2)}, u32[]{:S(2)}) %collective-permute-start.61) | collective-permute-done | bytes 3276832 | tf_op jit(solution)/shard_map/ppermute | solution.py:590
  3876.9 62.3 %collective-permute-done.60.peer_ref = f32[200,4096]{1,0:T(8,128)} collective-permute-done((f32[200,4096]{1,0:T(8,128)}, f32[200,4096]{1,0:T(8,128)}, u32[]{:S(2)}, u32[]{:S(2)}) %collective-permute-start.60) | collective-permute-done | bytes 3276832 | tf_op jit(solution)/shard_map/ppermute | solution.py:590
  3947.2 62.3 %collective-permute-done.59.peer_ref = f32[200,4096]{1,0:T(8,128)} collective-permute-done((f32[200,4096]{1,0:T(8,128)}, f32[200,4096]{1,0:T(8,128)}, u32[]{:S(2)}, u32[]{:S(2)}) %collective-permute-start.59) | collective-permute-done | bytes 3276832 | tf_op jit(solution)/shard_map/ppermute | solution.py:590
  (314 shorter events, 1425.1 us)
Async XLA Ops:
  118.3 192.1 %collective-permute-start.3 = (bf16[8192,256]{1,0:T(8,128)(2,1)}, bf16[8192,256]{1,0:T(8,128)(2,1)}, u32[]{:S(2)}, u32[]{:S(2)}) collective-permute-start(bf16[8192,256]{1,0:T(8,128)(2,1)} %get-tuple-element.143.qm_ref), channel_id=1, source_target_pairs={{0,4},{4,0},{1,5},{5,1},{2,6},{6,2},{3,7},{7,3}} | collective-permute-start | bytes 12582920 | tf_op jit(solution)/shard_map/ppermute | solution.py:562
  153.5 239.0 %collective-permute-start = (bf16[8192,256]{1,0:T(8,128)(2,1)}, bf16[8192,256]{1,0:T(8,128)(2,1)}, u32[]{:S(2)}, u32[]{:S(2)}) collective-permute-start(bf16[8192,256]{1,0:T(8,128)(2,1)} %get-tuple-element.137.qm_ref), channel_id=1, source_target_pairs={{0,4},{4,0},{1,5},{5,1},{2,6},{6,2},{3,7},{7,3}} | collective-permute-start | bytes 12582920 | tf_op jit(solution)/shard_map/ppermute | solution.py:562
  776.1 239.1 %collective-permute-start.13 = (bf16[8192,256]{1,0:T(8,128)(2,1)}, bf16[8192,256]{1,0:T(8,128)(2,1)}, u32[]{:S(2)}, u32[]{:S(2)}) collective-permute-start(bf16[8192,256]{1,0:T(8,128)(2,1)} %get-tuple-element.166.qm_ref), channel_id=1, source_target_pairs={{0,4},{4,0},{1,5},{5,1},{2,6},{6,2},{3,7},{7,3}} | collective-permute-start | bytes 12582920 | tf_op jit(solution)/shard_map/ppermute | solution.py:562
  1105.6 349.2 %collective-permute-start.21 = (f32[16384,128]{1,0:T(8,128)}, f32[16384,128]{1,0:T(8,128)}, u32[]{:S(2)}, u32[]{:S(2)}) collective-permute-start(f32[16384,128]{1,0:T(8,128)} %get-tuple-element.179), channel_id=1, source_target_pairs={{0,1},{1,2},{2,3},{3,0},{4,5},{5,6},{6,7},{7,4}} | collective-permute-start | bytes 25165832 | tf_op jit(solution)/shard_map/ppermute | solution.py:573
  1106.1 388.7 %collective-permute-start.19 = (f32[16384,128]{1,0:T(8,128)}, f32[16384,128]{1,0:T(8,128)}, u32[]{:S(2)}, u32[]{:S(2)}) collective-permute-start(f32[16384,128]{1,0:T(8,128)} %get-tuple-element.177), channel_id=1, source_target_pairs={{0,1},{1,2},{2,3},{3,0},{4,5},{5,6},{6,7},{7,4}} | collective-permute-start | bytes 25165832 | tf_op jit(solution)/shard_map/ppermute | solution.py:573
  1123.3 450.1 %collective-permute-start.26 = (f32[14824,128]{1,0:T(8,128)}, f32[14824,128]{1,0:T(8,128)}, u32[]{:S(2)}, u32[]{:S(2)}) collective-permute-start(f32[14824,128]{1,0:T(8,128)} %add.25.one_ref), channel_id=1, source_target_pairs={{0,2},{1,3},{2,0},{3,1},{4,6},{5,7},{6,4},{7,5}} | collective-permute-start | bytes 22769672 | tf_op jit(solution)/shard_map/ppermute | solution.py:578
  1128.5 323.5 %collective-permute-start.7 = (s32[2,8392]{1,0:T(2,128)S(1)}, s32[2,8392]{1,0:T(2,128)S(1)}, u32[]{:S(2)}, u32[]{:S(2)}) collective-permute-start(s32[2,8392]{1,0:T(2,128)S(1)} %pad_add_fusion), channel_id=1, source_target_pairs={{0,1},{1,2},{2,3},{3,0},{4,5},{5,6},{6,7},{7,4}} | collective-permute-start | bytes 201416 | tf_op jit(solution)/shard_map/ppermute | solution.py:541
  1128.5 326.3 %collective-permute-start.22 = (f32[512,128]{1,0:T(8,128)S(1)}, f32[512,128]{1,0:T(8,128)S(1)}, u32[]{:S(2)}, u32[]{:S(2)}) collective-permute-start(f32[512,128]{1,0:T(8,128)S(1)} %copy-done.47), channel_id=1, source_target_pairs={{0,1},{1,2},{2,3},{3,0},{4,5},{5,6},{6,7},{7,4}} | collective-permute-start | bytes 786440 | tf_op jit(solution)/shard_map/ppermute | solution.py:574
  1651.5 206.0 %collective-permute-start.33 = (bf16[8192,256]{1,0:T(8,128)(2,1)}, bf16[8192,256]{1,0:T(8,128)(2,1)}, u32[]{:S(2)}, u32[]{:S(2)}) collective-permute-start(bf16[8192,256]{1,0:T(8,128)(2,1)} %get-tuple-element.202.qm_ref), channel_id=1, source_target_pairs={{0,4},{4,0},{1,5},{5,1},{2,6},{6,2},{3,7},{7,3}} | collective-permute-start | bytes 12582920 | tf_op jit(solution)/shard_map/ppermute | solution.py:562
  1685.1 254.5 %collective-permute-start.30 = (bf16[8192,256]{1,0:T(8,128)(2,1)}, bf16[8192,256]{1,0:T(8,128)(2,1)}, u32[]{:S(2)}, u32[]{:S(2)}) collective-permute-start(bf16[8192,256]{1,0:T(8,128)(2,1)} %get-tuple-element.196.qm_ref), channel_id=1, source_target_pairs={{0,4},{4,0},{1,5},{5,1},{2,6},{6,2},{3,7},{7,3}} | collective-permute-start | bytes 12582920 | tf_op jit(solution)/shard_map/ppermute | solution.py:562
  2029.9 533.0 %collective-permute-start.38 = (f32[16384,128]{1,0:T(8,128)}, f32[16384,128]{1,0:T(8,128)}, u32[]{:S(2)}, u32[]{:S(2)}) collective-permute-start(f32[16384,128]{1,0:T(8,128)} %get-tuple-element.209), channel_id=1, source_target_pairs={{0,2},{1,3},{2,0},{3,1},{4,6},{5,7},{6,4},{7,5}} | collective-permute-start | bytes 25165832 | tf_op jit(solution)/shard_map/ppermute | solution.py:573
  2031.5 571.4 %collective-permute-start.36 = (f32[16384,128]{1,0:T(8,128)}, f32[16384,128]{1,0:T(8,128)}, u32[]{:S(2)}, u32[]{:S(2)}) collective-permute-start(f32[16384,128]{1,0:T(8,128)} %get-tuple-element.207), channel_id=1, source_target_pairs={{0,2},{1,3},{2,0},{3,1},{4,6},{5,7},{6,4},{7,5}} | collective-permute-start | bytes 25165832 | tf_op jit(solution)/shard_map/ppermute | solution.py:573
  2047.6 633.9 %collective-permute-start.43 = (f32[14824,128]{1,0:T(8,128)}, f32[14824,128]{1,0:T(8,128)}, u32[]{:S(2)}, u32[]{:S(2)}) collective-permute-start(f32[14824,128]{1,0:T(8,128)} %add.26.one_ref), channel_id=1, source_target_pairs={{0,2},{1,3},{2,0},{3,1},{4,6},{5,7},{6,4},{7,5}} | collective-permute-start | bytes 22769672 | tf_op jit(solution)/shard_map/ppermute | solution.py:578
  2049.4 507.9 %collective-permute-start.24 = (s32[2,8392]{1,0:T(2,128)S(1)}, s32[2,8392]{1,0:T(2,128)S(1)}, u32[]{:S(2)}, u32[]{:S(2)}) collective-permute-start(s32[2,8392]{1,0:T(2,128)S(1)} %pad_add_fusion.1), channel_id=1, source_target_pairs={{0,2},{1,3},{2,0},{3,1},{4,6},{5,7},{6,4},{7,5}} | collective-permute-start | bytes 201416 | tf_op jit(solution)/shard_map/ppermute | solution.py:541
  2049.8 513.1 %collective-permute-start.39 = (f32[512,128]{1,0:T(8,128)S(1)}, f32[512,128]{1,0:T(8,128)S(1)}, u32[]{:S(2)}, u32[]{:S(2)}) collective-permute-start(f32[512,128]{1,0:T(8,128)S(1)} %copy-done.49), channel_id=1, source_target_pairs={{0,2},{1,3},{2,0},{3,1},{4,6},{5,7},{6,4},{7,5}} | collective-permute-start | bytes 786440 | tf_op jit(solution)/shard_map/ppermute | solution.py:574
  2792.5 239.3 %collective-permute-start.47 = (bf16[8192,256]{1,0:T(8,128)(2,1)}, bf16[8192,256]{1,0:T(8,128)(2,1)}, u32[]{:S(2)}, u32[]{:S(2)}) collective-permute-start(bf16[8192,256]{1,0:T(8,128)(2,1)} %get-tuple-element.226.qm_ref), channel_id=1, source_target_pairs={{0,4},{4,0},{1,5},{5,1},{2,6},{6,2},{3,7},{7,3}} | collective-permute-start | bytes 12582920 | tf_op jit(solution)/shard_map/ppermute | solution.py:562
  3122.0 349.2 %collective-permute-start.55 = (f32[16384,128]{1,0:T(8,128)}, f32[16384,128]{1,0:T(8,128)}, u32[]{:S(2)}, u32[]{:S(2)}) collective-permute-start(f32[16384,128]{1,0:T(8,128)} %get-tuple-element.239), channel_id=1, source_target_pairs={{0,3},{1,0},{2,1},{3,2},{4,7},{5,4},{6,5},{7,6}} | collective-permute-start | bytes 25165832 | tf_op jit(solution)/shard_map/ppermute | solution.py:573
  3123.6 387.6 %collective-permute-start.53 = (f32[16384,128]{1,0:T(8,128)}, f32[16384,128]{1,0:T(8,128)}, u32[]{:S(2)}, u32[]{:S(2)}) collective-permute-start(f32[16384,128]{1,0:T(8,128)} %get-tuple-element.237), channel_id=1, source_target_pairs={{0,3},{1,0},{2,1},{3,2},{4,7},{5,4},{6,5},{7,6}} | collective-permute-start | bytes 25165832 | tf_op jit(solution)/shard_map/ppermute | solution.py:573
  3139.8 457.4 %collective-permute-start.63 = (f32[14824,128]{1,0:T(8,128)}, f32[14824,128]{1,0:T(8,128)}, u32[]{:S(2)}, u32[]{:S(2)}) collective-permute-start(f32[14824,128]{1,0:T(8,128)} %add.27.one_ref), channel_id=1, source_target_pairs={{0,2},{1,3},{2,0},{3,1},{4,6},{5,7},{6,4},{7,5}} | collective-permute-start | bytes 22769672 | tf_op jit(solution)/shard_map/ppermute | solution.py:578
  3141.4 326.6 %collective-permute-start.41 = (s32[2,8392]{1,0:T(2,128)S(1)}, s32[2,8392]{1,0:T(2,128)S(1)}, u32[]{:S(2)}, u32[]{:S(2)}) collective-permute-start(s32[2,8392]{1,0:T(2,128)S(1)} %pad_add_fusion.2), channel_id=1, source_target_pairs={{0,3},{1,0},{2,1},{3,2},{4,7},{5,4},{6,5},{7,6}} | collective-permute-start | bytes 201416 | tf_op jit(solution)/shard_map/ppermute | solution.py:541
  3141.4 329.8 %collective-permute-start.56 = (f32[512,128]{1,0:T(8,128)S(1)}, f32[512,128]{1,0:T(8,128)S(1)}, u32[]{:S(2)}, u32[]{:S(2)}) collective-permute-start(f32[512,128]{1,0:T(8,128)S(1)} %copy-done.48), channel_id=1, source_target_pairs={{0,3},{1,0},{2,1},{3,2},{4,7},{5,4},{6,5},{7,6}} | collective-permute-start | bytes 786440 | tf_op jit(solution)/shard_map/ppermute | solution.py:574
  3795.0 222.3 %collective-permute-start.67 = (f32[400,7412]{1,0:T(8,128)}, f32[400,7412]{1,0:T(8,128)}, u32[]{:S(2)}, u32[]{:S(2)}) collective-permute-start(f32[400,7412]{1,0:T(8,128)} %join_columns.8), channel_id=1, source_target_pairs={{0,1},{1,0},{2,3},{3,2},{4,5},{5,4},{6,7},{7,6}} | collective-permute-start | bytes 35577608 | tf_op jit(solution)/shard_map/ppermute | solution.py:605
  3811.4 198.1 %collective-permute-start.59 = (f32[200,4096]{1,0:T(8,128)}, f32[200,4096]{1,0:T(8,128)}, u32[]{:S(2)}, u32[]{:S(2)}) collective-permute-start(f32[200,4096]{1,0:T(8,128)} %flip_half.6.mine_ref), channel_id=1, source_target_pairs={{0,4},{4,0},{1,5},{5,1},{2,6},{6,2},{3,7},{7,3}} | collective-permute-start | bytes 9830408 | tf_op jit(solution)/shard_map/ppermute | solution.py:590
  3819.8 259.4 %collective-permute-start.58 = (f32[200,4096]{1,0:T(8,128)}, f32[200,4096]{1,0:T(8,128)}, u32[]{:S(2)}, u32[]{:S(2)}) collective-permute-start(f32[200,4096]{1,0:T(8,128)} %flip_half.5.mine_ref), channel_id=1, source_target_pairs={{0,4},{4,0},{1,5},{5,1},{2,6},{6,2},{3,7},{7,3}} | collective-permute-start | bytes 9830408 | tf_op jit(solution)/shard_map/ppermute | solution.py:590
  (98 other events, 4621.9 us)
Sparse Core Ops, SparseCore 0:
  12.6 21.3 all-gather.3
